TPU v7x, 128 devices: a whole 4x4x4 slice. The times are simulated.
128 devices in a mesh: aux: 8 (over z, core), orb: 16 (over x, y).
Axes of the slice: x: 4, y: 4, z: 4, core: 2. Of those that a mesh axis runs over, the one named last changes fastest.
Arguments:
- half: bfloat16 [128, 384, 3072], P('aux', 'orb'), may hold values from -1 to 1
- metric: bfloat16 [128, 128], P('aux'), may hold values from -1 to 2
- survive: int32 [8, 16, 24], P('aux', 'orb'), may hold values 0 or 1
Outputs:
- exchange_k: float32 [3072, 3072], P('orb', 'aux')
All inputs are finite; a program needn't handle non-finite values. No bound on the sum of `survive` on one device may be relied on, other than what follows from the above.
Results may differ from a plain program's by a relative error of at most 0.00098.
Values may be sent and summed in bfloat16 or wider, within the bound.
No kernel may reach another device: no remote copies, remote signals or barrier semaphores. Data moves between devices by JAX's collectives and lax.ppermute only.
A program may use at most 128 MiB of HBM per device.

v0:
```python
import functools

import jax
import jax.numpy as jnp
from jax import lax
from jax.experimental import pallas as pl
from jax.experimental.pallas import tpu as pltpu
from jax.sharding import Mesh
from jax.sharding import PartitionSpec as P


AXES = ("z", "c", "x", "y")
BF = jnp.bfloat16
F32 = jnp.float32
I16 = jnp.int16
MIB = 1 << 20
RING = 4
ORDER = (2, 0, 1, 3)
TAIL = 16


def whole():
    return pl.BlockSpec(memory_space=pltpu.VMEM)


def scalars():
    return pl.BlockSpec(memory_space=pltpu.SMEM)


def position():
    return [lax.axis_index(a) for a in AXES]


def params(mib):
    return pltpu.CompilerParams(vmem_limit_bytes=mib * MIB)


def cost(flops, moved):
    return pl.CostEstimate(flops=flops, bytes_accessed=moved, transcendentals=0)


def place(z, c, x, y):
    return ((z % 4) * 2 + c) * 16 + (x % 4) * 4 + y % 4


def moves(shift):
    every = [(z, c, x, y) for z in range(4) for c in range(2) for x in range(4) for y in range(4)]
    return [(place(*d), place(*shift(*d))) for d in every]


def send(v, shift):
    return lax.ppermute(v, AXES, moves(shift))


def along_z(k):
    return lambda z, c, x, y: (z + k, c, x, y)


def other_core(z, c, x, y):
    return (z, 1 - c, x, y)


def first_axis(k):
    return lambda z, c, x, y: (z, c, x + k, y) if c == 0 else (z, c, x, y + k)


def second_axis(k):
    return lambda z, c, x, y: (z, c, x, y + k) if c == 0 else (z, c, x + k, y)


def screen_body(survive, half, *rest):
    outs, (held, turned, sems) = rest[:4], rest[4:]
    at = position()
    ao = half.shape[2]
    block = ao // survive.shape[2]
    chunks = sems.shape[0]
    lanes = ao // chunks
    copies = [
        pltpu.make_async_copy(half.at[:, :, cut], held.at[:, :, cut], sems.at[n])
        for n, cut in enumerate(slice(n * lanes, (n + 1) * lanes) for n in range(chunks))
    ]
    for copy in copies:
        copy.start()
    for n in range(chunks):
        copies[n].wait()

        def step(m, carry):
            m = n * (lanes // block) + m
            cut = pl.ds(pl.multiple_of(m * block, block), block)
            keep = survive[0, 0, m].astype(F32)
            turned[:, :, cut] = jnp.swapaxes(held[:, :, cut].astype(F32) * keep, 0, 1).astype(BF)
            return carry

        lax.fori_loop(0, lanes // block, step, 0, unroll=True)
    group = outs[0].shape[0]
    for k in range(RING):
        first = lax.rem(at[0] + k, RING) * group
        outs[k][...] = turned[pl.ds(first, group)]


def screen(survive, half):
    aux, occ, ao = half.shape
    out = jax.ShapeDtypeStruct((occ // RING, aux, ao), BF)
    in_hbm = pl.BlockSpec(memory_space=pltpu.HBM)
    return pl.pallas_call(
        screen_body,
        out_shape=[out] * RING,
        in_specs=[scalars(), in_hbm],
        out_specs=[whole()] * RING,
        scratch_shapes=[
            pltpu.VMEM(half.shape, BF),
            pltpu.VMEM((occ, aux, ao), BF),
            pltpu.SemaphoreType.DMA((4,)),
        ],
        compiler_params=params(50),
        cost_estimate=cost(half.size, half.size * 4),
        name="screen",
    )(survive, half)


def join_body(*refs):
    metrics, mixed = refs[:4], refs[4]
    at = position()
    aux = mixed.shape[0]
    part = aux // 8
    metric = jnp.concatenate([m[...] for m in metrics], axis=0)
    source = lax.broadcasted_iota(jnp.int32, (aux, aux), 0)
    n = lax.broadcasted_iota(jnp.int32, (aux, aux), 1)
    slot = n // part
    up = lax.rem(at[0] - slot // 2 + RING, RING)
    core = jnp.where(slot % 2 == 0, at[1], 1 - at[1])
    wanted = (up * 2 + core) * part + n % part
    pick = jnp.where(source == wanted, 1.0, 0.0).astype(BF)
    mixed[...] = jnp.dot(metric, pick, preferred_element_type=F32).astype(BF)


def join(metrics):
    aux = metrics[0].shape[1]
    return pl.pallas_call(
        join_body,
        out_shape=jax.ShapeDtypeStruct((aux, aux), BF),
        in_specs=[whole()] * 4,
        out_specs=whole(),
        compiler_params=params(4),
        cost_estimate=cost(2 * aux**3, aux * aux * 4),
        name="join",
    )(*metrics)


def fit_body(*refs):
    pieces, mixed, (bulk, rest, turned, fresh) = refs[:8], refs[8], refs[9:]
    at = position()
    step = pl.program_id(0)
    ao = fresh.shape[1]
    aux = mixed.shape[0]
    screened = jnp.concatenate([p[0] for p in pieces], axis=0)
    fitted = jnp.dot(mixed[...], screened, preferred_element_type=F32).astype(BF)
    fresh[...] = fitted
    wide, narrow = bulk.shape[1] // RING, rest.shape[1] // RING
    for n in range(RING):
        column = n * (ao // RING) + at[1] * (wide + narrow)
        bulk[:, n * wide:(n + 1) * wide] = fresh[:, pl.ds(pl.multiple_of(column, 128), wide)]
        column = lax.rem(at[0] + ORDER[n], RING) * (ao // RING) + at[1] * (wide + narrow) + wide
        rest[:, n * narrow:(n + 1) * narrow] = fresh[:, pl.ds(pl.multiple_of(column, 128), narrow)]
    flipped = fitted.T
    cut = pl.ds(pl.multiple_of(step * aux, aux), aux)
    high = ao // (RING * RING)
    for x in range(RING):
        for y in range(RING):
            n = x * RING + y
            to = jnp.where(at[1] == 0, n, y * RING + x) * high
            turned[pl.ds(pl.multiple_of(to, 64), high), cut] = flipped[n * high:(n + 1) * high]


def fit(pieces, mixed):
    group, part, ao = pieces[0].shape
    aux = part * 8
    piece = pl.BlockSpec((1, part, ao), lambda i: (i, 0, 0))
    return pl.pallas_call(
        fit_body,
        grid=(group,),
        out_shape=[jax.ShapeDtypeStruct((group * aux, n), BF) for n in (ao // 3, ao // 6)]
        + [jax.ShapeDtypeStruct((ao, group * aux), BF)],
        in_specs=[piece] * 8 + [whole()],
        out_specs=[pl.BlockSpec((aux, n), lambda i: (i, 0)) for n in (ao // 3, ao // 6)]
        + [pl.BlockSpec((ao, group * aux), lambda i: (0, 0))],
        scratch_shapes=[pltpu.VMEM((aux, ao), BF)],
        compiler_params=params(28),
        cost_estimate=cost(2 * group * aux * aux * ao, group * aux * ao * 6),
        name="fit",
    )(*pieces, mixed)


def exponent(top):
    return jnp.floor(14.9 - jnp.log2(jnp.maximum(top, 1e-30)))


def coded(v, e):
    return jnp.round(v * jnp.exp2(e)).astype(jnp.int32).astype(I16)


def marked(e):
    return jnp.broadcast_to(e, (TAIL, e.shape[1])).astype(jnp.int32).astype(I16)


def scale_of(tail):
    return jnp.exp2(-tail.astype(jnp.int32).astype(F32)[:1])


def plain(q):
    return q.astype(jnp.int32).astype(F32)


def write(out, first, block):
    if out.dtype == F32:
        out[first:first + block.shape[0], :] = block
    else:
        e = exponent(jnp.max(jnp.abs(block), axis=0, keepdims=True))
        end = first + block.shape[0]
        out[first:end, :] = coded(block, e)
        out[end:end + TAIL, :] = marked(e)


def bulk_body(blocks, bulk, turned, *refs):
    at = position()
    total = turned.shape[0] // RING
    own = jnp.where(at[1] == 0, at[2], at[3])
    outs = refs[len(refs) - len(blocks):]
    arrived = iter(refs)
    wide = bulk.shape[1] // 2
    for (shift, half, adds), out in zip(blocks, outs):
        rows = total if half is None else total // 2
        first = lax.rem(own + shift, RING) * total + (0 if half is None else half * rows)
        left = turned[pl.ds(pl.multiple_of(first, 128), rows), :]
        part = next(arrived) if adds else None
        for n in range(2):
            lanes = slice(n * wide, (n + 1) * wide)
            block = jnp.dot(left, bulk[:, lanes], preferred_element_type=F32)
            if adds:
                block = block + plain(part[:rows, lanes]) * scale_of(part[rows:, lanes])
            write(out.at[:, lanes], 0, block)


def bulk_k(bulk, turned, blocks, arrived=()):
    depth, columns = bulk.shape
    total = turned.shape[0] // RING
    sizes = [total if half is None else total // 2 for _, half, _ in blocks]
    return pl.pallas_call(
        functools.partial(bulk_body, blocks),
        out_shape=[
            jax.ShapeDtypeStruct((n + (TAIL if shift else 0), columns), I16 if shift else F32)
            for n, (shift, _, _) in zip(sizes, blocks)
        ],
        in_specs=[whole()] * (2 + len(arrived)),
        out_specs=[whole()] * len(blocks),
        compiler_params=params(28),
        cost_estimate=cost(2 * depth * sum(sizes) * columns, sum(sizes) * columns * 2),
    )(bulk, turned, *arrived)


def rest_body(slot, cut, rest, turned, *outs):
    narrow = rest.shape[1] // RING
    total = turned.shape[0] // RING
    right = rest[:, slot * narrow:(slot + 2) * narrow]
    for g in range(RING):
        block = jnp.dot(turned[g * total:(g + 1) * total, :], right, preferred_element_type=F32)
        for n in range(2):
            out = outs[cut[n][g // 2]]
            size = total if out.dtype == F32 else total + TAIL
            whole_block = out.shape[0] == RING * total
            write(out, (g if whole_block else g % 2) * size, block[:, n * narrow:(n + 1) * narrow])


def rest_k(rest, turned, slot, cut, kinds):
    depth = rest.shape[0]
    ao = turned.shape[0]
    narrow = rest.shape[1] // RING
    shapes = {
        "message": ((ao // 2 + 2 * TAIL, narrow), I16), "half": ((ao // 2, narrow), F32), "all": ((ao, narrow), F32)
    }
    return pl.pallas_call(
        functools.partial(rest_body, slot, cut),
        out_shape=[jax.ShapeDtypeStruct(*shapes[kind]) for kind in kinds],
        in_specs=[whole()] * 2,
        out_specs=[whole()] * len(kinds),
        compiler_params=params(28),
        cost_estimate=cost(4 * depth * ao * narrow, ao * narrow * 4),
    )(rest, turned)


def rest_mid_body(*refs):
    for own, arrived, out in ((refs[0], refs[1], refs[4]), (refs[2], refs[3], refs[5])):
        total = own.shape[0] // 2
        for g in range(2):
            first = g * (total + TAIL)
            v = own[g * total:(g + 1) * total, :] + plain(arrived[first:first + total, :]) * scale_of(
                arrived[first + total:first + total + TAIL, :]
            )
            write(out, first, v)


def rest_mid(up, arrived_up, down, arrived_down):
    shape = jax.ShapeDtypeStruct(arrived_up.shape, I16)
    return pl.pallas_call(
        rest_mid_body,
        out_shape=[shape] * 2,
        in_specs=[whole()] * 4,
        out_specs=[whole()] * 2,
        compiler_params=params(16),
        cost_estimate=cost(up.size * 16, up.size * 16),
        name="rest_mid",
    )(up, arrived_up, down, arrived_down)


def gathered(own, arrived, first, tail, row, lanes):
    v = own[pl.ds(pl.multiple_of(first[0] + row, 64), first[2]), lanes]
    for m in arrived:
        cut = pl.ds(pl.multiple_of(first[1] + row, 16), first[2])
        v = v + plain(m[cut, lanes]) * scale_of(m[tail:tail + TAIL, lanes])
    return v


def rest_second_body(own, a, b, d, e, after, kept, *outs):
    at = position()
    high = kept.shape[0]
    total, step = own.shape[0] // RING, own.shape[1]
    h = jnp.where(at[1] == 0, at[3], at[2])
    for k in range(RING):
        row = lax.rem(h + k, RING) * high
        out = kept if k == 0 else outs[k - 1]
        for n in range(RING):
            start = n % 2 * (total + TAIL)
            v = gathered(
                own, (a, b) if n < 2 else (d, e), (n * total, start, high), start + total, row, slice(0, step)
            )
            write(out.at[:, n * step:(n + 1) * step], 0, v)


def rest_second(own, upper, lower, after):
    total, columns = own.shape
    high, every = total // RING // RING, columns * RING
    return list(pl.pallas_call(
        rest_second_body,
        out_shape=[jax.ShapeDtypeStruct((high, every), F32)]
        + [jax.ShapeDtypeStruct((high + TAIL, every), I16)] * 3,
        in_specs=[whole()] * 6,
        out_specs=[whole()] * 4,
        compiler_params=params(24),
        cost_estimate=cost(total * columns * 12, total * columns * 8),
        name="rest_second_sum",
    )(own, *upper, *lower, after))


def bulk_second_body(own, a, b, d, e, after, kept, *outs):
    at = position()
    high = kept.shape[0]
    h = jnp.where(at[1] == 0, at[3], at[2])
    half = own.shape[0] // 2
    step = 256
    for k in range(RING):
        block = lax.rem(h + k, RING)
        out = kept if k == 0 else outs[k - 1]

        def part(upper, arrived, block=block, out=out):
            @pl.when((block < RING // 2) == upper)
            def _():
                row = pl.multiple_of(lax.rem(block, RING // 2) * high, 64)
                first = pl.multiple_of(block * high, 64)
                for lane in range(0, own.shape[1], step):
                    lanes = slice(lane, lane + step)
                    v = own[pl.ds(first, high), lanes]
                    for m in arrived:
                        v = v + plain(m[pl.ds(row, high), lanes]) * scale_of(m[half:, lanes])
                    write(out.at[:, lanes], 0, v)

        part(True, (a, b))
        part(False, (d, e))


def bulk_second(own, upper, lower, after):
    total, columns = own.shape
    high = total // RING
    return list(pl.pallas_call(
        bulk_second_body,
        out_shape=[jax.ShapeDtypeStruct((high, columns), F32)]
        + [jax.ShapeDtypeStruct((high + TAIL, columns), I16)] * 3,
        in_specs=[whole()] * 6,
        out_specs=[whole()] * 4,
        compiler_params=params(24),
        cost_estimate=cost(total * columns * 12, total * columns * 8),
        name="bulk_second_sum",
    )(own, *upper, *lower, after))


def third_body(by_z, own, a, b, d, after, *outs):
    at = position()
    high, step = outs[0].shape
    start = at[0] if by_z else jnp.where(at[1] == 0, at[2], at[3])
    for k in range(RING):
        cut = pl.ds(pl.multiple_of(lax.rem(start + k, RING) * step, 128), step)
        write(outs[k], 0, gathered(own, (a, b, d), (0, 0, high), high, 0, cut))


def third(parts, by_z, after):
    high, every = parts[0].shape
    wide = every // RING
    return list(pl.pallas_call(
        functools.partial(third_body, by_z),
        out_shape=[jax.ShapeDtypeStruct((high, wide), F32)] + [jax.ShapeDtypeStruct((high + TAIL, wide), I16)] * 3,
        in_specs=[whole()] * 5,
        out_specs=[whole()] * 4,
        compiler_params=params(16),
        cost_estimate=cost(high * every * 16, high * every * 10),
        name="third_sum",
    )(*parts, after))


def tick_body(v, out):
    out[...] = v[...]


def tick(v):
    return pl.pallas_call(
        tick_body,
        out_shape=jax.ShapeDtypeStruct(v.shape, v.dtype),
        in_specs=[whole()],
        out_specs=whole(),
        compiler_params=params(1),
        cost_estimate=cost(1000, 32),
        name="tick",
    )(v)


def finish_body(own, a, b, d, rest, ra, rb, rd, out):
    high, wide = own.shape
    for first, v, arrived in ((0, own[...], (a, b, d)), (wide, rest[...], (ra, rb, rd))):
        for m in arrived:
            v = v + plain(m[:high, :]) * scale_of(m[high:, :])
        out[:, first:first + v.shape[1]] = v


def finish(bulk, rest):
    high = bulk[0].shape[0]
    ao = bulk[0].shape[1] + rest[0].shape[1]
    return pl.pallas_call(
        finish_body,
        out_shape=jax.ShapeDtypeStruct((high, ao), F32),
        in_specs=[whole()] * 8,
        out_specs=whole(),
        compiler_params=params(8),
        cost_estimate=cost(high * ao * 8, high * ao * 14),
    )(*bulk, *rest)


def shards(half, metric, survive):
    parts = screen(survive, half)
    here = [parts[0]] + [None] * 3
    for k in (2, 1, 3):
        here[k] = send(parts[k], along_z(k))
    pair = jnp.concatenate([metric, send(metric, other_core)], axis=0)
    metrics = [pair] + [None] * 3
    for k in (1, 2, 3):
        metrics[k] = send(pair, along_z(k))
    mixed = join(metrics)
    there = [None] * 4
    for k in (0, 2, 1, 3):
        there[k] = send(here[k], other_core)
    bulk_rows, rest_rows, turned = fit([v for both in zip(here, there) for v in both], mixed)

    def bulk_step(*blocks, arrived=()):
        return bulk_k(bulk_rows, turned, blocks, arrived)

    def rest_step(*how):
        return rest_k(rest_rows, turned, *how)

    def near(axis, up, down):
        up = send(up, axis(1))
        down = send(down, axis(3))
        return up, down

    def onward(parts, shift):
        for k in (1, 2, 3):
            parts[k] = send(parts[k], shift(k))

    far = near(first_axis, *bulk_step((2, 0, False), (2, 1, False)))
    lower_up, upper_down = near(first_axis, *bulk_step((1, 1, False), (3, 0, False)))
    upper, lower, rest_own = rest_step(0, ((0, 1), (2, 2)), ("message", "message", "all"))
    rest_far = near(along_z, upper, lower)
    upper_up, lower_down = near(first_axis, *bulk_step((1, 0, True), (3, 1, True), arrived=far))
    keep_up, up, down, keep_down = rest_step(2, ((0, 1), (2, 3)), ("half", "message", "message", "half"))
    rest_near = near(along_z, up, down)
    up, down = rest_mid(keep_up, rest_far[0], keep_down, rest_far[1])
    mid = near(along_z, up, down)
    own = bulk_step((0, None, False))[0]
    bulk = bulk_second(own, (upper_up, upper_down), (lower_up, lower_down), metric)
    onward(bulk, second_axis)
    then = tick(metric)
    rest = rest_second(rest_own, (mid[0], rest_near[1]), (rest_near[0], mid[1]), then)
    onward(rest, second_axis)
    then = tick(then)
    bulk = third(bulk, True, then)
    onward(bulk, along_z)
    then = tick(then)
    rest = third(rest, False, then)
    onward(rest, first_axis)
    return finish(bulk, rest)


def solution(mesh):
    finer = Mesh(mesh.devices.reshape(4, 2, 4, 4), AXES)
    placed = (P(("z", "c"), ("x", "y"), None), P(("z", "c"), None), P(("z", "c"), ("x", "y"), None))
    return jax.shard_map(shards, mesh=finer, in_specs=placed, out_specs=P(("x", "y"), ("z", "c")), check_vma=False)
```

profile of v0, /device:TPU:8, one launch (start us, length us, event | category | flops | bytes accessed | tf_op | source)
XLA Modules:
  0.0 139.5 jit_solution(18208998216931494553)
XLA Ops:
  0.7 3.1 %screen.1 = (bf16[6,16,3072]{2,1,0:T(8,128)(2,1)S(1)}, bf16[6,16,3072]{2,1,0:T(8,128)(2,1)S(1)}, bf16[6,16,3072]{2,1,0:T(8,128)(2,1)S(1)}, bf16[6,16,3072]{2,1,0:T(8,128)(2,1)S(1)}) custom-call(s32[1,1,24]{2,1,0:T(1,128)S(1)} %copy-done.1, bf16[16,24,3072]{2,1,0:T(8,128)(2,1)} %half.1), custom_call_target="tpu_custom_call" | custom-call | flops 1179648 | bytes 4718592 | tf_op jit(solution)/shard_map/screen/pallas_call | solution.py:105
  3.8 2.0 %collective-permute-start.1 = (bf16[6,16,3072]{2,1,0:T(8,128)(2,1)S(1)}, bf16[6,16,3072]{2,1,0:T(8,128)(2,1)S(1)}, u32[]{:S(2)}, u32[]{:S(2)}) collective-permute-start(bf16[6,16,3072]{2,1,0:T(8,128)(2,1)S(1)} %get-tuple-element.44), channel_id=1, source_target_pairs={{0,32},{1,33},{2,34},{3,35},{4,36},{5,37},{6,38},{7,39},{8,40},{9,... | collective-permute-start | bytes 1769480 | tf_op jit(solution)/shard_map/ppermute | solution.py:52
  5.8 3.6 %collective-permute-start.3 = (bf16[6,16,3072]{2,1,0:T(8,128)(2,1)S(1)}, bf16[6,16,3072]{2,1,0:T(8,128)(2,1)S(1)}, u32[]{:S(2)}, u32[]{:S(2)}) collective-permute-start(bf16[6,16,3072]{2,1,0:T(8,128)(2,1)S(1)} %get-tuple-element.45), channel_id=1, source_target_pairs={{0,64},{1,65},{2,66},{3,67},{4,68},{5,69},{6,70},{7,71},{8,72},{9,... | collective-permute-start | bytes 1769480 | tf_op jit(solution)/shard_map/ppermute | solution.py:52
  10.4 10.9 %collective-permute-done.1.refs_2_ = bf16[6,16,3072]{2,1,0:T(8,128)(2,1)S(1)} collective-permute-done((bf16[6,16,3072]{2,1,0:T(8,128)(2,1)S(1)}, bf16[6,16,3072]{2,1,0:T(8,128)(2,1)S(1)}, u32[]{:S(2)}, u32[]{:S(2)}) %collective-permute-start.1) | collective-permute-done | bytes 589856 | tf_op jit(solution)/shard_map/ppermute | solution.py:52
  21.2 13.8 %collective-permute-done.3.refs_4_ = bf16[6,16,3072]{2,1,0:T(8,128)(2,1)S(1)} collective-permute-done((bf16[6,16,3072]{2,1,0:T(8,128)(2,1)S(1)}, bf16[6,16,3072]{2,1,0:T(8,128)(2,1)S(1)}, u32[]{:S(2)}, u32[]{:S(2)}) %collective-permute-start.3) | collective-permute-done | bytes 589856 | tf_op jit(solution)/shard_map/ppermute | solution.py:52
  35.6 2.2 %collective-permute-done.7 = bf16[16,128]{1,0:T(8,128)(2,1)S(1)} collective-permute-done((bf16[16,128]{1,0:T(8,128)(2,1)S(1)}, bf16[16,128]{1,0:T(8,128)(2,1)S(1)}, u32[]{:S(2)}, u32[]{:S(2)}) %collective-permute-start.7) | collective-permute-done | bytes 4128 | tf_op jit(solution)/shard_map/ppermute | solution.py:52
  39.2 2.3 %collective-permute-done.10.refs_3_ = bf16[32,128]{1,0:T(8,128)(2,1)S(1)} collective-permute-done((bf16[32,128]{1,0:T(8,128)(2,1)S(1)}, bf16[32,128]{1,0:T(8,128)(2,1)S(1)}, u32[]{:S(2)}, u32[]{:S(2)}) %collective-permute-start.10) | collective-permute-done | bytes 8224 | tf_op jit(solution)/shard_map/ppermute | solution.py:52
  41.9 4.5 %collective-permute-done.8.refs_1_ = bf16[32,128]{1,0:T(8,128)(2,1)S(1)} collective-permute-done((bf16[32,128]{1,0:T(8,128)(2,1)S(1)}, bf16[32,128]{1,0:T(8,128)(2,1)S(1)}, u32[]{:S(2)}, u32[]{:S(2)}) %collective-permute-start.8) | collective-permute-done | bytes 8224 | tf_op jit(solution)/shard_map/ppermute | solution.py:52
  46.9 4.7 %collective-permute-done.9.refs_2_ = bf16[32,128]{1,0:T(8,128)(2,1)S(1)} collective-permute-done((bf16[32,128]{1,0:T(8,128)(2,1)S(1)}, bf16[32,128]{1,0:T(8,128)(2,1)S(1)}, u32[]{:S(2)}, u32[]{:S(2)}) %collective-permute-start.9) | collective-permute-done | bytes 8224 | tf_op jit(solution)/shard_map/ppermute | solution.py:52
  51.8 3.3 %fit.1 = (bf16[768,1024]{1,0:T(8,128)(2,1)S(1)}, bf16[768,512]{1,0:T(8,128)(2,1)S(1)}, bf16[3072,768]{1,0:T(8,128)(2,1)S(1)}) custom-call(bf16[6,16,3072]{2,1,0:T(8,128)(2,1)S(1)} %get-tuple-element.43.refs_0_, bf16[6,16,3072]{2,1,0:T(8,128)(2,1)S(1)} %collective-permute-done.refs_1_, bf16[6,16,3072]{2,1,0:T(8,128)(2,1)S(1)} %collective-permute-done.1.refs_2_, ...), custom_call_target="tpu_custom_call" | custom-call | flops 603979776 | bytes 14155776 | tf_op jit(solution)/shard_map/fit/pallas_call | solution.py:179
  55.1 1.7 %shard_map.38 = (s16[400,1024]{1,0:T(8,128)(2,1)S(1)}, s16[400,1024]{1,0:T(8,128)(2,1)S(1)}) custom-call(bf16[768,1024]{1,0:T(8,128)(2,1)S(1)} %get-tuple-element.47.bulk, bf16[3072,768]{1,0:T(8,128)(2,1)S(1)} %get-tuple-element.48.turned), custom_call_target="tpu_custom_call" | custom-call | flops 1207959552 | bytes 1572864 | tf_op jit(solution)/shard_map/pallas_call | solution.py:248
  56.8 1.6 %collective-permute-start.11 = (s16[400,1024]{1,0:T(8,128)(2,1)S(1)}, s16[400,1024]{1,0:T(8,128)(2,1)S(1)}, u32[]{:S(2)}, u32[]{:S(2)}) collective-permute-start(s16[400,1024]{1,0:T(8,128)(2,1)S(1)} %get-tuple-element.49), channel_id=1, source_target_pairs={{0,4},{1,5},{2,6},{3,7},{4,8},{5,9},{6,10},{7,11},{8,12},{9,13},{1... | collective-permute-start | bytes 2457608 | tf_op jit(solution)/shard_map/ppermute | solution.py:52
  58.4 1.7 %collective-permute-start.12 = (s16[400,1024]{1,0:T(8,128)(2,1)S(1)}, s16[400,1024]{1,0:T(8,128)(2,1)S(1)}, u32[]{:S(2)}, u32[]{:S(2)}) collective-permute-start(s16[400,1024]{1,0:T(8,128)(2,1)S(1)} %get-tuple-element.50), channel_id=1, source_target_pairs={{0,12},{1,13},{2,14},{3,15},{4,0},{5,1},{6,2},{7,3},{8,4},{9,5},{1... | collective-permute-start | bytes 2457608 | tf_op jit(solution)/shard_map/ppermute | solution.py:52
  60.1 1.6 %shard_map.41 = (s16[1568,128]{1,0:T(8,128)(2,1)S(1)}, s16[1568,128]{1,0:T(8,128)(2,1)S(1)}, f32[3072,128]{1,0:T(8,128)S(1)}) custom-call(bf16[768,512]{1,0:T(8,128)(2,1)S(1)} %get-tuple-element.63.rest, bf16[3072,768]{1,0:T(8,128)(2,1)S(1)} %get-tuple-element.48.turned), custom_call_target="tpu_custom_call" | custom-call | flops 1207959552 | bytes 1572864 | tf_op jit(solution)/shard_map/pallas_call | solution.py:281
  61.8 3.2 %collective-permute-start.24 = (s16[1568,128]{1,0:T(8,128)(2,1)S(1)}, s16[1568,128]{1,0:T(8,128)(2,1)S(1)}, u32[]{:S(2)}, u32[]{:S(2)}) collective-permute-start(s16[1568,128]{1,0:T(8,128)(2,1)S(1)} %get-tuple-element.68), channel_id=1, source_target_pairs={{0,96},{1,97},{2,98},{3,99},{4,100},{5,101},{6,102},{7,103},{8,104... | collective-permute-start | bytes 1204232 | tf_op jit(solution)/shard_map/ppermute | solution.py:52
  65.0 1.6 %shard_map.42 = (f32[1536,128]{1,0:T(8,128)S(1)}, s16[1568,128]{1,0:T(8,128)(2,1)S(1)}, s16[1568,128]{1,0:T(8,128)(2,1)S(1)}, f32[1536,128]{1,0:T(8,128)S(1)}) custom-call(bf16[768,512]{1,0:T(8,128)(2,1)S(1)} %get-tuple-element.63.rest, bf16[3072,768]{1,0:T(8,128)(2,1)S(1)} %get-tuple-element.48.turned), custom_call_target="tpu_custom_call" | custom-call | flops 1207959552 | bytes 1572864 | tf_op jit(solution)/shard_map/pallas_call | solution.py:281
  66.8 3.7 %collective-permute-done.11.refs_0_ = s16[400,1024]{1,0:T(8,128)(2,1)S(1)} collective-permute-done((s16[400,1024]{1,0:T(8,128)(2,1)S(1)}, s16[400,1024]{1,0:T(8,128)(2,1)S(1)}, u32[]{:S(2)}, u32[]{:S(2)}) %collective-permute-start.11) | collective-permute-done | bytes 819232 | tf_op jit(solution)/shard_map/ppermute | solution.py:52
  70.4 1.7 %shard_map.40 = (s16[400,1024]{1,0:T(8,128)(2,1)S(1)}, s16[400,1024]{1,0:T(8,128)(2,1)S(1)}) custom-call(bf16[768,1024]{1,0:T(8,128)(2,1)S(1)} %get-tuple-element.47.bulk, bf16[3072,768]{1,0:T(8,128)(2,1)S(1)} %get-tuple-element.48.turned), custom_call_target="tpu_custom_call" | custom-call | flops 1207959552 | bytes 1572864 | tf_op jit(solution)/shard_map/pallas_call | solution.py:248
  72.2 1.6 %collective-permute-start.14 = (s16[400,1024]{1,0:T(8,128)(2,1)S(1)}, s16[400,1024]{1,0:T(8,128)(2,1)S(1)}, u32[]{:S(2)}, u32[]{:S(2)}) collective-permute-start(s16[400,1024]{1,0:T(8,128)(2,1)S(1)} %get-tuple-element.52), channel_id=1, source_target_pairs={{0,12},{1,13},{2,14},{3,15},{4,0},{5,1},{6,2},{7,3},{8,4},{9,5},{1... | collective-permute-start | bytes 2457608 | tf_op jit(solution)/shard_map/ppermute | solution.py:52
  73.8 1.8 %shard_map.39 = (s16[400,1024]{1,0:T(8,128)(2,1)S(1)}, s16[400,1024]{1,0:T(8,128)(2,1)S(1)}) custom-call(bf16[768,1024]{1,0:T(8,128)(2,1)S(1)} %get-tuple-element.47.bulk, bf16[3072,768]{1,0:T(8,128)(2,1)S(1)} %get-tuple-element.48.turned, s16[400,1024]{1,0:T(8,128)(2,1)S(1)} %collective-permute-done.11.refs_0_, ...), custom_call_target="tpu_custom_call" | custom-call | flops 1207959552 | bytes 1572864 | tf_op jit(solution)/shard_map/pallas_call | solution.py:248
  77.0 2.8 %collective-permute-start.16 = (s16[400,1024]{1,0:T(8,128)(2,1)S(1)}, s16[400,1024]{1,0:T(8,128)(2,1)S(1)}, u32[]{:S(2)}, u32[]{:S(2)}) collective-permute-start(s16[400,1024]{1,0:T(8,128)(2,1)S(1)} %get-tuple-element.54), channel_id=1, source_target_pairs={{0,12},{1,13},{2,14},{3,15},{4,0},{5,1},{6,2},{7,3},{8,4},{9,5},{1... | collective-permute-start | bytes 2457608 | tf_op jit(solution)/shard_map/ppermute | solution.py:52
  80.6 9.3 %collective-permute-done.25.a = s16[1568,128]{1,0:T(8,128)(2,1)S(1)} collective-permute-done((s16[1568,128]{1,0:T(8,128)(2,1)S(1)}, s16[1568,128]{1,0:T(8,128)(2,1)S(1)}, u32[]{:S(2)}, u32[]{:S(2)}) %collective-permute-start.25) | collective-permute-done | bytes 401440 | tf_op jit(solution)/shard_map/ppermute | solution.py:52
  89.9 2.0 %collective-permute-start.28 = (s16[1568,128]{1,0:T(8,128)(2,1)S(1)}, s16[1568,128]{1,0:T(8,128)(2,1)S(1)}, u32[]{:S(2)}, u32[]{:S(2)}) collective-permute-start(s16[1568,128]{1,0:T(8,128)(2,1)S(1)} %get-tuple-element.72), channel_id=1, source_target_pairs={{0,96},{1,97},{2,98},{3,99},{4,100},{5,101},{6,102},{7,103},{8,104... | collective-permute-start | bytes 1204232 | tf_op jit(solution)/shard_map/ppermute | solution.py:52
  93.3 4.5 %collective-permute-done.28.e = s16[1568,128]{1,0:T(8,128)(2,1)S(1)} collective-permute-done((s16[1568,128]{1,0:T(8,128)(2,1)S(1)}, s16[1568,128]{1,0:T(8,128)(2,1)S(1)}, u32[]{:S(2)}, u32[]{:S(2)}) %collective-permute-start.28) | collective-permute-done | bytes 401440 | tf_op jit(solution)/shard_map/ppermute | solution.py:52
  98.4 1.6 %collective-permute-start.29 = (s16[208,512]{1,0:T(8,128)(2,1)S(1)}, s16[208,512]{1,0:T(8,128)(2,1)S(1)}, u32[]{:S(2)}, u32[]{:S(2)}) collective-permute-start(s16[208,512]{1,0:T(8,128)(2,1)S(1)} %get-tuple-element.74), channel_id=1, source_target_pairs={{0,1},{1,2},{2,3},{3,0},{4,5},{5,6},{6,7},{7,4},{8,9},{9,10},{10,1... | collective-permute-start | bytes 638984 | tf_op jit(solution)/shard_map/ppermute | solution.py:52
  101.4 2.1 %collective-permute-start.17 = (s16[208,1024]{1,0:T(8,128)(2,1)S(1)}, s16[208,1024]{1,0:T(8,128)(2,1)S(1)}, u32[]{:S(2)}, u32[]{:S(2)}) collective-permute-start(s16[208,1024]{1,0:T(8,128)(2,1)S(1)} %get-tuple-element.56), channel_id=1, source_target_pairs={{0,1},{1,2},{2,3},{3,0},{4,5},{5,6},{6,7},{7,4},{8,9},{9,10},{10,1... | collective-permute-start | bytes 1277960 | tf_op jit(solution)/shard_map/ppermute | solution.py:52
  104.2 2.5 %collective-permute-start.19 = (s16[208,1024]{1,0:T(8,128)(2,1)S(1)}, s16[208,1024]{1,0:T(8,128)(2,1)S(1)}, u32[]{:S(2)}, u32[]{:S(2)}) collective-permute-start(s16[208,1024]{1,0:T(8,128)(2,1)S(1)} %get-tuple-element.58), channel_id=1, source_target_pairs={{0,3},{1,0},{2,1},{3,2},{4,7},{5,4},{6,5},{7,6},{8,11},{9,8},{10,9... | collective-permute-start | bytes 1277960 | tf_op jit(solution)/shard_map/ppermute | solution.py:52
  108.3 11.7 %collective-permute-done.30.b = s16[208,512]{1,0:T(8,128)(2,1)S(1)} collective-permute-done((s16[208,512]{1,0:T(8,128)(2,1)S(1)}, s16[208,512]{1,0:T(8,128)(2,1)S(1)}, u32[]{:S(2)}, u32[]{:S(2)}) %collective-permute-start.30) | collective-permute-done | bytes 213024 | tf_op jit(solution)/shard_map/ppermute | solution.py:52
  123.8 6.2 %collective-permute-start.21 = (s16[208,256]{1,0:T(8,128)(2,1)S(1)}, s16[208,256]{1,0:T(8,128)(2,1)S(1)}, u32[]{:S(2)}, u32[]{:S(2)}) collective-permute-start(s16[208,256]{1,0:T(8,128)(2,1)S(1)} %get-tuple-element.61), channel_id=1, source_target_pairs={{0,64},{1,65},{2,66},{3,67},{4,68},{5,69},{6,70},{7,71},{8,72},{9,... | collective-permute-start | bytes 319496 | tf_op jit(solution)/shard_map/ppermute | solution.py:52
  129.9 2.0 %collective-permute-start.22 = (s16[208,256]{1,0:T(8,128)(2,1)S(1)}, s16[208,256]{1,0:T(8,128)(2,1)S(1)}, u32[]{:S(2)}, u32[]{:S(2)}) collective-permute-start(s16[208,256]{1,0:T(8,128)(2,1)S(1)} %get-tuple-element.62), channel_id=1, source_target_pairs={{0,96},{1,97},{2,98},{3,99},{4,100},{5,101},{6,102},{7,103},{8,104... | collective-permute-start | bytes 319496 | tf_op jit(solution)/shard_map/ppermute | solution.py:52
  132.5 2.6 %collective-permute-start.34 = (s16[208,128]{1,0:T(8,128)(2,1)S(1)}, s16[208,128]{1,0:T(8,128)(2,1)S(1)}, u32[]{:S(2)}, u32[]{:S(2)}) collective-permute-start(s16[208,128]{1,0:T(8,128)(2,1)S(1)} %get-tuple-element.80), channel_id=1, source_target_pairs={{0,12},{1,13},{2,14},{3,15},{4,0},{5,1},{6,2},{7,3},{8,4},{9,5},{1... | collective-permute-start | bytes 159752 | tf_op jit(solution)/shard_map/ppermute | solution.py:52
  135.1 2.4 %collective-permute-done.33.rb = s16[208,128]{1,0:T(8,128)(2,1)S(1)} collective-permute-done((s16[208,128]{1,0:T(8,128)(2,1)S(1)}, s16[208,128]{1,0:T(8,128)(2,1)S(1)}, u32[]{:S(2)}, u32[]{:S(2)}) %collective-permute-start.33) | collective-permute-done | bytes 53280 | tf_op jit(solution)/shard_map/ppermute | solution.py:52
  (62 shorter events, 19.1 us)
Async XLA Ops:
  3.8 17.4 %collective-permute-start.1 = (bf16[6,16,3072]{2,1,0:T(8,128)(2,1)S(1)}, bf16[6,16,3072]{2,1,0:T(8,128)(2,1)S(1)}, u32[]{:S(2)}, u32[]{:S(2)}) collective-permute-start(bf16[6,16,3072]{2,1,0:T(8,128)(2,1)S(1)} %get-tuple-element.44), channel_id=1, source_target_pairs={{0,32},{1,33},{2,34},{3,35},{4,36},{5,37},{6,38},{7,39},{8,40},{9,... | collective-permute-start | bytes 1769480 | tf_op jit(solution)/shard_map/ppermute | solution.py:52
  5.8 29.3 %collective-permute-start.3 = (bf16[6,16,3072]{2,1,0:T(8,128)(2,1)S(1)}, bf16[6,16,3072]{2,1,0:T(8,128)(2,1)S(1)}, u32[]{:S(2)}, u32[]{:S(2)}) collective-permute-start(bf16[6,16,3072]{2,1,0:T(8,128)(2,1)S(1)} %get-tuple-element.45), channel_id=1, source_target_pairs={{0,64},{1,65},{2,66},{3,67},{4,68},{5,69},{6,70},{7,71},{8,72},{9,... | collective-permute-start | bytes 1769480 | tf_op jit(solution)/shard_map/ppermute | solution.py:52
  9.4 25.7 %collective-permute-start.5 = (bf16[6,16,3072]{2,1,0:T(8,128)(2,1)S(1)}, bf16[6,16,3072]{2,1,0:T(8,128)(2,1)S(1)}, u32[]{:S(2)}, u32[]{:S(2)}) collective-permute-start(bf16[6,16,3072]{2,1,0:T(8,128)(2,1)S(1)} %get-tuple-element.46), channel_id=1, source_target_pairs={{0,96},{1,97},{2,98},{3,99},{4,100},{5,101},{6,102},{7,103},{8,104... | collective-permute-start | bytes 1769480 | tf_op jit(solution)/shard_map/ppermute | solution.py:52
  10.4 41.4 %collective-permute-start = (bf16[6,16,3072]{2,1,0:T(8,128)(2,1)S(1)}, bf16[6,16,3072]{2,1,0:T(8,128)(2,1)S(1)}, u32[]{:S(2)}, u32[]{:S(2)}) collective-permute-start(bf16[6,16,3072]{2,1,0:T(8,128)(2,1)S(1)} %get-tuple-element.43.refs_0_), channel_id=1, source_target_pairs={{0,16},{1,17},{2,18},{3,19},{4,20},{5,21},{6,22},{7,23},{8,24},{9,... | collective-permute-start | bytes 1769480 | tf_op jit(solution)/shard_map/ppermute | solution.py:52
  21.2 30.5 %collective-permute-start.2 = (bf16[6,16,3072]{2,1,0:T(8,128)(2,1)S(1)}, bf16[6,16,3072]{2,1,0:T(8,128)(2,1)S(1)}, u32[]{:S(2)}, u32[]{:S(2)}) collective-permute-start(bf16[6,16,3072]{2,1,0:T(8,128)(2,1)S(1)} %collective-permute-done.1.refs_2_), channel_id=1, source_target_pairs={{0,16},{1,17},{2,18},{3,19},{4,20},{5,21},{6,22},{7,23},{8,24},{9,... | collective-permute-start | bytes 1769480 | tf_op jit(solution)/shard_map/ppermute | solution.py:52
  35.0 16.7 %collective-permute-start.4 = (bf16[6,16,3072]{2,1,0:T(8,128)(2,1)S(1)}, bf16[6,16,3072]{2,1,0:T(8,128)(2,1)S(1)}, u32[]{:S(2)}, u32[]{:S(2)}) collective-permute-start(bf16[6,16,3072]{2,1,0:T(8,128)(2,1)S(1)} %collective-permute-done.3.refs_4_), channel_id=1, source_target_pairs={{0,16},{1,17},{2,18},{3,19},{4,20},{5,21},{6,22},{7,23},{8,24},{9,... | collective-permute-start | bytes 1769480 | tf_op jit(solution)/shard_map/ppermute | solution.py:52
  35.0 16.7 %collective-permute-start.6 = (bf16[6,16,3072]{2,1,0:T(8,128)(2,1)S(1)}, bf16[6,16,3072]{2,1,0:T(8,128)(2,1)S(1)}, u32[]{:S(2)}, u32[]{:S(2)}) collective-permute-start(bf16[6,16,3072]{2,1,0:T(8,128)(2,1)S(1)} %collective-permute-done.5.refs_6_), channel_id=1, source_target_pairs={{0,16},{1,17},{2,18},{3,19},{4,20},{5,21},{6,22},{7,23},{8,24},{9,... | collective-permute-start | bytes 1769480 | tf_op jit(solution)/shard_map/ppermute | solution.py:52
  46.4 5.2 %collective-permute-start.9 = (bf16[32,128]{1,0:T(8,128)(2,1)S(1)}, bf16[32,128]{1,0:T(8,128)(2,1)S(1)}, u32[]{:S(2)}, u32[]{:S(2)}) collective-permute-start(bf16[32,128]{1,0:T(8,128)(2,1)S(1)} %constant_dynamic-update-slice_fusion.refs_0_), channel_id=1, source_target_pairs={{0,64},{1,65},{2,66},{3,67},{4,68},{5,69},{6,70},{7,71},{8,72},{9,... | collective-permute-start | bytes 24584 | tf_op jit(solution)/shard_map/ppermute | solution.py:52
  56.8 13.6 %collective-permute-start.11 = (s16[400,1024]{1,0:T(8,128)(2,1)S(1)}, s16[400,1024]{1,0:T(8,128)(2,1)S(1)}, u32[]{:S(2)}, u32[]{:S(2)}) collective-permute-start(s16[400,1024]{1,0:T(8,128)(2,1)S(1)} %get-tuple-element.49), channel_id=1, source_target_pairs={{0,4},{1,5},{2,6},{3,7},{4,8},{5,9},{6,10},{7,11},{8,12},{9,13},{1... | collective-permute-start | bytes 2457608 | tf_op jit(solution)/shard_map/ppermute | solution.py:52
  58.4 13.8 %collective-permute-start.12 = (s16[400,1024]{1,0:T(8,128)(2,1)S(1)}, s16[400,1024]{1,0:T(8,128)(2,1)S(1)}, u32[]{:S(2)}, u32[]{:S(2)}) collective-permute-start(s16[400,1024]{1,0:T(8,128)(2,1)S(1)} %get-tuple-element.50), channel_id=1, source_target_pairs={{0,12},{1,13},{2,14},{3,15},{4,0},{5,1},{6,2},{7,3},{8,4},{9,5},{1... | collective-permute-start | bytes 2457608 | tf_op jit(solution)/shard_map/ppermute | solution.py:52
  61.7 13.9 %collective-permute-start.23 = (s16[1568,128]{1,0:T(8,128)(2,1)S(1)}, s16[1568,128]{1,0:T(8,128)(2,1)S(1)}, u32[]{:S(2)}, u32[]{:S(2)}) collective-permute-start(s16[1568,128]{1,0:T(8,128)(2,1)S(1)} %get-tuple-element.66), channel_id=1, source_target_pairs={{0,32},{1,33},{2,34},{3,35},{4,36},{5,37},{6,38},{7,39},{8,40},{9,... | collective-permute-start | bytes 1204232 | tf_op jit(solution)/shard_map/ppermute | solution.py:52
  61.8 14.3 %collective-permute-start.24 = (s16[1568,128]{1,0:T(8,128)(2,1)S(1)}, s16[1568,128]{1,0:T(8,128)(2,1)S(1)}, u32[]{:S(2)}, u32[]{:S(2)}) collective-permute-start(s16[1568,128]{1,0:T(8,128)(2,1)S(1)} %get-tuple-element.68), channel_id=1, source_target_pairs={{0,96},{1,97},{2,98},{3,99},{4,100},{5,101},{6,102},{7,103},{8,104... | collective-permute-start | bytes 1204232 | tf_op jit(solution)/shard_map/ppermute | solution.py:52
  66.6 10.4 %collective-permute-start.26 = (s16[1568,128]{1,0:T(8,128)(2,1)S(1)}, s16[1568,128]{1,0:T(8,128)(2,1)S(1)}, u32[]{:S(2)}, u32[]{:S(2)}) collective-permute-start(s16[1568,128]{1,0:T(8,128)(2,1)S(1)} %get-tuple-element.70), channel_id=1, source_target_pairs={{0,96},{1,97},{2,98},{3,99},{4,100},{5,101},{6,102},{7,103},{8,104... | collective-permute-start | bytes 1204232 | tf_op jit(solution)/shard_map/ppermute | solution.py:52
  70.4 9.8 %collective-permute-start.27 = (s16[1568,128]{1,0:T(8,128)(2,1)S(1)}, s16[1568,128]{1,0:T(8,128)(2,1)S(1)}, u32[]{:S(2)}, u32[]{:S(2)}) collective-permute-start(s16[1568,128]{1,0:T(8,128)(2,1)S(1)} %get-tuple-element.71), channel_id=1, source_target_pairs={{0,32},{1,33},{2,34},{3,35},{4,36},{5,37},{6,38},{7,39},{8,40},{9,... | collective-permute-start | bytes 1204232 | tf_op jit(solution)/shard_map/ppermute | solution.py:52
  72.2 27.8 %collective-permute-start.14 = (s16[400,1024]{1,0:T(8,128)(2,1)S(1)}, s16[400,1024]{1,0:T(8,128)(2,1)S(1)}, u32[]{:S(2)}, u32[]{:S(2)}) collective-permute-start(s16[400,1024]{1,0:T(8,128)(2,1)S(1)} %get-tuple-element.52), channel_id=1, source_target_pairs={{0,12},{1,13},{2,14},{3,15},{4,0},{5,1},{6,2},{7,3},{8,4},{9,5},{1... | collective-permute-start | bytes 2457608 | tf_op jit(solution)/shard_map/ppermute | solution.py:52
  75.6 24.4 %collective-permute-start.15 = (s16[400,1024]{1,0:T(8,128)(2,1)S(1)}, s16[400,1024]{1,0:T(8,128)(2,1)S(1)}, u32[]{:S(2)}, u32[]{:S(2)}) collective-permute-start(s16[400,1024]{1,0:T(8,128)(2,1)S(1)} %get-tuple-element.53), channel_id=1, source_target_pairs={{0,4},{1,5},{2,6},{3,7},{4,8},{5,9},{6,10},{7,11},{8,12},{9,13},{1... | collective-permute-start | bytes 2457608 | tf_op jit(solution)/shard_map/ppermute | solution.py:52
  76.1 23.9 %collective-permute-start.13 = (s16[400,1024]{1,0:T(8,128)(2,1)S(1)}, s16[400,1024]{1,0:T(8,128)(2,1)S(1)}, u32[]{:S(2)}, u32[]{:S(2)}) collective-permute-start(s16[400,1024]{1,0:T(8,128)(2,1)S(1)} %get-tuple-element.51), channel_id=1, source_target_pairs={{0,4},{1,5},{2,6},{3,7},{4,8},{5,9},{6,10},{7,11},{8,12},{9,13},{1... | collective-permute-start | bytes 2457608 | tf_op jit(solution)/shard_map/ppermute | solution.py:52
  77.0 23.0 %collective-permute-start.16 = (s16[400,1024]{1,0:T(8,128)(2,1)S(1)}, s16[400,1024]{1,0:T(8,128)(2,1)S(1)}, u32[]{:S(2)}, u32[]{:S(2)}) collective-permute-start(s16[400,1024]{1,0:T(8,128)(2,1)S(1)} %get-tuple-element.54), channel_id=1, source_target_pairs={{0,12},{1,13},{2,14},{3,15},{4,0},{5,1},{6,2},{7,3},{8,4},{9,5},{1... | collective-permute-start | bytes 2457608 | tf_op jit(solution)/shard_map/ppermute | solution.py:52
  80.2 9.6 %collective-permute-start.25 = (s16[1568,128]{1,0:T(8,128)(2,1)S(1)}, s16[1568,128]{1,0:T(8,128)(2,1)S(1)}, u32[]{:S(2)}, u32[]{:S(2)}) collective-permute-start(s16[1568,128]{1,0:T(8,128)(2,1)S(1)} %get-tuple-element.69), channel_id=1, source_target_pairs={{0,32},{1,33},{2,34},{3,35},{4,36},{5,37},{6,38},{7,39},{8,40},{9,... | collective-permute-start | bytes 1204232 | tf_op jit(solution)/shard_map/ppermute | solution.py:52
  89.9 7.9 %collective-permute-start.28 = (s16[1568,128]{1,0:T(8,128)(2,1)S(1)}, s16[1568,128]{1,0:T(8,128)(2,1)S(1)}, u32[]{:S(2)}, u32[]{:S(2)}) collective-permute-start(s16[1568,128]{1,0:T(8,128)(2,1)S(1)} %get-tuple-element.72), channel_id=1, source_target_pairs={{0,96},{1,97},{2,98},{3,99},{4,100},{5,101},{6,102},{7,103},{8,104... | collective-permute-start | bytes 1204232 | tf_op jit(solution)/shard_map/ppermute | solution.py:52
  98.4 8.6 %collective-permute-start.29 = (s16[208,512]{1,0:T(8,128)(2,1)S(1)}, s16[208,512]{1,0:T(8,128)(2,1)S(1)}, u32[]{:S(2)}, u32[]{:S(2)}) collective-permute-start(s16[208,512]{1,0:T(8,128)(2,1)S(1)} %get-tuple-element.74), channel_id=1, source_target_pairs={{0,1},{1,2},{2,3},{3,0},{4,5},{5,6},{6,7},{7,4},{8,9},{9,10},{10,1... | collective-permute-start | bytes 638984 | tf_op jit(solution)/shard_map/ppermute | solution.py:52
  101.4 20.5 %collective-permute-start.17 = (s16[208,1024]{1,0:T(8,128)(2,1)S(1)}, s16[208,1024]{1,0:T(8,128)(2,1)S(1)}, u32[]{:S(2)}, u32[]{:S(2)}) collective-permute-start(s16[208,1024]{1,0:T(8,128)(2,1)S(1)} %get-tuple-element.56), channel_id=1, source_target_pairs={{0,1},{1,2},{2,3},{3,0},{4,5},{5,6},{6,7},{7,4},{8,9},{9,10},{10,1... | collective-permute-start | bytes 1277960 | tf_op jit(solution)/shard_map/ppermute | solution.py:52
  103.4 18.4 %collective-permute-start.18 = (s16[208,1024]{1,0:T(8,128)(2,1)S(1)}, s16[208,1024]{1,0:T(8,128)(2,1)S(1)}, u32[]{:S(2)}, u32[]{:S(2)}) collective-permute-start(s16[208,1024]{1,0:T(8,128)(2,1)S(1)} %get-tuple-element.57), channel_id=1, source_target_pairs={{0,2},{1,3},{2,0},{3,1},{4,6},{5,7},{6,4},{7,5},{8,10},{9,11},{10,... | collective-permute-start | bytes 1277960 | tf_op jit(solution)/shard_map/ppermute | solution.py:52
  104.2 17.6 %collective-permute-start.19 = (s16[208,1024]{1,0:T(8,128)(2,1)S(1)}, s16[208,1024]{1,0:T(8,128)(2,1)S(1)}, u32[]{:S(2)}, u32[]{:S(2)}) collective-permute-start(s16[208,1024]{1,0:T(8,128)(2,1)S(1)} %get-tuple-element.58), channel_id=1, source_target_pairs={{0,3},{1,0},{2,1},{3,2},{4,7},{5,4},{6,5},{7,6},{8,11},{9,8},{10,9... | collective-permute-start | bytes 1277960 | tf_op jit(solution)/shard_map/ppermute | solution.py:52
  106.8 13.3 %collective-permute-start.30 = (s16[208,512]{1,0:T(8,128)(2,1)S(1)}, s16[208,512]{1,0:T(8,128)(2,1)S(1)}, u32[]{:S(2)}, u32[]{:S(2)}) collective-permute-start(s16[208,512]{1,0:T(8,128)(2,1)S(1)} %get-tuple-element.75), channel_id=1, source_target_pairs={{0,2},{1,3},{2,0},{3,1},{4,6},{5,7},{6,4},{7,5},{8,10},{9,11},{10,... | collective-permute-start | bytes 638984 | tf_op jit(solution)/shard_map/ppermute | solution.py:52
  107.0 14.5 %collective-permute-start.31 = (s16[208,512]{1,0:T(8,128)(2,1)S(1)}, s16[208,512]{1,0:T(8,128)(2,1)S(1)}, u32[]{:S(2)}, u32[]{:S(2)}) collective-permute-start(s16[208,512]{1,0:T(8,128)(2,1)S(1)} %get-tuple-element.76), channel_id=1, source_target_pairs={{0,3},{1,0},{2,1},{3,2},{4,7},{5,4},{6,5},{7,6},{8,11},{9,8},{10,9... | collective-permute-start | bytes 638984 | tf_op jit(solution)/shard_map/ppermute | solution.py:52
  121.7 10.8 %collective-permute-start.32 = (s16[208,128]{1,0:T(8,128)(2,1)S(1)}, s16[208,128]{1,0:T(8,128)(2,1)S(1)}, u32[]{:S(2)}, u32[]{:S(2)}) collective-permute-start(s16[208,128]{1,0:T(8,128)(2,1)S(1)} %get-tuple-element.78), channel_id=1, source_target_pairs={{0,4},{1,5},{2,6},{3,7},{4,8},{5,9},{6,10},{7,11},{8,12},{9,13},{1... | collective-permute-start | bytes 159752 | tf_op jit(solution)/shard_map/ppermute | solution.py:52
  122.4 16.3 %collective-permute-start.20 = (s16[208,256]{1,0:T(8,128)(2,1)S(1)}, s16[208,256]{1,0:T(8,128)(2,1)S(1)}, u32[]{:S(2)}, u32[]{:S(2)}) collective-permute-start(s16[208,256]{1,0:T(8,128)(2,1)S(1)} %get-tuple-element.60), channel_id=1, source_target_pairs={{0,32},{1,33},{2,34},{3,35},{4,36},{5,37},{6,38},{7,39},{8,40},{9,... | collective-permute-start | bytes 319496 | tf_op jit(solution)/shard_map/ppermute | solution.py:52
  123.8 14.9 %collective-permute-start.21 = (s16[208,256]{1,0:T(8,128)(2,1)S(1)}, s16[208,256]{1,0:T(8,128)(2,1)S(1)}, u32[]{:S(2)}, u32[]{:S(2)}) collective-permute-start(s16[208,256]{1,0:T(8,128)(2,1)S(1)} %get-tuple-element.61), channel_id=1, source_target_pairs={{0,64},{1,65},{2,66},{3,67},{4,68},{5,69},{6,70},{7,71},{8,72},{9,... | collective-permute-start | bytes 319496 | tf_op jit(solution)/shard_map/ppermute | solution.py:52
  129.9 8.7 %collective-permute-start.22 = (s16[208,256]{1,0:T(8,128)(2,1)S(1)}, s16[208,256]{1,0:T(8,128)(2,1)S(1)}, u32[]{:S(2)}, u32[]{:S(2)}) collective-permute-start(s16[208,256]{1,0:T(8,128)(2,1)S(1)} %get-tuple-element.62), channel_id=1, source_target_pairs={{0,96},{1,97},{2,98},{3,99},{4,100},{5,101},{6,102},{7,103},{8,104... | collective-permute-start | bytes 319496 | tf_op jit(solution)/shard_map/ppermute | solution.py:52
  131.9 5.6 %collective-permute-start.33 = (s16[208,128]{1,0:T(8,128)(2,1)S(1)}, s16[208,128]{1,0:T(8,128)(2,1)S(1)}, u32[]{:S(2)}, u32[]{:S(2)}) collective-permute-start(s16[208,128]{1,0:T(8,128)(2,1)S(1)} %get-tuple-element.79), channel_id=1, source_target_pairs={{0,8},{1,9},{2,10},{3,11},{4,12},{5,13},{6,14},{7,15},{8,0},{9,1},... | collective-permute-start | bytes 159752 | tf_op jit(solution)/shard_map/ppermute | solution.py:52
  132.5 6.1 %collective-permute-start.34 = (s16[208,128]{1,0:T(8,128)(2,1)S(1)}, s16[208,128]{1,0:T(8,128)(2,1)S(1)}, u32[]{:S(2)}, u32[]{:S(2)}) collective-permute-start(s16[208,128]{1,0:T(8,128)(2,1)S(1)} %get-tuple-element.80), channel_id=1, source_target_pairs={{0,12},{1,13},{2,14},{3,15},{4,0},{5,1},{6,2},{7,3},{8,4},{9,5},{1... | collective-permute-start | bytes 159752 | tf_op jit(solution)/shard_map/ppermute | solution.py:52
  (5 other events, 46.4 us)
where the time goes:
time: 140 us; the launch traced here: 139 us
  waiting for transfers between devices  73.1 us (52%)
  starting transfers between devices  45.2 us (32%)
  Pallas kernels  20.3 us (14%)
    ppermute x35, waiting for transfers between devices, send(): return lax.ppermute(v, AXES, moves(shift))  73.1 us
    ppermute x35, starting transfers between devices, send(): return lax.ppermute(v, AXES, moves(shift))  45.2 us
    pallas_call x4, Pallas kernels, bulk_k(): pl.pallas_call(functools.partial(bulk_body, blocks), out_shape=[jax.Shape...  6.58 us
    pallas_call x1, Pallas kernels, fit(): pl.pallas_call(fit_body, grid=(group,), out_shape=[jax.ShapeDtypeStruct((...  3.31 us
    pallas_call x2, Pallas kernels, rest_k(): pl.pallas_call(functools.partial(rest_body, slot, cut), out_shape=[jax.Sh...  3.15 us
    pallas_call x1, Pallas kernels, screen(): pl.pallas_call(screen_body, out_shape=[out] * RING, in_specs=[scalars(),...  3.12 us
  transfers between devices with their start and end apart: 35, of which 14 were waited for; matrix products, arithmetic and copies ran while one was open for 0% of the time, Pallas kernels for 8%

commit v1 on v0

--- a/solution.py
+++ b/solution.py
@@ -15,8 +15,7 @@
 I16 = jnp.int16
 MIB = 1 << 20
 RING = 4
-ORDER = (2, 0, 1, 3)
-TAIL = 16
+TAIL = 8
 
 
 def whole():
@@ -148,20 +147,22 @@
 
 
 def fit_body(*refs):
-    pieces, mixed, (bulk, rest, turned, fresh) = refs[:8], refs[8], refs[9:]
+    pieces, mixed, (bulk, rest, turned) = refs[:8], refs[8], refs[9:]
     at = position()
     step = pl.program_id(0)
-    ao = fresh.shape[1]
+    ao = turned.shape[0]
     aux = mixed.shape[0]
     screened = jnp.concatenate([p[0] for p in pieces], axis=0)
     fitted = jnp.dot(mixed[...], screened, preferred_element_type=F32).astype(BF)
-    fresh[...] = fitted
     wide, narrow = bulk.shape[1] // RING, rest.shape[1] // RING
+
+    def chosen(column, lanes):
+        first, second = column, column + wide + narrow
+        return jnp.where(at[1] == 0, fitted[:, first:first + lanes], fitted[:, second:second + lanes])
+
     for n in range(RING):
-        column = n * (ao // RING) + at[1] * (wide + narrow)
-        bulk[:, n * wide:(n + 1) * wide] = fresh[:, pl.ds(pl.multiple_of(column, 128), wide)]
-        column = lax.rem(at[0] + ORDER[n], RING) * (ao // RING) + at[1] * (wide + narrow) + wide
-        rest[:, n * narrow:(n + 1) * narrow] = fresh[:, pl.ds(pl.multiple_of(column, 128), narrow)]
+        bulk[:, n * wide:(n + 1) * wide] = chosen(n * (ao // RING), wide)
+        rest[:, n * narrow:(n + 1) * narrow] = chosen(n * (ao // RING) + wide, narrow)
     flipped = fitted.T
     cut = pl.ds(pl.multiple_of(step * aux, aux), aux)
     high = ao // (RING * RING)
@@ -184,7 +185,6 @@
         in_specs=[piece] * 8 + [whole()],
         out_specs=[pl.BlockSpec((aux, n), lambda i: (i, 0)) for n in (ao // 3, ao // 6)]
         + [pl.BlockSpec((ao, group * aux), lambda i: (0, 0))],
-        scratch_shapes=[pltpu.VMEM((aux, ao), BF)],
         compiler_params=params(28),
         cost_estimate=cost(2 * group * aux * aux * ao, group * aux * ao * 6),
         name="fit",
@@ -211,14 +211,15 @@
     return q.astype(jnp.int32).astype(F32)
 
 
-def write(out, first, block):
+def write(out, first, block, tail=None):
+    end = first + block.shape[0]
     if out.dtype == F32:
-        out[first:first + block.shape[0], :] = block
+        out[first:end, :] = block
     else:
         e = exponent(jnp.max(jnp.abs(block), axis=0, keepdims=True))
-        end = first + block.shape[0]
+        tail = end if tail is None else tail
         out[first:end, :] = coded(block, e)
-        out[end:end + TAIL, :] = marked(e)
+        out[tail:tail + TAIL, :] = marked(e)
 
 
 def bulk_body(blocks, bulk, turned, *refs):
@@ -258,20 +259,22 @@
     )(bulk, turned, *arrived)
 
 
-def rest_body(slot, cut, rest, turned, *outs):
+def rest_body(steps, cut, rest, turned, *outs):
+    at = position()
     narrow = rest.shape[1] // RING
     total = turned.shape[0] // RING
-    right = rest[:, slot * narrow:(slot + 2) * narrow]
+    right = jnp.concatenate(
+        [rest[:, pl.ds(pl.multiple_of(lax.rem(at[0] + k, RING) * narrow, 128), narrow)] for k in steps], axis=1
+    )
     for g in range(RING):
         block = jnp.dot(turned[g * total:(g + 1) * total, :], right, preferred_element_type=F32)
         for n in range(2):
             out = outs[cut[n][g // 2]]
-            size = total if out.dtype == F32 else total + TAIL
-            whole_block = out.shape[0] == RING * total
-            write(out, (g if whole_block else g % 2) * size, block[:, n * narrow:(n + 1) * narrow])
-
-
-def rest_k(rest, turned, slot, cut, kinds):
+            row = g if out.shape[0] == RING * total else g % 2
+            write(out, row * total, block[:, n * narrow:(n + 1) * narrow], 2 * total + g % 2 * TAIL)
+
+
+def rest_k(rest, turned, steps, cut, kinds):
     depth = rest.shape[0]
     ao = turned.shape[0]
     narrow = rest.shape[1] // RING
@@ -279,7 +282,7 @@
         "message": ((ao // 2 + 2 * TAIL, narrow), I16), "half": ((ao // 2, narrow), F32), "all": ((ao, narrow), F32)
     }
     return pl.pallas_call(
-        functools.partial(rest_body, slot, cut),
+        functools.partial(rest_body, steps, cut),
         out_shape=[jax.ShapeDtypeStruct(*shapes[kind]) for kind in kinds],
         in_specs=[whole()] * 2,
         out_specs=[whole()] * len(kinds),
@@ -292,11 +295,11 @@
     for own, arrived, out in ((refs[0], refs[1], refs[4]), (refs[2], refs[3], refs[5])):
         total = own.shape[0] // 2
         for g in range(2):
-            first = g * (total + TAIL)
-            v = own[g * total:(g + 1) * total, :] + plain(arrived[first:first + total, :]) * scale_of(
-                arrived[first + total:first + total + TAIL, :]
+            first, tail = g * total, 2 * total + g * TAIL
+            v = own[first:first + total, :] + plain(arrived[first:first + total, :]) * scale_of(
+                arrived[tail:tail + TAIL, :]
             )
-            write(out, first, v)
+            write(out, first, v, tail)
 
 
 def rest_mid(up, arrived_up, down, arrived_down):
@@ -329,10 +332,8 @@
         row = lax.rem(h + k, RING) * high
         out = kept if k == 0 else outs[k - 1]
         for n in range(RING):
-            start = n % 2 * (total + TAIL)
-            v = gathered(
-                own, (a, b) if n < 2 else (d, e), (n * total, start, high), start + total, row, slice(0, step)
-            )
+            start, tail = n % 2 * total, 2 * total + n % 2 * TAIL
+            v = gathered(own, (a, b) if n < 2 else (d, e), (n * total, start, high), tail, row, slice(0, step))
             write(out.at[:, n * step:(n + 1) * step], 0, v)
 
 
@@ -483,12 +484,12 @@
             parts[k] = send(parts[k], shift(k))
 
     far = near(first_axis, *bulk_step((2, 0, False), (2, 1, False)))
+    upper, lower, rest_own = rest_step((2, 0), ((0, 1), (2, 2)), ("message", "message", "all"))
+    rest_far = near(along_z, upper, lower)
     lower_up, upper_down = near(first_axis, *bulk_step((1, 1, False), (3, 0, False)))
-    upper, lower, rest_own = rest_step(0, ((0, 1), (2, 2)), ("message", "message", "all"))
-    rest_far = near(along_z, upper, lower)
+    keep_up, up, down, keep_down = rest_step((1, 3), ((0, 1), (2, 3)), ("half", "message", "message", "half"))
+    rest_near = near(along_z, up, down)
     upper_up, lower_down = near(first_axis, *bulk_step((1, 0, True), (3, 1, True), arrived=far))
-    keep_up, up, down, keep_down = rest_step(2, ((0, 1), (2, 3)), ("half", "message", "message", "half"))
-    rest_near = near(along_z, up, down)
     up, down = rest_mid(keep_up, rest_far[0], keep_down, rest_far[1])
     mid = near(along_z, up, down)
     own = bulk_step((0, None, False))[0]

time: 140 us -> 138 us (0.986)
  no operation moved by 1% of the time
where the time goes in v1:
time: 138 us; the launch traced here: 137 us
  waiting for transfers between devices  72.3 us (52%)
  starting transfers between devices  44.6 us (32%)
  Pallas kernels  19.6 us (14%)
    ppermute x35, waiting for transfers between devices, send(): return lax.ppermute(v, AXES, moves(shift))  72.3 us
    ppermute x35, starting transfers between devices, send(): return lax.ppermute(v, AXES, moves(shift))  44.6 us
    pallas_call x4, Pallas kernels, bulk_k(): pl.pallas_call(functools.partial(bulk_body, blocks), out_shape=[jax.Shape...  6.55 us
    pallas_call x2, Pallas kernels, rest_k(): pl.pallas_call(functools.partial(rest_body, steps, cut), out_shape=[jax.S...  3.17 us
    pallas_call x1, Pallas kernels, screen(): pl.pallas_call(screen_body, out_shape=[out] * RING, in_specs=[scalars(),...  3.12 us
  transfers between devices with their start and end apart: 35, of which 14 were waited for; matrix products, arithmetic and copies ran while one was open for 0% of the time, Pallas kernels for 8%

profile of v1, /device:TPU:8, one launch (start us, length us, event | category | flops | bytes accessed | tf_op | source)
XLA Modules:
  0.0 137.4 jit_solution(3712736140456341683)
XLA Ops:
  0.7 3.1 %screen.1 = (bf16[6,16,3072]{2,1,0:T(8,128)(2,1)S(1)}, bf16[6,16,3072]{2,1,0:T(8,128)(2,1)S(1)}, bf16[6,16,3072]{2,1,0:T(8,128)(2,1)S(1)}, bf16[6,16,3072]{2,1,0:T(8,128)(2,1)S(1)}) custom-call(s32[1,1,24]{2,1,0:T(1,128)S(1)} %copy-done.1, bf16[16,24,3072]{2,1,0:T(8,128)(2,1)} %half.1), custom_call_target="tpu_custom_call" | custom-call | flops 1179648 | bytes 4718592 | tf_op jit(solution)/shard_map/screen/pallas_call | solution.py:104
  3.8 2.0 %collective-permute-start.1 = (bf16[6,16,3072]{2,1,0:T(8,128)(2,1)S(1)}, bf16[6,16,3072]{2,1,0:T(8,128)(2,1)S(1)}, u32[]{:S(2)}, u32[]{:S(2)}) collective-permute-start(bf16[6,16,3072]{2,1,0:T(8,128)(2,1)S(1)} %get-tuple-element.44), channel_id=1, source_target_pairs={{0,32},{1,33},{2,34},{3,35},{4,36},{5,37},{6,38},{7,39},{8,40},{9,... | collective-permute-start | bytes 1769480 | tf_op jit(solution)/shard_map/ppermute | solution.py:51
  5.8 3.6 %collective-permute-start.3 = (bf16[6,16,3072]{2,1,0:T(8,128)(2,1)S(1)}, bf16[6,16,3072]{2,1,0:T(8,128)(2,1)S(1)}, u32[]{:S(2)}, u32[]{:S(2)}) collective-permute-start(bf16[6,16,3072]{2,1,0:T(8,128)(2,1)S(1)} %get-tuple-element.45), channel_id=1, source_target_pairs={{0,64},{1,65},{2,66},{3,67},{4,68},{5,69},{6,70},{7,71},{8,72},{9,... | collective-permute-start | bytes 1769480 | tf_op jit(solution)/shard_map/ppermute | solution.py:51
  10.4 10.9 %collective-permute-done.1.refs_2_ = bf16[6,16,3072]{2,1,0:T(8,128)(2,1)S(1)} collective-permute-done((bf16[6,16,3072]{2,1,0:T(8,128)(2,1)S(1)}, bf16[6,16,3072]{2,1,0:T(8,128)(2,1)S(1)}, u32[]{:S(2)}, u32[]{:S(2)}) %collective-permute-start.1) | collective-permute-done | bytes 589856 | tf_op jit(solution)/shard_map/ppermute | solution.py:51
  21.2 13.8 %collective-permute-done.3.refs_4_ = bf16[6,16,3072]{2,1,0:T(8,128)(2,1)S(1)} collective-permute-done((bf16[6,16,3072]{2,1,0:T(8,128)(2,1)S(1)}, bf16[6,16,3072]{2,1,0:T(8,128)(2,1)S(1)}, u32[]{:S(2)}, u32[]{:S(2)}) %collective-permute-start.3) | collective-permute-done | bytes 589856 | tf_op jit(solution)/shard_map/ppermute | solution.py:51
  35.6 2.2 %collective-permute-done.7 = bf16[16,128]{1,0:T(8,128)(2,1)S(1)} collective-permute-done((bf16[16,128]{1,0:T(8,128)(2,1)S(1)}, bf16[16,128]{1,0:T(8,128)(2,1)S(1)}, u32[]{:S(2)}, u32[]{:S(2)}) %collective-permute-start.7) | collective-permute-done | bytes 4128 | tf_op jit(solution)/shard_map/ppermute | solution.py:51
  39.2 2.3 %collective-permute-done.10.refs_3_ = bf16[32,128]{1,0:T(8,128)(2,1)S(1)} collective-permute-done((bf16[32,128]{1,0:T(8,128)(2,1)S(1)}, bf16[32,128]{1,0:T(8,128)(2,1)S(1)}, u32[]{:S(2)}, u32[]{:S(2)}) %collective-permute-start.10) | collective-permute-done | bytes 8224 | tf_op jit(solution)/shard_map/ppermute | solution.py:51
  41.9 4.5 %collective-permute-done.8.refs_1_ = bf16[32,128]{1,0:T(8,128)(2,1)S(1)} collective-permute-done((bf16[32,128]{1,0:T(8,128)(2,1)S(1)}, bf16[32,128]{1,0:T(8,128)(2,1)S(1)}, u32[]{:S(2)}, u32[]{:S(2)}) %collective-permute-start.8) | collective-permute-done | bytes 8224 | tf_op jit(solution)/shard_map/ppermute | solution.py:51
  46.9 4.7 %collective-permute-done.9.refs_2_ = bf16[32,128]{1,0:T(8,128)(2,1)S(1)} collective-permute-done((bf16[32,128]{1,0:T(8,128)(2,1)S(1)}, bf16[32,128]{1,0:T(8,128)(2,1)S(1)}, u32[]{:S(2)}, u32[]{:S(2)}) %collective-permute-start.9) | collective-permute-done | bytes 8224 | tf_op jit(solution)/shard_map/ppermute | solution.py:51
  51.8 2.6 %fit.1 = (bf16[768,1024]{1,0:T(8,128)(2,1)S(1)}, bf16[768,512]{1,0:T(8,128)(2,1)S(1)}, bf16[3072,768]{1,0:T(8,128)(2,1)S(1)}) custom-call(bf16[6,16,3072]{2,1,0:T(8,128)(2,1)S(1)} %get-tuple-element.43.refs_0_, bf16[6,16,3072]{2,1,0:T(8,128)(2,1)S(1)} %collective-permute-done.refs_1_, bf16[6,16,3072]{2,1,0:T(8,128)(2,1)S(1)} %collective-permute-done.1.refs_2_, ...), custom_call_target="tpu_custom_call" | custom-call | flops 603979776 | bytes 14155776 | tf_op jit(solution)/shard_map/fit/pallas_call | solution.py:180
  54.4 1.7 %shard_map.38 = (s16[392,1024]{1,0:T(8,128)(2,1)S(1)}, s16[392,1024]{1,0:T(8,128)(2,1)S(1)}) custom-call(bf16[768,1024]{1,0:T(8,128)(2,1)S(1)} %get-tuple-element.47.bulk, bf16[3072,768]{1,0:T(8,128)(2,1)S(1)} %get-tuple-element.48.turned), custom_call_target="tpu_custom_call" | custom-call | flops 1207959552 | bytes 1572864 | tf_op jit(solution)/shard_map/pallas_call | solution.py:249
  57.7 1.7 %collective-permute-start.12 = (s16[392,1024]{1,0:T(8,128)(2,1)S(1)}, s16[392,1024]{1,0:T(8,128)(2,1)S(1)}, u32[]{:S(2)}, u32[]{:S(2)}) collective-permute-start(s16[392,1024]{1,0:T(8,128)(2,1)S(1)} %get-tuple-element.50), channel_id=1, source_target_pairs={{0,12},{1,13},{2,14},{3,15},{4,0},{5,1},{6,2},{7,3},{8,4},{9,5},{1... | collective-permute-start | bytes 2408456 | tf_op jit(solution)/shard_map/ppermute | solution.py:51
  59.5 1.6 %shard_map.41 = (s16[1552,128]{1,0:T(8,128)(2,1)S(1)}, s16[1552,128]{1,0:T(8,128)(2,1)S(1)}, f32[3072,128]{1,0:T(8,128)S(1)}) custom-call(bf16[768,512]{1,0:T(8,128)(2,1)S(1)} %get-tuple-element.63.rest, bf16[3072,768]{1,0:T(8,128)(2,1)S(1)} %get-tuple-element.48.turned), custom_call_target="tpu_custom_call" | custom-call | flops 1207959552 | bytes 1572864 | tf_op jit(solution)/shard_map/pallas_call | solution.py:284
  61.1 3.2 %collective-permute-start.24 = (s16[1552,128]{1,0:T(8,128)(2,1)S(1)}, s16[1552,128]{1,0:T(8,128)(2,1)S(1)}, u32[]{:S(2)}, u32[]{:S(2)}) collective-permute-start(s16[1552,128]{1,0:T(8,128)(2,1)S(1)} %get-tuple-element.68), channel_id=1, source_target_pairs={{0,96},{1,97},{2,98},{3,99},{4,100},{5,101},{6,102},{7,103},{8,104... | collective-permute-start | bytes 1191944 | tf_op jit(solution)/shard_map/ppermute | solution.py:51
  64.4 1.6 %shard_map.42 = (f32[1536,128]{1,0:T(8,128)S(1)}, s16[1552,128]{1,0:T(8,128)(2,1)S(1)}, s16[1552,128]{1,0:T(8,128)(2,1)S(1)}, f32[1536,128]{1,0:T(8,128)S(1)}) custom-call(bf16[768,512]{1,0:T(8,128)(2,1)S(1)} %get-tuple-element.63.rest, bf16[3072,768]{1,0:T(8,128)(2,1)S(1)} %get-tuple-element.48.turned), custom_call_target="tpu_custom_call" | custom-call | flops 1207959552 | bytes 1572864 | tf_op jit(solution)/shard_map/pallas_call | solution.py:284
  66.1 3.5 %collective-permute-done.11.refs_0_ = s16[392,1024]{1,0:T(8,128)(2,1)S(1)} collective-permute-done((s16[392,1024]{1,0:T(8,128)(2,1)S(1)}, s16[392,1024]{1,0:T(8,128)(2,1)S(1)}, u32[]{:S(2)}, u32[]{:S(2)}) %collective-permute-start.11) | collective-permute-done | bytes 802848 | tf_op jit(solution)/shard_map/ppermute | solution.py:51
  69.6 1.7 %shard_map.40 = (s16[392,1024]{1,0:T(8,128)(2,1)S(1)}, s16[392,1024]{1,0:T(8,128)(2,1)S(1)}) custom-call(bf16[768,1024]{1,0:T(8,128)(2,1)S(1)} %get-tuple-element.47.bulk, bf16[3072,768]{1,0:T(8,128)(2,1)S(1)} %get-tuple-element.48.turned), custom_call_target="tpu_custom_call" | custom-call | flops 1207959552 | bytes 1572864 | tf_op jit(solution)/shard_map/pallas_call | solution.py:249
  71.3 1.6 %collective-permute-start.14 = (s16[392,1024]{1,0:T(8,128)(2,1)S(1)}, s16[392,1024]{1,0:T(8,128)(2,1)S(1)}, u32[]{:S(2)}, u32[]{:S(2)}) collective-permute-start(s16[392,1024]{1,0:T(8,128)(2,1)S(1)} %get-tuple-element.52), channel_id=1, source_target_pairs={{0,12},{1,13},{2,14},{3,15},{4,0},{5,1},{6,2},{7,3},{8,4},{9,5},{1... | collective-permute-start | bytes 2408456 | tf_op jit(solution)/shard_map/ppermute | solution.py:51
  73.0 1.7 %shard_map.39 = (s16[392,1024]{1,0:T(8,128)(2,1)S(1)}, s16[392,1024]{1,0:T(8,128)(2,1)S(1)}) custom-call(bf16[768,1024]{1,0:T(8,128)(2,1)S(1)} %get-tuple-element.47.bulk, bf16[3072,768]{1,0:T(8,128)(2,1)S(1)} %get-tuple-element.48.turned, s16[392,1024]{1,0:T(8,128)(2,1)S(1)} %collective-permute-done.11.refs_0_, ...), custom_call_target="tpu_custom_call" | custom-call | flops 1207959552 | bytes 1572864 | tf_op jit(solution)/shard_map/pallas_call | solution.py:249
  76.1 2.8 %collective-permute-start.16 = (s16[392,1024]{1,0:T(8,128)(2,1)S(1)}, s16[392,1024]{1,0:T(8,128)(2,1)S(1)}, u32[]{:S(2)}, u32[]{:S(2)}) collective-permute-start(s16[392,1024]{1,0:T(8,128)(2,1)S(1)} %get-tuple-element.54), channel_id=1, source_target_pairs={{0,12},{1,13},{2,14},{3,15},{4,0},{5,1},{6,2},{7,3},{8,4},{9,5},{1... | collective-permute-start | bytes 2408456 | tf_op jit(solution)/shard_map/ppermute | solution.py:51
  79.7 9.2 %collective-permute-done.25.a = s16[1552,128]{1,0:T(8,128)(2,1)S(1)} collective-permute-done((s16[1552,128]{1,0:T(8,128)(2,1)S(1)}, s16[1552,128]{1,0:T(8,128)(2,1)S(1)}, u32[]{:S(2)}, u32[]{:S(2)}) %collective-permute-start.25) | collective-permute-done | bytes 397344 | tf_op jit(solution)/shard_map/ppermute | solution.py:51
  89.0 2.0 %collective-permute-start.28 = (s16[1552,128]{1,0:T(8,128)(2,1)S(1)}, s16[1552,128]{1,0:T(8,128)(2,1)S(1)}, u32[]{:S(2)}, u32[]{:S(2)}) collective-permute-start(s16[1552,128]{1,0:T(8,128)(2,1)S(1)} %get-tuple-element.72), channel_id=1, source_target_pairs={{0,96},{1,97},{2,98},{3,99},{4,100},{5,101},{6,102},{7,103},{8,104... | collective-permute-start | bytes 1191944 | tf_op jit(solution)/shard_map/ppermute | solution.py:51
  92.4 4.4 %collective-permute-done.28.e = s16[1552,128]{1,0:T(8,128)(2,1)S(1)} collective-permute-done((s16[1552,128]{1,0:T(8,128)(2,1)S(1)}, s16[1552,128]{1,0:T(8,128)(2,1)S(1)}, u32[]{:S(2)}, u32[]{:S(2)}) %collective-permute-start.28) | collective-permute-done | bytes 397344 | tf_op jit(solution)/shard_map/ppermute | solution.py:51
  97.4 1.6 %collective-permute-start.29 = (s16[200,512]{1,0:T(8,128)(2,1)S(1)}, s16[200,512]{1,0:T(8,128)(2,1)S(1)}, u32[]{:S(2)}, u32[]{:S(2)}) collective-permute-start(s16[200,512]{1,0:T(8,128)(2,1)S(1)} %get-tuple-element.74), channel_id=1, source_target_pairs={{0,1},{1,2},{2,3},{3,0},{4,5},{5,6},{6,7},{7,4},{8,9},{9,10},{10,1... | collective-permute-start | bytes 614408 | tf_op jit(solution)/shard_map/ppermute | solution.py:51
  103.0 2.4 %collective-permute-start.19 = (s16[200,1024]{1,0:T(8,128)(2,1)S(1)}, s16[200,1024]{1,0:T(8,128)(2,1)S(1)}, u32[]{:S(2)}, u32[]{:S(2)}) collective-permute-start(s16[200,1024]{1,0:T(8,128)(2,1)S(1)} %get-tuple-element.58), channel_id=1, source_target_pairs={{0,3},{1,0},{2,1},{3,2},{4,7},{5,4},{6,5},{7,6},{8,11},{9,8},{10,9... | collective-permute-start | bytes 1228808 | tf_op jit(solution)/shard_map/ppermute | solution.py:51
  105.5 1.6 %collective-permute-start.31 = (s16[200,512]{1,0:T(8,128)(2,1)S(1)}, s16[200,512]{1,0:T(8,128)(2,1)S(1)}, u32[]{:S(2)}, u32[]{:S(2)}) collective-permute-start(s16[200,512]{1,0:T(8,128)(2,1)S(1)} %get-tuple-element.76), channel_id=1, source_target_pairs={{0,3},{1,0},{2,1},{3,2},{4,7},{5,4},{6,5},{7,6},{8,11},{9,8},{10,9... | collective-permute-start | bytes 614408 | tf_op jit(solution)/shard_map/ppermute | solution.py:51
  107.1 11.0 %collective-permute-done.30.b = s16[200,512]{1,0:T(8,128)(2,1)S(1)} collective-permute-done((s16[200,512]{1,0:T(8,128)(2,1)S(1)}, s16[200,512]{1,0:T(8,128)(2,1)S(1)}, u32[]{:S(2)}, u32[]{:S(2)}) %collective-permute-start.30) | collective-permute-done | bytes 204832 | tf_op jit(solution)/shard_map/ppermute | solution.py:51
  118.1 1.6 %collective-permute-done.31.d = s16[200,512]{1,0:T(8,128)(2,1)S(1)} collective-permute-done((s16[200,512]{1,0:T(8,128)(2,1)S(1)}, s16[200,512]{1,0:T(8,128)(2,1)S(1)}, u32[]{:S(2)}, u32[]{:S(2)}) %collective-permute-start.31) | collective-permute-done | bytes 204832 | tf_op jit(solution)/shard_map/ppermute | solution.py:51
  121.8 6.2 %collective-permute-start.21 = (s16[200,256]{1,0:T(8,128)(2,1)S(1)}, s16[200,256]{1,0:T(8,128)(2,1)S(1)}, u32[]{:S(2)}, u32[]{:S(2)}) collective-permute-start(s16[200,256]{1,0:T(8,128)(2,1)S(1)} %get-tuple-element.61), channel_id=1, source_target_pairs={{0,64},{1,65},{2,66},{3,67},{4,68},{5,69},{6,70},{7,71},{8,72},{9,... | collective-permute-start | bytes 307208 | tf_op jit(solution)/shard_map/ppermute | solution.py:51
  127.9 1.9 %collective-permute-start.22 = (s16[200,256]{1,0:T(8,128)(2,1)S(1)}, s16[200,256]{1,0:T(8,128)(2,1)S(1)}, u32[]{:S(2)}, u32[]{:S(2)}) collective-permute-start(s16[200,256]{1,0:T(8,128)(2,1)S(1)} %get-tuple-element.62), channel_id=1, source_target_pairs={{0,96},{1,97},{2,98},{3,99},{4,100},{5,101},{6,102},{7,103},{8,104... | collective-permute-start | bytes 307208 | tf_op jit(solution)/shard_map/ppermute | solution.py:51
  129.8 3.2 %collective-permute-start.34 = (s16[200,128]{1,0:T(8,128)(2,1)S(1)}, s16[200,128]{1,0:T(8,128)(2,1)S(1)}, u32[]{:S(2)}, u32[]{:S(2)}) collective-permute-start(s16[200,128]{1,0:T(8,128)(2,1)S(1)} %get-tuple-element.80), channel_id=1, source_target_pairs={{0,12},{1,13},{2,14},{3,15},{4,0},{5,1},{6,2},{7,3},{8,4},{9,5},{1... | collective-permute-start | bytes 153608 | tf_op jit(solution)/shard_map/ppermute | solution.py:51
  133.1 2.4 %collective-permute-done.33.rb = s16[200,128]{1,0:T(8,128)(2,1)S(1)} collective-permute-done((s16[200,128]{1,0:T(8,128)(2,1)S(1)}, s16[200,128]{1,0:T(8,128)(2,1)S(1)}, u32[]{:S(2)}, u32[]{:S(2)}) %collective-permute-start.33) | collective-permute-done | bytes 51232 | tf_op jit(solution)/shard_map/ppermute | solution.py:51
  (62 shorter events, 18.6 us)
Async XLA Ops:
  3.8 17.4 %collective-permute-start.1 = (bf16[6,16,3072]{2,1,0:T(8,128)(2,1)S(1)}, bf16[6,16,3072]{2,1,0:T(8,128)(2,1)S(1)}, u32[]{:S(2)}, u32[]{:S(2)}) collective-permute-start(bf16[6,16,3072]{2,1,0:T(8,128)(2,1)S(1)} %get-tuple-element.44), channel_id=1, source_target_pairs={{0,32},{1,33},{2,34},{3,35},{4,36},{5,37},{6,38},{7,39},{8,40},{9,... | collective-permute-start | bytes 1769480 | tf_op jit(solution)/shard_map/ppermute | solution.py:51
  5.8 29.3 %collective-permute-start.3 = (bf16[6,16,3072]{2,1,0:T(8,128)(2,1)S(1)}, bf16[6,16,3072]{2,1,0:T(8,128)(2,1)S(1)}, u32[]{:S(2)}, u32[]{:S(2)}) collective-permute-start(bf16[6,16,3072]{2,1,0:T(8,128)(2,1)S(1)} %get-tuple-element.45), channel_id=1, source_target_pairs={{0,64},{1,65},{2,66},{3,67},{4,68},{5,69},{6,70},{7,71},{8,72},{9,... | collective-permute-start | bytes 1769480 | tf_op jit(solution)/shard_map/ppermute | solution.py:51
  9.4 25.7 %collective-permute-start.5 = (bf16[6,16,3072]{2,1,0:T(8,128)(2,1)S(1)}, bf16[6,16,3072]{2,1,0:T(8,128)(2,1)S(1)}, u32[]{:S(2)}, u32[]{:S(2)}) collective-permute-start(bf16[6,16,3072]{2,1,0:T(8,128)(2,1)S(1)} %get-tuple-element.46), channel_id=1, source_target_pairs={{0,96},{1,97},{2,98},{3,99},{4,100},{5,101},{6,102},{7,103},{8,104... | collective-permute-start | bytes 1769480 | tf_op jit(solution)/shard_map/ppermute | solution.py:51
  10.4 41.4 %collective-permute-start = (bf16[6,16,3072]{2,1,0:T(8,128)(2,1)S(1)}, bf16[6,16,3072]{2,1,0:T(8,128)(2,1)S(1)}, u32[]{:S(2)}, u32[]{:S(2)}) collective-permute-start(bf16[6,16,3072]{2,1,0:T(8,128)(2,1)S(1)} %get-tuple-element.43.refs_0_), channel_id=1, source_target_pairs={{0,16},{1,17},{2,18},{3,19},{4,20},{5,21},{6,22},{7,23},{8,24},{9,... | collective-permute-start | bytes 1769480 | tf_op jit(solution)/shard_map/ppermute | solution.py:51
  21.2 30.5 %collective-permute-start.2 = (bf16[6,16,3072]{2,1,0:T(8,128)(2,1)S(1)}, bf16[6,16,3072]{2,1,0:T(8,128)(2,1)S(1)}, u32[]{:S(2)}, u32[]{:S(2)}) collective-permute-start(bf16[6,16,3072]{2,1,0:T(8,128)(2,1)S(1)} %collective-permute-done.1.refs_2_), channel_id=1, source_target_pairs={{0,16},{1,17},{2,18},{3,19},{4,20},{5,21},{6,22},{7,23},{8,24},{9,... | collective-permute-start | bytes 1769480 | tf_op jit(solution)/shard_map/ppermute | solution.py:51
  35.0 16.7 %collective-permute-start.4 = (bf16[6,16,3072]{2,1,0:T(8,128)(2,1)S(1)}, bf16[6,16,3072]{2,1,0:T(8,128)(2,1)S(1)}, u32[]{:S(2)}, u32[]{:S(2)}) collective-permute-start(bf16[6,16,3072]{2,1,0:T(8,128)(2,1)S(1)} %collective-permute-done.3.refs_4_), channel_id=1, source_target_pairs={{0,16},{1,17},{2,18},{3,19},{4,20},{5,21},{6,22},{7,23},{8,24},{9,... | collective-permute-start | bytes 1769480 | tf_op jit(solution)/shard_map/ppermute | solution.py:51
  35.0 16.7 %collective-permute-start.6 = (bf16[6,16,3072]{2,1,0:T(8,128)(2,1)S(1)}, bf16[6,16,3072]{2,1,0:T(8,128)(2,1)S(1)}, u32[]{:S(2)}, u32[]{:S(2)}) collective-permute-start(bf16[6,16,3072]{2,1,0:T(8,128)(2,1)S(1)} %collective-permute-done.5.refs_6_), channel_id=1, source_target_pairs={{0,16},{1,17},{2,18},{3,19},{4,20},{5,21},{6,22},{7,23},{8,24},{9,... | collective-permute-start | bytes 1769480 | tf_op jit(solution)/shard_map/ppermute | solution.py:51
  46.4 5.2 %collective-permute-start.9 = (bf16[32,128]{1,0:T(8,128)(2,1)S(1)}, bf16[32,128]{1,0:T(8,128)(2,1)S(1)}, u32[]{:S(2)}, u32[]{:S(2)}) collective-permute-start(bf16[32,128]{1,0:T(8,128)(2,1)S(1)} %constant_dynamic-update-slice_fusion.refs_0_), channel_id=1, source_target_pairs={{0,64},{1,65},{2,66},{3,67},{4,68},{5,69},{6,70},{7,71},{8,72},{9,... | collective-permute-start | bytes 24584 | tf_op jit(solution)/shard_map/ppermute | solution.py:51
  56.2 13.4 %collective-permute-start.11 = (s16[392,1024]{1,0:T(8,128)(2,1)S(1)}, s16[392,1024]{1,0:T(8,128)(2,1)S(1)}, u32[]{:S(2)}, u32[]{:S(2)}) collective-permute-start(s16[392,1024]{1,0:T(8,128)(2,1)S(1)} %get-tuple-element.49), channel_id=1, source_target_pairs={{0,4},{1,5},{2,6},{3,7},{4,8},{5,9},{6,10},{7,11},{8,12},{9,13},{1... | collective-permute-start | bytes 2408456 | tf_op jit(solution)/shard_map/ppermute | solution.py:51
  57.7 13.6 %collective-permute-start.12 = (s16[392,1024]{1,0:T(8,128)(2,1)S(1)}, s16[392,1024]{1,0:T(8,128)(2,1)S(1)}, u32[]{:S(2)}, u32[]{:S(2)}) collective-permute-start(s16[392,1024]{1,0:T(8,128)(2,1)S(1)} %get-tuple-element.50), channel_id=1, source_target_pairs={{0,12},{1,13},{2,14},{3,15},{4,0},{5,1},{6,2},{7,3},{8,4},{9,5},{1... | collective-permute-start | bytes 2408456 | tf_op jit(solution)/shard_map/ppermute | solution.py:51
  61.1 13.6 %collective-permute-start.23 = (s16[1552,128]{1,0:T(8,128)(2,1)S(1)}, s16[1552,128]{1,0:T(8,128)(2,1)S(1)}, u32[]{:S(2)}, u32[]{:S(2)}) collective-permute-start(s16[1552,128]{1,0:T(8,128)(2,1)S(1)} %get-tuple-element.66), channel_id=1, source_target_pairs={{0,32},{1,33},{2,34},{3,35},{4,36},{5,37},{6,38},{7,39},{8,40},{9,... | collective-permute-start | bytes 1191944 | tf_op jit(solution)/shard_map/ppermute | solution.py:51
  61.1 14.1 %collective-permute-start.24 = (s16[1552,128]{1,0:T(8,128)(2,1)S(1)}, s16[1552,128]{1,0:T(8,128)(2,1)S(1)}, u32[]{:S(2)}, u32[]{:S(2)}) collective-permute-start(s16[1552,128]{1,0:T(8,128)(2,1)S(1)} %get-tuple-element.68), channel_id=1, source_target_pairs={{0,96},{1,97},{2,98},{3,99},{4,100},{5,101},{6,102},{7,103},{8,104... | collective-permute-start | bytes 1191944 | tf_op jit(solution)/shard_map/ppermute | solution.py:51
  66.0 10.2 %collective-permute-start.26 = (s16[1552,128]{1,0:T(8,128)(2,1)S(1)}, s16[1552,128]{1,0:T(8,128)(2,1)S(1)}, u32[]{:S(2)}, u32[]{:S(2)}) collective-permute-start(s16[1552,128]{1,0:T(8,128)(2,1)S(1)} %get-tuple-element.70), channel_id=1, source_target_pairs={{0,96},{1,97},{2,98},{3,99},{4,100},{5,101},{6,102},{7,103},{8,104... | collective-permute-start | bytes 1191944 | tf_op jit(solution)/shard_map/ppermute | solution.py:51
  69.6 9.8 %collective-permute-start.27 = (s16[1552,128]{1,0:T(8,128)(2,1)S(1)}, s16[1552,128]{1,0:T(8,128)(2,1)S(1)}, u32[]{:S(2)}, u32[]{:S(2)}) collective-permute-start(s16[1552,128]{1,0:T(8,128)(2,1)S(1)} %get-tuple-element.71), channel_id=1, source_target_pairs={{0,32},{1,33},{2,34},{3,35},{4,36},{5,37},{6,38},{7,39},{8,40},{9,... | collective-permute-start | bytes 1191944 | tf_op jit(solution)/shard_map/ppermute | solution.py:51
  71.3 27.7 %collective-permute-start.14 = (s16[392,1024]{1,0:T(8,128)(2,1)S(1)}, s16[392,1024]{1,0:T(8,128)(2,1)S(1)}, u32[]{:S(2)}, u32[]{:S(2)}) collective-permute-start(s16[392,1024]{1,0:T(8,128)(2,1)S(1)} %get-tuple-element.52), channel_id=1, source_target_pairs={{0,12},{1,13},{2,14},{3,15},{4,0},{5,1},{6,2},{7,3},{8,4},{9,5},{1... | collective-permute-start | bytes 2408456 | tf_op jit(solution)/shard_map/ppermute | solution.py:51
  74.7 24.4 %collective-permute-start.15 = (s16[392,1024]{1,0:T(8,128)(2,1)S(1)}, s16[392,1024]{1,0:T(8,128)(2,1)S(1)}, u32[]{:S(2)}, u32[]{:S(2)}) collective-permute-start(s16[392,1024]{1,0:T(8,128)(2,1)S(1)} %get-tuple-element.53), channel_id=1, source_target_pairs={{0,4},{1,5},{2,6},{3,7},{4,8},{5,9},{6,10},{7,11},{8,12},{9,13},{1... | collective-permute-start | bytes 2408456 | tf_op jit(solution)/shard_map/ppermute | solution.py:51
  75.3 23.8 %collective-permute-start.13 = (s16[392,1024]{1,0:T(8,128)(2,1)S(1)}, s16[392,1024]{1,0:T(8,128)(2,1)S(1)}, u32[]{:S(2)}, u32[]{:S(2)}) collective-permute-start(s16[392,1024]{1,0:T(8,128)(2,1)S(1)} %get-tuple-element.51), channel_id=1, source_target_pairs={{0,4},{1,5},{2,6},{3,7},{4,8},{5,9},{6,10},{7,11},{8,12},{9,13},{1... | collective-permute-start | bytes 2408456 | tf_op jit(solution)/shard_map/ppermute | solution.py:51
  76.1 22.9 %collective-permute-start.16 = (s16[392,1024]{1,0:T(8,128)(2,1)S(1)}, s16[392,1024]{1,0:T(8,128)(2,1)S(1)}, u32[]{:S(2)}, u32[]{:S(2)}) collective-permute-start(s16[392,1024]{1,0:T(8,128)(2,1)S(1)} %get-tuple-element.54), channel_id=1, source_target_pairs={{0,12},{1,13},{2,14},{3,15},{4,0},{5,1},{6,2},{7,3},{8,4},{9,5},{1... | collective-permute-start | bytes 2408456 | tf_op jit(solution)/shard_map/ppermute | solution.py:51
  79.4 9.6 %collective-permute-start.25 = (s16[1552,128]{1,0:T(8,128)(2,1)S(1)}, s16[1552,128]{1,0:T(8,128)(2,1)S(1)}, u32[]{:S(2)}, u32[]{:S(2)}) collective-permute-start(s16[1552,128]{1,0:T(8,128)(2,1)S(1)} %get-tuple-element.69), channel_id=1, source_target_pairs={{0,32},{1,33},{2,34},{3,35},{4,36},{5,37},{6,38},{7,39},{8,40},{9,... | collective-permute-start | bytes 1191944 | tf_op jit(solution)/shard_map/ppermute | solution.py:51
  89.0 7.8 %collective-permute-start.28 = (s16[1552,128]{1,0:T(8,128)(2,1)S(1)}, s16[1552,128]{1,0:T(8,128)(2,1)S(1)}, u32[]{:S(2)}, u32[]{:S(2)}) collective-permute-start(s16[1552,128]{1,0:T(8,128)(2,1)S(1)} %get-tuple-element.72), channel_id=1, source_target_pairs={{0,96},{1,97},{2,98},{3,99},{4,100},{5,101},{6,102},{7,103},{8,104... | collective-permute-start | bytes 1191944 | tf_op jit(solution)/shard_map/ppermute | solution.py:51
  97.4 8.1 %collective-permute-start.29 = (s16[200,512]{1,0:T(8,128)(2,1)S(1)}, s16[200,512]{1,0:T(8,128)(2,1)S(1)}, u32[]{:S(2)}, u32[]{:S(2)}) collective-permute-start(s16[200,512]{1,0:T(8,128)(2,1)S(1)} %get-tuple-element.74), channel_id=1, source_target_pairs={{0,1},{1,2},{2,3},{3,0},{4,5},{5,6},{6,7},{7,4},{8,9},{9,10},{10,1... | collective-permute-start | bytes 614408 | tf_op jit(solution)/shard_map/ppermute | solution.py:51
  100.4 19.6 %collective-permute-start.17 = (s16[200,1024]{1,0:T(8,128)(2,1)S(1)}, s16[200,1024]{1,0:T(8,128)(2,1)S(1)}, u32[]{:S(2)}, u32[]{:S(2)}) collective-permute-start(s16[200,1024]{1,0:T(8,128)(2,1)S(1)} %get-tuple-element.56), channel_id=1, source_target_pairs={{0,1},{1,2},{2,3},{3,0},{4,5},{5,6},{6,7},{7,4},{8,9},{9,10},{10,1... | collective-permute-start | bytes 1228808 | tf_op jit(solution)/shard_map/ppermute | solution.py:51
  101.9 18.1 %collective-permute-start.18 = (s16[200,1024]{1,0:T(8,128)(2,1)S(1)}, s16[200,1024]{1,0:T(8,128)(2,1)S(1)}, u32[]{:S(2)}, u32[]{:S(2)}) collective-permute-start(s16[200,1024]{1,0:T(8,128)(2,1)S(1)} %get-tuple-element.57), channel_id=1, source_target_pairs={{0,2},{1,3},{2,0},{3,1},{4,6},{5,7},{6,4},{7,5},{8,10},{9,11},{10,... | collective-permute-start | bytes 1228808 | tf_op jit(solution)/shard_map/ppermute | solution.py:51
  103.0 17.1 %collective-permute-start.19 = (s16[200,1024]{1,0:T(8,128)(2,1)S(1)}, s16[200,1024]{1,0:T(8,128)(2,1)S(1)}, u32[]{:S(2)}, u32[]{:S(2)}) collective-permute-start(s16[200,1024]{1,0:T(8,128)(2,1)S(1)} %get-tuple-element.58), channel_id=1, source_target_pairs={{0,3},{1,0},{2,1},{3,2},{4,7},{5,4},{6,5},{7,6},{8,11},{9,8},{10,9... | collective-permute-start | bytes 1228808 | tf_op jit(solution)/shard_map/ppermute | solution.py:51
  105.4 12.7 %collective-permute-start.30 = (s16[200,512]{1,0:T(8,128)(2,1)S(1)}, s16[200,512]{1,0:T(8,128)(2,1)S(1)}, u32[]{:S(2)}, u32[]{:S(2)}) collective-permute-start(s16[200,512]{1,0:T(8,128)(2,1)S(1)} %get-tuple-element.75), channel_id=1, source_target_pairs={{0,2},{1,3},{2,0},{3,1},{4,6},{5,7},{6,4},{7,5},{8,10},{9,11},{10,... | collective-permute-start | bytes 614408 | tf_op jit(solution)/shard_map/ppermute | solution.py:51
  105.5 14.2 %collective-permute-start.31 = (s16[200,512]{1,0:T(8,128)(2,1)S(1)}, s16[200,512]{1,0:T(8,128)(2,1)S(1)}, u32[]{:S(2)}, u32[]{:S(2)}) collective-permute-start(s16[200,512]{1,0:T(8,128)(2,1)S(1)} %get-tuple-element.76), channel_id=1, source_target_pairs={{0,3},{1,0},{2,1},{3,2},{4,7},{5,4},{6,5},{7,6},{8,11},{9,8},{10,9... | collective-permute-start | bytes 614408 | tf_op jit(solution)/shard_map/ppermute | solution.py:51
  120.0 9.9 %collective-permute-start.32 = (s16[200,128]{1,0:T(8,128)(2,1)S(1)}, s16[200,128]{1,0:T(8,128)(2,1)S(1)}, u32[]{:S(2)}, u32[]{:S(2)}) collective-permute-start(s16[200,128]{1,0:T(8,128)(2,1)S(1)} %get-tuple-element.78), channel_id=1, source_target_pairs={{0,4},{1,5},{2,6},{3,7},{4,8},{5,9},{6,10},{7,11},{8,12},{9,13},{1... | collective-permute-start | bytes 153608 | tf_op jit(solution)/shard_map/ppermute | solution.py:51
  120.6 16.0 %collective-permute-start.20 = (s16[200,256]{1,0:T(8,128)(2,1)S(1)}, s16[200,256]{1,0:T(8,128)(2,1)S(1)}, u32[]{:S(2)}, u32[]{:S(2)}) collective-permute-start(s16[200,256]{1,0:T(8,128)(2,1)S(1)} %get-tuple-element.60), channel_id=1, source_target_pairs={{0,32},{1,33},{2,34},{3,35},{4,36},{5,37},{6,38},{7,39},{8,40},{9,... | collective-permute-start | bytes 307208 | tf_op jit(solution)/shard_map/ppermute | solution.py:51
  121.8 14.8 %collective-permute-start.21 = (s16[200,256]{1,0:T(8,128)(2,1)S(1)}, s16[200,256]{1,0:T(8,128)(2,1)S(1)}, u32[]{:S(2)}, u32[]{:S(2)}) collective-permute-start(s16[200,256]{1,0:T(8,128)(2,1)S(1)} %get-tuple-element.61), channel_id=1, source_target_pairs={{0,64},{1,65},{2,66},{3,67},{4,68},{5,69},{6,70},{7,71},{8,72},{9,... | collective-permute-start | bytes 307208 | tf_op jit(solution)/shard_map/ppermute | solution.py:51
  127.9 8.6 %collective-permute-start.22 = (s16[200,256]{1,0:T(8,128)(2,1)S(1)}, s16[200,256]{1,0:T(8,128)(2,1)S(1)}, u32[]{:S(2)}, u32[]{:S(2)}) collective-permute-start(s16[200,256]{1,0:T(8,128)(2,1)S(1)} %get-tuple-element.62), channel_id=1, source_target_pairs={{0,96},{1,97},{2,98},{3,99},{4,100},{5,101},{6,102},{7,103},{8,104... | collective-permute-start | bytes 307208 | tf_op jit(solution)/shard_map/ppermute | solution.py:51
  129.8 5.6 %collective-permute-start.33 = (s16[200,128]{1,0:T(8,128)(2,1)S(1)}, s16[200,128]{1,0:T(8,128)(2,1)S(1)}, u32[]{:S(2)}, u32[]{:S(2)}) collective-permute-start(s16[200,128]{1,0:T(8,128)(2,1)S(1)} %get-tuple-element.79), channel_id=1, source_target_pairs={{0,8},{1,9},{2,10},{3,11},{4,12},{5,13},{6,14},{7,15},{8,0},{9,1},... | collective-permute-start | bytes 153608 | tf_op jit(solution)/shard_map/ppermute | solution.py:51
  129.8 6.7 %collective-permute-start.34 = (s16[200,128]{1,0:T(8,128)(2,1)S(1)}, s16[200,128]{1,0:T(8,128)(2,1)S(1)}, u32[]{:S(2)}, u32[]{:S(2)}) collective-permute-start(s16[200,128]{1,0:T(8,128)(2,1)S(1)} %get-tuple-element.80), channel_id=1, source_target_pairs={{0,12},{1,13},{2,14},{3,15},{4,0},{5,1},{6,2},{7,3},{8,4},{9,5},{1... | collective-permute-start | bytes 153608 | tf_op jit(solution)/shard_map/ppermute | solution.py:51
  (5 other events, 46.4 us)

commit v2 on v1

--- a/solution.py
+++ b/solution.py
@@ -80,21 +80,16 @@
     ]
     for copy in copies:
         copy.start()
+    group = outs[0].shape[0]
     for n in range(chunks):
         copies[n].wait()
-
-        def step(m, carry):
-            m = n * (lanes // block) + m
-            cut = pl.ds(pl.multiple_of(m * block, block), block)
+        for m in range(n * (lanes // block), (n + 1) * (lanes // block)):
+            cut = slice(m * block, (m + 1) * block)
             keep = survive[0, 0, m].astype(F32)
             turned[:, :, cut] = jnp.swapaxes(held[:, :, cut].astype(F32) * keep, 0, 1).astype(BF)
-            return carry
-
-        lax.fori_loop(0, lanes // block, step, 0, unroll=True)
-    group = outs[0].shape[0]
-    for k in range(RING):
-        first = lax.rem(at[0] + k, RING) * group
-        outs[k][...] = turned[pl.ds(first, group)]
+        cut = slice(n * lanes, (n + 1) * lanes)
+        for k in range(RING):
+            outs[k][:, :, cut] = turned[pl.ds(lax.rem(at[0] + k, RING) * group, group), :, cut]
 
 
 def screen(survive, half):
@@ -109,7 +104,7 @@
         scratch_shapes=[
             pltpu.VMEM(half.shape, BF),
             pltpu.VMEM((occ, aux, ao), BF),
-            pltpu.SemaphoreType.DMA((4,)),
+            pltpu.SemaphoreType.DMA((6,)),
         ],
         compiler_params=params(50),
         cost_estimate=cost(half.size, half.size * 4),
@@ -120,7 +115,7 @@
 def join_body(*refs):
     metrics, mixed = refs[:4], refs[4]
     at = position()
-    aux = mixed.shape[0]
+    aux = metrics[0].shape[1]
     part = aux // 8
     metric = jnp.concatenate([m[...] for m in metrics], axis=0)
     source = lax.broadcasted_iota(jnp.int32, (aux, aux), 0)
@@ -130,14 +125,17 @@
     core = jnp.where(slot % 2 == 0, at[1], 1 - at[1])
     wanted = (up * 2 + core) * part + n % part
     pick = jnp.where(source == wanted, 1.0, 0.0).astype(BF)
-    mixed[...] = jnp.dot(metric, pick, preferred_element_type=F32).astype(BF)
+    mixed[...] = jnp.zeros_like(mixed)
+    for n in range(2):
+        cut = slice(n * aux, (n + 1) * aux)
+        mixed[cut, cut] = jnp.dot(metric, pick, preferred_element_type=F32).astype(BF)
 
 
 def join(metrics):
     aux = metrics[0].shape[1]
     return pl.pallas_call(
         join_body,
-        out_shape=jax.ShapeDtypeStruct((aux, aux), BF),
+        out_shape=jax.ShapeDtypeStruct((2 * aux, 2 * aux), BF),
         in_specs=[whole()] * 4,
         out_specs=whole(),
         compiler_params=params(4),
@@ -152,7 +150,7 @@
     step = pl.program_id(0)
     ao = turned.shape[0]
     aux = mixed.shape[0]
-    screened = jnp.concatenate([p[0] for p in pieces], axis=0)
+    screened = jnp.concatenate([p[n] for n in range(2) for p in pieces], axis=0)
     fitted = jnp.dot(mixed[...], screened, preferred_element_type=F32).astype(BF)
     wide, narrow = bulk.shape[1] // RING, rest.shape[1] // RING
 
@@ -175,18 +173,18 @@
 
 def fit(pieces, mixed):
     group, part, ao = pieces[0].shape
-    aux = part * 8
-    piece = pl.BlockSpec((1, part, ao), lambda i: (i, 0, 0))
+    aux, steps = 2 * part * 8, group // 2
+    piece = pl.BlockSpec((2, part, ao), lambda i: (i, 0, 0))
     return pl.pallas_call(
         fit_body,
-        grid=(group,),
-        out_shape=[jax.ShapeDtypeStruct((group * aux, n), BF) for n in (ao // 3, ao // 6)]
-        + [jax.ShapeDtypeStruct((ao, group * aux), BF)],
+        grid=(steps,),
+        out_shape=[jax.ShapeDtypeStruct((steps * aux, n), BF) for n in (ao // 3, ao // 6)]
+        + [jax.ShapeDtypeStruct((ao, steps * aux), BF)],
         in_specs=[piece] * 8 + [whole()],
         out_specs=[pl.BlockSpec((aux, n), lambda i: (i, 0)) for n in (ao // 3, ao // 6)]
-        + [pl.BlockSpec((ao, group * aux), lambda i: (0, 0))],
+        + [pl.BlockSpec((ao, steps * aux), lambda i: (0, 0))],
         compiler_params=params(28),
-        cost_estimate=cost(2 * group * aux * aux * ao, group * aux * ao * 6),
+        cost_estimate=cost(2 * steps * aux * aux * ao, steps * aux * ao * 6),
         name="fit",
     )(*pieces, mixed)
 
@@ -456,7 +454,7 @@
 def shards(half, metric, survive):
     parts = screen(survive, half)
     here = [parts[0]] + [None] * 3
-    for k in (2, 1, 3):
+    for k in (1, 3, 2):
         here[k] = send(parts[k], along_z(k))
     pair = jnp.concatenate([metric, send(metric, other_core)], axis=0)
     metrics = [pair] + [None] * 3
@@ -464,7 +462,7 @@
         metrics[k] = send(pair, along_z(k))
     mixed = join(metrics)
     there = [None] * 4
-    for k in (0, 2, 1, 3):
+    for k in (0, 1, 3, 2):
         there[k] = send(here[k], other_core)
     bulk_rows, rest_rows, turned = fit([v for both in zip(here, there) for v in both], mixed)
 

time: 138 us -> 137 us (level)
  no operation moved by 1% of the time
where the time goes in v2:
time: 137 us
  waiting for transfers between devices  72.3 us (53%)
  starting transfers between devices  44.6 us (33%)
  Pallas kernels  19.4 us (14%)
    ppermute x35, waiting for transfers between devices, send(): return lax.ppermute(v, AXES, moves(shift))  72.3 us
    ppermute x35, starting transfers between devices, send(): return lax.ppermute(v, AXES, moves(shift))  44.6 us
    pallas_call x4, Pallas kernels, bulk_k(): pl.pallas_call(functools.partial(bulk_body, blocks), out_shape=[jax.Shape...  6.55 us
    pallas_call x1, Pallas kernels, screen(): pl.pallas_call(screen_body, out_shape=[out] * RING, in_specs=[scalars(),...  3.55 us
    pallas_call x2, Pallas kernels, rest_k(): pl.pallas_call(functools.partial(rest_body, steps, cut), out_shape=[jax.S...  3.17 us
  transfers between devices with their start and end apart: 35, of which 14 were waited for; matrix products, arithmetic and copies ran while one was open for 0% of the time, Pallas kernels for 8%

profile of v2, /device:TPU:8, one launch (start us, length us, event | category | flops | bytes accessed | tf_op | source)
XLA Modules:
  0.0 137.2 jit_solution(3599727849810942628)
XLA Ops:
  0.7 3.5 %screen.1 = (bf16[6,16,3072]{2,1,0:T(8,128)(2,1)S(1)}, bf16[6,16,3072]{2,1,0:T(8,128)(2,1)S(1)}, bf16[6,16,3072]{2,1,0:T(8,128)(2,1)S(1)}, bf16[6,16,3072]{2,1,0:T(8,128)(2,1)S(1)}) custom-call(s32[1,1,24]{2,1,0:T(1,128)S(1)} %copy-done.1, bf16[16,24,3072]{2,1,0:T(8,128)(2,1)} %half.1), custom_call_target="tpu_custom_call" | custom-call | flops 1179648 | bytes 4718592 | tf_op jit(solution)/shard_map/screen/pallas_call | solution.py:99
  4.2 2.0 %collective-permute-start.1 = (bf16[6,16,3072]{2,1,0:T(8,128)(2,1)S(1)}, bf16[6,16,3072]{2,1,0:T(8,128)(2,1)S(1)}, u32[]{:S(2)}, u32[]{:S(2)}) collective-permute-start(bf16[6,16,3072]{2,1,0:T(8,128)(2,1)S(1)} %get-tuple-element.44), channel_id=1, source_target_pairs={{0,32},{1,33},{2,34},{3,35},{4,36},{5,37},{6,38},{7,39},{8,40},{9,... | collective-permute-start | bytes 1769480 | tf_op jit(solution)/shard_map/ppermute | solution.py:51
  6.2 3.6 %collective-permute-start.3 = (bf16[6,16,3072]{2,1,0:T(8,128)(2,1)S(1)}, bf16[6,16,3072]{2,1,0:T(8,128)(2,1)S(1)}, u32[]{:S(2)}, u32[]{:S(2)}) collective-permute-start(bf16[6,16,3072]{2,1,0:T(8,128)(2,1)S(1)} %get-tuple-element.45), channel_id=1, source_target_pairs={{0,64},{1,65},{2,66},{3,67},{4,68},{5,69},{6,70},{7,71},{8,72},{9,... | collective-permute-start | bytes 1769480 | tf_op jit(solution)/shard_map/ppermute | solution.py:51
  10.8 10.9 %collective-permute-done.1.refs_2_ = bf16[6,16,3072]{2,1,0:T(8,128)(2,1)S(1)} collective-permute-done((bf16[6,16,3072]{2,1,0:T(8,128)(2,1)S(1)}, bf16[6,16,3072]{2,1,0:T(8,128)(2,1)S(1)}, u32[]{:S(2)}, u32[]{:S(2)}) %collective-permute-start.1) | collective-permute-done | bytes 589856 | tf_op jit(solution)/shard_map/ppermute | solution.py:51
  21.7 13.8 %collective-permute-done.3.refs_4_ = bf16[6,16,3072]{2,1,0:T(8,128)(2,1)S(1)} collective-permute-done((bf16[6,16,3072]{2,1,0:T(8,128)(2,1)S(1)}, bf16[6,16,3072]{2,1,0:T(8,128)(2,1)S(1)}, u32[]{:S(2)}, u32[]{:S(2)}) %collective-permute-start.3) | collective-permute-done | bytes 589856 | tf_op jit(solution)/shard_map/ppermute | solution.py:51
  36.1 2.2 %collective-permute-done.7 = bf16[16,128]{1,0:T(8,128)(2,1)S(1)} collective-permute-done((bf16[16,128]{1,0:T(8,128)(2,1)S(1)}, bf16[16,128]{1,0:T(8,128)(2,1)S(1)}, u32[]{:S(2)}, u32[]{:S(2)}) %collective-permute-start.7) | collective-permute-done | bytes 4128 | tf_op jit(solution)/shard_map/ppermute | solution.py:51
  39.6 2.3 %collective-permute-done.10.refs_3_ = bf16[32,128]{1,0:T(8,128)(2,1)S(1)} collective-permute-done((bf16[32,128]{1,0:T(8,128)(2,1)S(1)}, bf16[32,128]{1,0:T(8,128)(2,1)S(1)}, u32[]{:S(2)}, u32[]{:S(2)}) %collective-permute-start.10) | collective-permute-done | bytes 8224 | tf_op jit(solution)/shard_map/ppermute | solution.py:51
  42.4 4.5 %collective-permute-done.8.refs_1_ = bf16[32,128]{1,0:T(8,128)(2,1)S(1)} collective-permute-done((bf16[32,128]{1,0:T(8,128)(2,1)S(1)}, bf16[32,128]{1,0:T(8,128)(2,1)S(1)}, u32[]{:S(2)}, u32[]{:S(2)}) %collective-permute-start.8) | collective-permute-done | bytes 8224 | tf_op jit(solution)/shard_map/ppermute | solution.py:51
  47.3 4.7 %collective-permute-done.9.refs_2_ = bf16[32,128]{1,0:T(8,128)(2,1)S(1)} collective-permute-done((bf16[32,128]{1,0:T(8,128)(2,1)S(1)}, bf16[32,128]{1,0:T(8,128)(2,1)S(1)}, u32[]{:S(2)}, u32[]{:S(2)}) %collective-permute-start.9) | collective-permute-done | bytes 8224 | tf_op jit(solution)/shard_map/ppermute | solution.py:51
  52.2 2.0 %fit.1 = (bf16[768,1024]{1,0:T(8,128)(2,1)S(1)}, bf16[768,512]{1,0:T(8,128)(2,1)S(1)}, bf16[3072,768]{1,0:T(8,128)(2,1)S(1)}) custom-call(bf16[6,16,3072]{2,1,0:T(8,128)(2,1)S(1)} %get-tuple-element.43.refs_0_, bf16[6,16,3072]{2,1,0:T(8,128)(2,1)S(1)} %collective-permute-done.refs_1_, bf16[6,16,3072]{2,1,0:T(8,128)(2,1)S(1)} %collective-permute-done.1.refs_2_, ...), custom_call_target="tpu_custom_call" | custom-call | flops 1207959552 | bytes 14155776 | tf_op jit(solution)/shard_map/fit/pallas_call | solution.py:178
  54.2 1.7 %shard_map.38 = (s16[392,1024]{1,0:T(8,128)(2,1)S(1)}, s16[392,1024]{1,0:T(8,128)(2,1)S(1)}) custom-call(bf16[768,1024]{1,0:T(8,128)(2,1)S(1)} %get-tuple-element.47.bulk, bf16[3072,768]{1,0:T(8,128)(2,1)S(1)} %get-tuple-element.48.turned), custom_call_target="tpu_custom_call" | custom-call | flops 1207959552 | bytes 1572864 | tf_op jit(solution)/shard_map/pallas_call | solution.py:247
  57.5 1.7 %collective-permute-start.12 = (s16[392,1024]{1,0:T(8,128)(2,1)S(1)}, s16[392,1024]{1,0:T(8,128)(2,1)S(1)}, u32[]{:S(2)}, u32[]{:S(2)}) collective-permute-start(s16[392,1024]{1,0:T(8,128)(2,1)S(1)} %get-tuple-element.50), channel_id=1, source_target_pairs={{0,12},{1,13},{2,14},{3,15},{4,0},{5,1},{6,2},{7,3},{8,4},{9,5},{1... | collective-permute-start | bytes 2408456 | tf_op jit(solution)/shard_map/ppermute | solution.py:51
  59.3 1.6 %shard_map.41 = (s16[1552,128]{1,0:T(8,128)(2,1)S(1)}, s16[1552,128]{1,0:T(8,128)(2,1)S(1)}, f32[3072,128]{1,0:T(8,128)S(1)}) custom-call(bf16[768,512]{1,0:T(8,128)(2,1)S(1)} %get-tuple-element.63.rest, bf16[3072,768]{1,0:T(8,128)(2,1)S(1)} %get-tuple-element.48.turned), custom_call_target="tpu_custom_call" | custom-call | flops 1207959552 | bytes 1572864 | tf_op jit(solution)/shard_map/pallas_call | solution.py:282
  60.9 3.2 %collective-permute-start.24 = (s16[1552,128]{1,0:T(8,128)(2,1)S(1)}, s16[1552,128]{1,0:T(8,128)(2,1)S(1)}, u32[]{:S(2)}, u32[]{:S(2)}) collective-permute-start(s16[1552,128]{1,0:T(8,128)(2,1)S(1)} %get-tuple-element.68), channel_id=1, source_target_pairs={{0,96},{1,97},{2,98},{3,99},{4,100},{5,101},{6,102},{7,103},{8,104... | collective-permute-start | bytes 1191944 | tf_op jit(solution)/shard_map/ppermute | solution.py:51
  64.2 1.6 %shard_map.42 = (f32[1536,128]{1,0:T(8,128)S(1)}, s16[1552,128]{1,0:T(8,128)(2,1)S(1)}, s16[1552,128]{1,0:T(8,128)(2,1)S(1)}, f32[1536,128]{1,0:T(8,128)S(1)}) custom-call(bf16[768,512]{1,0:T(8,128)(2,1)S(1)} %get-tuple-element.63.rest, bf16[3072,768]{1,0:T(8,128)(2,1)S(1)} %get-tuple-element.48.turned), custom_call_target="tpu_custom_call" | custom-call | flops 1207959552 | bytes 1572864 | tf_op jit(solution)/shard_map/pallas_call | solution.py:282
  65.9 3.5 %collective-permute-done.11.refs_0_ = s16[392,1024]{1,0:T(8,128)(2,1)S(1)} collective-permute-done((s16[392,1024]{1,0:T(8,128)(2,1)S(1)}, s16[392,1024]{1,0:T(8,128)(2,1)S(1)}, u32[]{:S(2)}, u32[]{:S(2)}) %collective-permute-start.11) | collective-permute-done | bytes 802848 | tf_op jit(solution)/shard_map/ppermute | solution.py:51
  69.4 1.7 %shard_map.40 = (s16[392,1024]{1,0:T(8,128)(2,1)S(1)}, s16[392,1024]{1,0:T(8,128)(2,1)S(1)}) custom-call(bf16[768,1024]{1,0:T(8,128)(2,1)S(1)} %get-tuple-element.47.bulk, bf16[3072,768]{1,0:T(8,128)(2,1)S(1)} %get-tuple-element.48.turned), custom_call_target="tpu_custom_call" | custom-call | flops 1207959552 | bytes 1572864 | tf_op jit(solution)/shard_map/pallas_call | solution.py:247
  71.2 1.6 %collective-permute-start.14 = (s16[392,1024]{1,0:T(8,128)(2,1)S(1)}, s16[392,1024]{1,0:T(8,128)(2,1)S(1)}, u32[]{:S(2)}, u32[]{:S(2)}) collective-permute-start(s16[392,1024]{1,0:T(8,128)(2,1)S(1)} %get-tuple-element.52), channel_id=1, source_target_pairs={{0,12},{1,13},{2,14},{3,15},{4,0},{5,1},{6,2},{7,3},{8,4},{9,5},{1... | collective-permute-start | bytes 2408456 | tf_op jit(solution)/shard_map/ppermute | solution.py:51
  72.8 1.7 %shard_map.39 = (s16[392,1024]{1,0:T(8,128)(2,1)S(1)}, s16[392,1024]{1,0:T(8,128)(2,1)S(1)}) custom-call(bf16[768,1024]{1,0:T(8,128)(2,1)S(1)} %get-tuple-element.47.bulk, bf16[3072,768]{1,0:T(8,128)(2,1)S(1)} %get-tuple-element.48.turned, s16[392,1024]{1,0:T(8,128)(2,1)S(1)} %collective-permute-done.11.refs_0_, ...), custom_call_target="tpu_custom_call" | custom-call | flops 1207959552 | bytes 1572864 | tf_op jit(solution)/shard_map/pallas_call | solution.py:247
  76.0 2.8 %collective-permute-start.16 = (s16[392,1024]{1,0:T(8,128)(2,1)S(1)}, s16[392,1024]{1,0:T(8,128)(2,1)S(1)}, u32[]{:S(2)}, u32[]{:S(2)}) collective-permute-start(s16[392,1024]{1,0:T(8,128)(2,1)S(1)} %get-tuple-element.54), channel_id=1, source_target_pairs={{0,12},{1,13},{2,14},{3,15},{4,0},{5,1},{6,2},{7,3},{8,4},{9,5},{1... | collective-permute-start | bytes 2408456 | tf_op jit(solution)/shard_map/ppermute | solution.py:51
  79.5 9.2 %collective-permute-done.25.a = s16[1552,128]{1,0:T(8,128)(2,1)S(1)} collective-permute-done((s16[1552,128]{1,0:T(8,128)(2,1)S(1)}, s16[1552,128]{1,0:T(8,128)(2,1)S(1)}, u32[]{:S(2)}, u32[]{:S(2)}) %collective-permute-start.25) | collective-permute-done | bytes 397344 | tf_op jit(solution)/shard_map/ppermute | solution.py:51
  88.8 2.0 %collective-permute-start.28 = (s16[1552,128]{1,0:T(8,128)(2,1)S(1)}, s16[1552,128]{1,0:T(8,128)(2,1)S(1)}, u32[]{:S(2)}, u32[]{:S(2)}) collective-permute-start(s16[1552,128]{1,0:T(8,128)(2,1)S(1)} %get-tuple-element.72), channel_id=1, source_target_pairs={{0,96},{1,97},{2,98},{3,99},{4,100},{5,101},{6,102},{7,103},{8,104... | collective-permute-start | bytes 1191944 | tf_op jit(solution)/shard_map/ppermute | solution.py:51
  92.2 4.4 %collective-permute-done.28.e = s16[1552,128]{1,0:T(8,128)(2,1)S(1)} collective-permute-done((s16[1552,128]{1,0:T(8,128)(2,1)S(1)}, s16[1552,128]{1,0:T(8,128)(2,1)S(1)}, u32[]{:S(2)}, u32[]{:S(2)}) %collective-permute-start.28) | collective-permute-done | bytes 397344 | tf_op jit(solution)/shard_map/ppermute | solution.py:51
  97.2 1.6 %collective-permute-start.29 = (s16[200,512]{1,0:T(8,128)(2,1)S(1)}, s16[200,512]{1,0:T(8,128)(2,1)S(1)}, u32[]{:S(2)}, u32[]{:S(2)}) collective-permute-start(s16[200,512]{1,0:T(8,128)(2,1)S(1)} %get-tuple-element.74), channel_id=1, source_target_pairs={{0,1},{1,2},{2,3},{3,0},{4,5},{5,6},{6,7},{7,4},{8,9},{9,10},{10,1... | collective-permute-start | bytes 614408 | tf_op jit(solution)/shard_map/ppermute | solution.py:51
  102.8 2.4 %collective-permute-start.19 = (s16[200,1024]{1,0:T(8,128)(2,1)S(1)}, s16[200,1024]{1,0:T(8,128)(2,1)S(1)}, u32[]{:S(2)}, u32[]{:S(2)}) collective-permute-start(s16[200,1024]{1,0:T(8,128)(2,1)S(1)} %get-tuple-element.58), channel_id=1, source_target_pairs={{0,3},{1,0},{2,1},{3,2},{4,7},{5,4},{6,5},{7,6},{8,11},{9,8},{10,9... | collective-permute-start | bytes 1228808 | tf_op jit(solution)/shard_map/ppermute | solution.py:51
  105.3 1.6 %collective-permute-start.31 = (s16[200,512]{1,0:T(8,128)(2,1)S(1)}, s16[200,512]{1,0:T(8,128)(2,1)S(1)}, u32[]{:S(2)}, u32[]{:S(2)}) collective-permute-start(s16[200,512]{1,0:T(8,128)(2,1)S(1)} %get-tuple-element.76), channel_id=1, source_target_pairs={{0,3},{1,0},{2,1},{3,2},{4,7},{5,4},{6,5},{7,6},{8,11},{9,8},{10,9... | collective-permute-start | bytes 614408 | tf_op jit(solution)/shard_map/ppermute | solution.py:51
  106.9 11.0 %collective-permute-done.30.b = s16[200,512]{1,0:T(8,128)(2,1)S(1)} collective-permute-done((s16[200,512]{1,0:T(8,128)(2,1)S(1)}, s16[200,512]{1,0:T(8,128)(2,1)S(1)}, u32[]{:S(2)}, u32[]{:S(2)}) %collective-permute-start.30) | collective-permute-done | bytes 204832 | tf_op jit(solution)/shard_map/ppermute | solution.py:51
  117.9 1.6 %collective-permute-done.31.d = s16[200,512]{1,0:T(8,128)(2,1)S(1)} collective-permute-done((s16[200,512]{1,0:T(8,128)(2,1)S(1)}, s16[200,512]{1,0:T(8,128)(2,1)S(1)}, u32[]{:S(2)}, u32[]{:S(2)}) %collective-permute-start.31) | collective-permute-done | bytes 204832 | tf_op jit(solution)/shard_map/ppermute | solution.py:51
  121.6 6.2 %collective-permute-start.21 = (s16[200,256]{1,0:T(8,128)(2,1)S(1)}, s16[200,256]{1,0:T(8,128)(2,1)S(1)}, u32[]{:S(2)}, u32[]{:S(2)}) collective-permute-start(s16[200,256]{1,0:T(8,128)(2,1)S(1)} %get-tuple-element.61), channel_id=1, source_target_pairs={{0,64},{1,65},{2,66},{3,67},{4,68},{5,69},{6,70},{7,71},{8,72},{9,... | collective-permute-start | bytes 307208 | tf_op jit(solution)/shard_map/ppermute | solution.py:51
  127.7 1.9 %collective-permute-start.22 = (s16[200,256]{1,0:T(8,128)(2,1)S(1)}, s16[200,256]{1,0:T(8,128)(2,1)S(1)}, u32[]{:S(2)}, u32[]{:S(2)}) collective-permute-start(s16[200,256]{1,0:T(8,128)(2,1)S(1)} %get-tuple-element.62), channel_id=1, source_target_pairs={{0,96},{1,97},{2,98},{3,99},{4,100},{5,101},{6,102},{7,103},{8,104... | collective-permute-start | bytes 307208 | tf_op jit(solution)/shard_map/ppermute | solution.py:51
  129.7 3.2 %collective-permute-start.34 = (s16[200,128]{1,0:T(8,128)(2,1)S(1)}, s16[200,128]{1,0:T(8,128)(2,1)S(1)}, u32[]{:S(2)}, u32[]{:S(2)}) collective-permute-start(s16[200,128]{1,0:T(8,128)(2,1)S(1)} %get-tuple-element.80), channel_id=1, source_target_pairs={{0,12},{1,13},{2,14},{3,15},{4,0},{5,1},{6,2},{7,3},{8,4},{9,5},{1... | collective-permute-start | bytes 153608 | tf_op jit(solution)/shard_map/ppermute | solution.py:51
  132.9 2.4 %collective-permute-done.33.rb = s16[200,128]{1,0:T(8,128)(2,1)S(1)} collective-permute-done((s16[200,128]{1,0:T(8,128)(2,1)S(1)}, s16[200,128]{1,0:T(8,128)(2,1)S(1)}, u32[]{:S(2)}, u32[]{:S(2)}) %collective-permute-start.33) | collective-permute-done | bytes 51232 | tf_op jit(solution)/shard_map/ppermute | solution.py:51
  (62 shorter events, 18.6 us)
Async XLA Ops:
  4.2 17.4 %collective-permute-start.1 = (bf16[6,16,3072]{2,1,0:T(8,128)(2,1)S(1)}, bf16[6,16,3072]{2,1,0:T(8,128)(2,1)S(1)}, u32[]{:S(2)}, u32[]{:S(2)}) collective-permute-start(bf16[6,16,3072]{2,1,0:T(8,128)(2,1)S(1)} %get-tuple-element.44), channel_id=1, source_target_pairs={{0,32},{1,33},{2,34},{3,35},{4,36},{5,37},{6,38},{7,39},{8,40},{9,... | collective-permute-start | bytes 1769480 | tf_op jit(solution)/shard_map/ppermute | solution.py:51
  6.2 29.3 %collective-permute-start.3 = (bf16[6,16,3072]{2,1,0:T(8,128)(2,1)S(1)}, bf16[6,16,3072]{2,1,0:T(8,128)(2,1)S(1)}, u32[]{:S(2)}, u32[]{:S(2)}) collective-permute-start(bf16[6,16,3072]{2,1,0:T(8,128)(2,1)S(1)} %get-tuple-element.45), channel_id=1, source_target_pairs={{0,64},{1,65},{2,66},{3,67},{4,68},{5,69},{6,70},{7,71},{8,72},{9,... | collective-permute-start | bytes 1769480 | tf_op jit(solution)/shard_map/ppermute | solution.py:51
  9.8 25.7 %collective-permute-start.5 = (bf16[6,16,3072]{2,1,0:T(8,128)(2,1)S(1)}, bf16[6,16,3072]{2,1,0:T(8,128)(2,1)S(1)}, u32[]{:S(2)}, u32[]{:S(2)}) collective-permute-start(bf16[6,16,3072]{2,1,0:T(8,128)(2,1)S(1)} %get-tuple-element.46), channel_id=1, source_target_pairs={{0,96},{1,97},{2,98},{3,99},{4,100},{5,101},{6,102},{7,103},{8,104... | collective-permute-start | bytes 1769480 | tf_op jit(solution)/shard_map/ppermute | solution.py:51
  10.8 41.4 %collective-permute-start = (bf16[6,16,3072]{2,1,0:T(8,128)(2,1)S(1)}, bf16[6,16,3072]{2,1,0:T(8,128)(2,1)S(1)}, u32[]{:S(2)}, u32[]{:S(2)}) collective-permute-start(bf16[6,16,3072]{2,1,0:T(8,128)(2,1)S(1)} %get-tuple-element.43.refs_0_), channel_id=1, source_target_pairs={{0,16},{1,17},{2,18},{3,19},{4,20},{5,21},{6,22},{7,23},{8,24},{9,... | collective-permute-start | bytes 1769480 | tf_op jit(solution)/shard_map/ppermute | solution.py:51
  21.7 30.5 %collective-permute-start.2 = (bf16[6,16,3072]{2,1,0:T(8,128)(2,1)S(1)}, bf16[6,16,3072]{2,1,0:T(8,128)(2,1)S(1)}, u32[]{:S(2)}, u32[]{:S(2)}) collective-permute-start(bf16[6,16,3072]{2,1,0:T(8,128)(2,1)S(1)} %collective-permute-done.1.refs_2_), channel_id=1, source_target_pairs={{0,16},{1,17},{2,18},{3,19},{4,20},{5,21},{6,22},{7,23},{8,24},{9,... | collective-permute-start | bytes 1769480 | tf_op jit(solution)/shard_map/ppermute | solution.py:51
  35.5 16.7 %collective-permute-start.4 = (bf16[6,16,3072]{2,1,0:T(8,128)(2,1)S(1)}, bf16[6,16,3072]{2,1,0:T(8,128)(2,1)S(1)}, u32[]{:S(2)}, u32[]{:S(2)}) collective-permute-start(bf16[6,16,3072]{2,1,0:T(8,128)(2,1)S(1)} %collective-permute-done.3.refs_4_), channel_id=1, source_target_pairs={{0,16},{1,17},{2,18},{3,19},{4,20},{5,21},{6,22},{7,23},{8,24},{9,... | collective-permute-start | bytes 1769480 | tf_op jit(solution)/shard_map/ppermute | solution.py:51
  35.5 16.7 %collective-permute-start.6 = (bf16[6,16,3072]{2,1,0:T(8,128)(2,1)S(1)}, bf16[6,16,3072]{2,1,0:T(8,128)(2,1)S(1)}, u32[]{:S(2)}, u32[]{:S(2)}) collective-permute-start(bf16[6,16,3072]{2,1,0:T(8,128)(2,1)S(1)} %collective-permute-done.5.refs_6_), channel_id=1, source_target_pairs={{0,16},{1,17},{2,18},{3,19},{4,20},{5,21},{6,22},{7,23},{8,24},{9,... | collective-permute-start | bytes 1769480 | tf_op jit(solution)/shard_map/ppermute | solution.py:51
  46.8 5.2 %collective-permute-start.9 = (bf16[32,128]{1,0:T(8,128)(2,1)S(1)}, bf16[32,128]{1,0:T(8,128)(2,1)S(1)}, u32[]{:S(2)}, u32[]{:S(2)}) collective-permute-start(bf16[32,128]{1,0:T(8,128)(2,1)S(1)} %constant_dynamic-update-slice_fusion.refs_0_), channel_id=1, source_target_pairs={{0,64},{1,65},{2,66},{3,67},{4,68},{5,69},{6,70},{7,71},{8,72},{9,... | collective-permute-start | bytes 24584 | tf_op jit(solution)/shard_map/ppermute | solution.py:51
  56.0 13.4 %collective-permute-start.11 = (s16[392,1024]{1,0:T(8,128)(2,1)S(1)}, s16[392,1024]{1,0:T(8,128)(2,1)S(1)}, u32[]{:S(2)}, u32[]{:S(2)}) collective-permute-start(s16[392,1024]{1,0:T(8,128)(2,1)S(1)} %get-tuple-element.49), channel_id=1, source_target_pairs={{0,4},{1,5},{2,6},{3,7},{4,8},{5,9},{6,10},{7,11},{8,12},{9,13},{1... | collective-permute-start | bytes 2408456 | tf_op jit(solution)/shard_map/ppermute | solution.py:51
  57.5 13.6 %collective-permute-start.12 = (s16[392,1024]{1,0:T(8,128)(2,1)S(1)}, s16[392,1024]{1,0:T(8,128)(2,1)S(1)}, u32[]{:S(2)}, u32[]{:S(2)}) collective-permute-start(s16[392,1024]{1,0:T(8,128)(2,1)S(1)} %get-tuple-element.50), channel_id=1, source_target_pairs={{0,12},{1,13},{2,14},{3,15},{4,0},{5,1},{6,2},{7,3},{8,4},{9,5},{1... | collective-permute-start | bytes 2408456 | tf_op jit(solution)/shard_map/ppermute | solution.py:51
  60.9 13.6 %collective-permute-start.23 = (s16[1552,128]{1,0:T(8,128)(2,1)S(1)}, s16[1552,128]{1,0:T(8,128)(2,1)S(1)}, u32[]{:S(2)}, u32[]{:S(2)}) collective-permute-start(s16[1552,128]{1,0:T(8,128)(2,1)S(1)} %get-tuple-element.66), channel_id=1, source_target_pairs={{0,32},{1,33},{2,34},{3,35},{4,36},{5,37},{6,38},{7,39},{8,40},{9,... | collective-permute-start | bytes 1191944 | tf_op jit(solution)/shard_map/ppermute | solution.py:51
  60.9 14.1 %collective-permute-start.24 = (s16[1552,128]{1,0:T(8,128)(2,1)S(1)}, s16[1552,128]{1,0:T(8,128)(2,1)S(1)}, u32[]{:S(2)}, u32[]{:S(2)}) collective-permute-start(s16[1552,128]{1,0:T(8,128)(2,1)S(1)} %get-tuple-element.68), channel_id=1, source_target_pairs={{0,96},{1,97},{2,98},{3,99},{4,100},{5,101},{6,102},{7,103},{8,104... | collective-permute-start | bytes 1191944 | tf_op jit(solution)/shard_map/ppermute | solution.py:51
  65.8 10.2 %collective-permute-start.26 = (s16[1552,128]{1,0:T(8,128)(2,1)S(1)}, s16[1552,128]{1,0:T(8,128)(2,1)S(1)}, u32[]{:S(2)}, u32[]{:S(2)}) collective-permute-start(s16[1552,128]{1,0:T(8,128)(2,1)S(1)} %get-tuple-element.70), channel_id=1, source_target_pairs={{0,96},{1,97},{2,98},{3,99},{4,100},{5,101},{6,102},{7,103},{8,104... | collective-permute-start | bytes 1191944 | tf_op jit(solution)/shard_map/ppermute | solution.py:51
  69.4 9.8 %collective-permute-start.27 = (s16[1552,128]{1,0:T(8,128)(2,1)S(1)}, s16[1552,128]{1,0:T(8,128)(2,1)S(1)}, u32[]{:S(2)}, u32[]{:S(2)}) collective-permute-start(s16[1552,128]{1,0:T(8,128)(2,1)S(1)} %get-tuple-element.71), channel_id=1, source_target_pairs={{0,32},{1,33},{2,34},{3,35},{4,36},{5,37},{6,38},{7,39},{8,40},{9,... | collective-permute-start | bytes 1191944 | tf_op jit(solution)/shard_map/ppermute | solution.py:51
  71.2 27.7 %collective-permute-start.14 = (s16[392,1024]{1,0:T(8,128)(2,1)S(1)}, s16[392,1024]{1,0:T(8,128)(2,1)S(1)}, u32[]{:S(2)}, u32[]{:S(2)}) collective-permute-start(s16[392,1024]{1,0:T(8,128)(2,1)S(1)} %get-tuple-element.52), channel_id=1, source_target_pairs={{0,12},{1,13},{2,14},{3,15},{4,0},{5,1},{6,2},{7,3},{8,4},{9,5},{1... | collective-permute-start | bytes 2408456 | tf_op jit(solution)/shard_map/ppermute | solution.py:51
  74.5 24.4 %collective-permute-start.15 = (s16[392,1024]{1,0:T(8,128)(2,1)S(1)}, s16[392,1024]{1,0:T(8,128)(2,1)S(1)}, u32[]{:S(2)}, u32[]{:S(2)}) collective-permute-start(s16[392,1024]{1,0:T(8,128)(2,1)S(1)} %get-tuple-element.53), channel_id=1, source_target_pairs={{0,4},{1,5},{2,6},{3,7},{4,8},{5,9},{6,10},{7,11},{8,12},{9,13},{1... | collective-permute-start | bytes 2408456 | tf_op jit(solution)/shard_map/ppermute | solution.py:51
  75.1 23.8 %collective-permute-start.13 = (s16[392,1024]{1,0:T(8,128)(2,1)S(1)}, s16[392,1024]{1,0:T(8,128)(2,1)S(1)}, u32[]{:S(2)}, u32[]{:S(2)}) collective-permute-start(s16[392,1024]{1,0:T(8,128)(2,1)S(1)} %get-tuple-element.51), channel_id=1, source_target_pairs={{0,4},{1,5},{2,6},{3,7},{4,8},{5,9},{6,10},{7,11},{8,12},{9,13},{1... | collective-permute-start | bytes 2408456 | tf_op jit(solution)/shard_map/ppermute | solution.py:51
  76.0 22.9 %collective-permute-start.16 = (s16[392,1024]{1,0:T(8,128)(2,1)S(1)}, s16[392,1024]{1,0:T(8,128)(2,1)S(1)}, u32[]{:S(2)}, u32[]{:S(2)}) collective-permute-start(s16[392,1024]{1,0:T(8,128)(2,1)S(1)} %get-tuple-element.54), channel_id=1, source_target_pairs={{0,12},{1,13},{2,14},{3,15},{4,0},{5,1},{6,2},{7,3},{8,4},{9,5},{1... | collective-permute-start | bytes 2408456 | tf_op jit(solution)/shard_map/ppermute | solution.py:51
  79.2 9.6 %collective-permute-start.25 = (s16[1552,128]{1,0:T(8,128)(2,1)S(1)}, s16[1552,128]{1,0:T(8,128)(2,1)S(1)}, u32[]{:S(2)}, u32[]{:S(2)}) collective-permute-start(s16[1552,128]{1,0:T(8,128)(2,1)S(1)} %get-tuple-element.69), channel_id=1, source_target_pairs={{0,32},{1,33},{2,34},{3,35},{4,36},{5,37},{6,38},{7,39},{8,40},{9,... | collective-permute-start | bytes 1191944 | tf_op jit(solution)/shard_map/ppermute | solution.py:51
  88.8 7.8 %collective-permute-start.28 = (s16[1552,128]{1,0:T(8,128)(2,1)S(1)}, s16[1552,128]{1,0:T(8,128)(2,1)S(1)}, u32[]{:S(2)}, u32[]{:S(2)}) collective-permute-start(s16[1552,128]{1,0:T(8,128)(2,1)S(1)} %get-tuple-element.72), channel_id=1, source_target_pairs={{0,96},{1,97},{2,98},{3,99},{4,100},{5,101},{6,102},{7,103},{8,104... | collective-permute-start | bytes 1191944 | tf_op jit(solution)/shard_map/ppermute | solution.py:51
  97.2 8.1 %collective-permute-start.29 = (s16[200,512]{1,0:T(8,128)(2,1)S(1)}, s16[200,512]{1,0:T(8,128)(2,1)S(1)}, u32[]{:S(2)}, u32[]{:S(2)}) collective-permute-start(s16[200,512]{1,0:T(8,128)(2,1)S(1)} %get-tuple-element.74), channel_id=1, source_target_pairs={{0,1},{1,2},{2,3},{3,0},{4,5},{5,6},{6,7},{7,4},{8,9},{9,10},{10,1... | collective-permute-start | bytes 614408 | tf_op jit(solution)/shard_map/ppermute | solution.py:51
  100.2 19.6 %collective-permute-start.17 = (s16[200,1024]{1,0:T(8,128)(2,1)S(1)}, s16[200,1024]{1,0:T(8,128)(2,1)S(1)}, u32[]{:S(2)}, u32[]{:S(2)}) collective-permute-start(s16[200,1024]{1,0:T(8,128)(2,1)S(1)} %get-tuple-element.56), channel_id=1, source_target_pairs={{0,1},{1,2},{2,3},{3,0},{4,5},{5,6},{6,7},{7,4},{8,9},{9,10},{10,1... | collective-permute-start | bytes 1228808 | tf_op jit(solution)/shard_map/ppermute | solution.py:51
  101.8 18.1 %collective-permute-start.18 = (s16[200,1024]{1,0:T(8,128)(2,1)S(1)}, s16[200,1024]{1,0:T(8,128)(2,1)S(1)}, u32[]{:S(2)}, u32[]{:S(2)}) collective-permute-start(s16[200,1024]{1,0:T(8,128)(2,1)S(1)} %get-tuple-element.57), channel_id=1, source_target_pairs={{0,2},{1,3},{2,0},{3,1},{4,6},{5,7},{6,4},{7,5},{8,10},{9,11},{10,... | collective-permute-start | bytes 1228808 | tf_op jit(solution)/shard_map/ppermute | solution.py:51
  102.8 17.1 %collective-permute-start.19 = (s16[200,1024]{1,0:T(8,128)(2,1)S(1)}, s16[200,1024]{1,0:T(8,128)(2,1)S(1)}, u32[]{:S(2)}, u32[]{:S(2)}) collective-permute-start(s16[200,1024]{1,0:T(8,128)(2,1)S(1)} %get-tuple-element.58), channel_id=1, source_target_pairs={{0,3},{1,0},{2,1},{3,2},{4,7},{5,4},{6,5},{7,6},{8,11},{9,8},{10,9... | collective-permute-start | bytes 1228808 | tf_op jit(solution)/shard_map/ppermute | solution.py:51
  105.2 12.7 %collective-permute-start.30 = (s16[200,512]{1,0:T(8,128)(2,1)S(1)}, s16[200,512]{1,0:T(8,128)(2,1)S(1)}, u32[]{:S(2)}, u32[]{:S(2)}) collective-permute-start(s16[200,512]{1,0:T(8,128)(2,1)S(1)} %get-tuple-element.75), channel_id=1, source_target_pairs={{0,2},{1,3},{2,0},{3,1},{4,6},{5,7},{6,4},{7,5},{8,10},{9,11},{10,... | collective-permute-start | bytes 614408 | tf_op jit(solution)/shard_map/ppermute | solution.py:51
  105.3 14.2 %collective-permute-start.31 = (s16[200,512]{1,0:T(8,128)(2,1)S(1)}, s16[200,512]{1,0:T(8,128)(2,1)S(1)}, u32[]{:S(2)}, u32[]{:S(2)}) collective-permute-start(s16[200,512]{1,0:T(8,128)(2,1)S(1)} %get-tuple-element.76), channel_id=1, source_target_pairs={{0,3},{1,0},{2,1},{3,2},{4,7},{5,4},{6,5},{7,6},{8,11},{9,8},{10,9... | collective-permute-start | bytes 614408 | tf_op jit(solution)/shard_map/ppermute | solution.py:51
  119.8 9.9 %collective-permute-start.32 = (s16[200,128]{1,0:T(8,128)(2,1)S(1)}, s16[200,128]{1,0:T(8,128)(2,1)S(1)}, u32[]{:S(2)}, u32[]{:S(2)}) collective-permute-start(s16[200,128]{1,0:T(8,128)(2,1)S(1)} %get-tuple-element.78), channel_id=1, source_target_pairs={{0,4},{1,5},{2,6},{3,7},{4,8},{5,9},{6,10},{7,11},{8,12},{9,13},{1... | collective-permute-start | bytes 153608 | tf_op jit(solution)/shard_map/ppermute | solution.py:51
  120.4 16.0 %collective-permute-start.20 = (s16[200,256]{1,0:T(8,128)(2,1)S(1)}, s16[200,256]{1,0:T(8,128)(2,1)S(1)}, u32[]{:S(2)}, u32[]{:S(2)}) collective-permute-start(s16[200,256]{1,0:T(8,128)(2,1)S(1)} %get-tuple-element.60), channel_id=1, source_target_pairs={{0,32},{1,33},{2,34},{3,35},{4,36},{5,37},{6,38},{7,39},{8,40},{9,... | collective-permute-start | bytes 307208 | tf_op jit(solution)/shard_map/ppermute | solution.py:51
  121.6 14.8 %collective-permute-start.21 = (s16[200,256]{1,0:T(8,128)(2,1)S(1)}, s16[200,256]{1,0:T(8,128)(2,1)S(1)}, u32[]{:S(2)}, u32[]{:S(2)}) collective-permute-start(s16[200,256]{1,0:T(8,128)(2,1)S(1)} %get-tuple-element.61), channel_id=1, source_target_pairs={{0,64},{1,65},{2,66},{3,67},{4,68},{5,69},{6,70},{7,71},{8,72},{9,... | collective-permute-start | bytes 307208 | tf_op jit(solution)/shard_map/ppermute | solution.py:51
  127.7 8.6 %collective-permute-start.22 = (s16[200,256]{1,0:T(8,128)(2,1)S(1)}, s16[200,256]{1,0:T(8,128)(2,1)S(1)}, u32[]{:S(2)}, u32[]{:S(2)}) collective-permute-start(s16[200,256]{1,0:T(8,128)(2,1)S(1)} %get-tuple-element.62), channel_id=1, source_target_pairs={{0,96},{1,97},{2,98},{3,99},{4,100},{5,101},{6,102},{7,103},{8,104... | collective-permute-start | bytes 307208 | tf_op jit(solution)/shard_map/ppermute | solution.py:51
  129.7 5.6 %collective-permute-start.33 = (s16[200,128]{1,0:T(8,128)(2,1)S(1)}, s16[200,128]{1,0:T(8,128)(2,1)S(1)}, u32[]{:S(2)}, u32[]{:S(2)}) collective-permute-start(s16[200,128]{1,0:T(8,128)(2,1)S(1)} %get-tuple-element.79), channel_id=1, source_target_pairs={{0,8},{1,9},{2,10},{3,11},{4,12},{5,13},{6,14},{7,15},{8,0},{9,1},... | collective-permute-start | bytes 153608 | tf_op jit(solution)/shard_map/ppermute | solution.py:51
  129.7 6.7 %collective-permute-start.34 = (s16[200,128]{1,0:T(8,128)(2,1)S(1)}, s16[200,128]{1,0:T(8,128)(2,1)S(1)}, u32[]{:S(2)}, u32[]{:S(2)}) collective-permute-start(s16[200,128]{1,0:T(8,128)(2,1)S(1)} %get-tuple-element.80), channel_id=1, source_target_pairs={{0,12},{1,13},{2,14},{3,15},{4,0},{5,1},{6,2},{7,3},{8,4},{9,5},{1... | collective-permute-start | bytes 153608 | tf_op jit(solution)/shard_map/ppermute | solution.py:51
  (5 other events, 46.8 us)

commit v3 on v2

--- a/solution.py
+++ b/solution.py
@@ -104,7 +104,7 @@
         scratch_shapes=[
             pltpu.VMEM(half.shape, BF),
             pltpu.VMEM((occ, aux, ao), BF),
-            pltpu.SemaphoreType.DMA((6,)),
+            pltpu.SemaphoreType.DMA((4,)),
         ],
         compiler_params=params(50),
         cost_estimate=cost(half.size, half.size * 4),
@@ -145,7 +145,7 @@
 
 
 def fit_body(*refs):
-    pieces, mixed, (bulk, rest, turned) = refs[:8], refs[8], refs[9:]
+    pieces, mixed, (bulk, rest, turned, *far) = refs[:8], refs[8], refs[9:]
     at = position()
     step = pl.program_id(0)
     ao = turned.shape[0]
@@ -153,14 +153,15 @@
     screened = jnp.concatenate([p[n] for n in range(2) for p in pieces], axis=0)
     fitted = jnp.dot(mixed[...], screened, preferred_element_type=F32).astype(BF)
     wide, narrow = bulk.shape[1] // RING, rest.shape[1] // RING
+    rows = pl.ds(pl.multiple_of(step * aux, aux), aux)
 
     def chosen(column, lanes):
         first, second = column, column + wide + narrow
         return jnp.where(at[1] == 0, fitted[:, first:first + lanes], fitted[:, second:second + lanes])
 
     for n in range(RING):
-        bulk[:, n * wide:(n + 1) * wide] = chosen(n * (ao // RING), wide)
-        rest[:, n * narrow:(n + 1) * narrow] = chosen(n * (ao // RING) + wide, narrow)
+        bulk[rows, n * wide:(n + 1) * wide] = chosen(n * (ao // RING), wide)
+        rest[rows, n * narrow:(n + 1) * narrow] = chosen(n * (ao // RING) + wide, narrow)
     flipped = fitted.T
     cut = pl.ds(pl.multiple_of(step * aux, aux), aux)
     high = ao // (RING * RING)
@@ -170,21 +171,24 @@
             to = jnp.where(at[1] == 0, n, y * RING + x) * high
             turned[pl.ds(pl.multiple_of(to, 64), high), cut] = flipped[n * high:(n + 1) * high]
 
+    @pl.when(step == pl.num_programs(0) - 1)
+    def _():
+        bulk_body(FAR, bulk, turned, *far)
+
 
 def fit(pieces, mixed):
     group, part, ao = pieces[0].shape
     aux, steps = 2 * part * 8, group // 2
-    piece = pl.BlockSpec((2, part, ao), lambda i: (i, 0, 0))
+    shapes = [((steps * aux, ao // 3), BF), ((steps * aux, ao // 6), BF), ((ao, steps * aux), BF)]
+    shapes += [((ao // RING // 2 + TAIL, ao // 3), I16)] * 2
     return pl.pallas_call(
         fit_body,
         grid=(steps,),
-        out_shape=[jax.ShapeDtypeStruct((steps * aux, n), BF) for n in (ao // 3, ao // 6)]
-        + [jax.ShapeDtypeStruct((ao, steps * aux), BF)],
-        in_specs=[piece] * 8 + [whole()],
-        out_specs=[pl.BlockSpec((aux, n), lambda i: (i, 0)) for n in (ao // 3, ao // 6)]
-        + [pl.BlockSpec((ao, steps * aux), lambda i: (0, 0))],
-        compiler_params=params(28),
-        cost_estimate=cost(2 * steps * aux * aux * ao, steps * aux * ao * 6),
+        out_shape=[jax.ShapeDtypeStruct(*shape) for shape in shapes],
+        in_specs=[pl.BlockSpec((2, part, ao), lambda i: (i, 0, 0))] * 8 + [whole()],
+        out_specs=[pl.BlockSpec(shape, lambda i: (0, 0)) for shape, _ in shapes],
+        compiler_params=params(36),
+        cost_estimate=cost(2 * steps * aux * aux * ao + steps * aux * ao * ao // 6, steps * aux * ao * 6),
         name="fit",
     )(*pieces, mixed)
 
@@ -218,6 +222,9 @@
         tail = end if tail is None else tail
         out[first:end, :] = coded(block, e)
         out[tail:tail + TAIL, :] = marked(e)
+
+
+FAR = ((2, 0, False), (2, 1, False))
 
 
 def bulk_body(blocks, bulk, turned, *refs):
@@ -350,15 +357,14 @@
     )(own, *upper, *lower, after))
 
 
-def bulk_second_body(own, a, b, d, e, after, kept, *outs):
-    at = position()
-    high = kept.shape[0]
+def bulk_second_body(steps, own, a, b, d, e, after, *outs):
+    at = position()
+    high = own.shape[0] // RING
     h = jnp.where(at[1] == 0, at[3], at[2])
     half = own.shape[0] // 2
     step = 256
-    for k in range(RING):
+    for k, out in zip(steps, outs):
         block = lax.rem(h + k, RING)
-        out = kept if k == 0 else outs[k - 1]
 
         def part(upper, arrived, block=block, out=out):
             @pl.when((block < RING // 2) == upper)
@@ -376,17 +382,19 @@
         part(False, (d, e))
 
 
-def bulk_second(own, upper, lower, after):
+def bulk_second(steps, own, upper, lower, after):
     total, columns = own.shape
     high = total // RING
     return list(pl.pallas_call(
-        bulk_second_body,
-        out_shape=[jax.ShapeDtypeStruct((high, columns), F32)]
-        + [jax.ShapeDtypeStruct((high + TAIL, columns), I16)] * 3,
+        functools.partial(bulk_second_body, steps),
+        out_shape=[
+            jax.ShapeDtypeStruct((high + TAIL, columns), I16) if k else jax.ShapeDtypeStruct((high, columns), F32)
+            for k in steps
+        ],
         in_specs=[whole()] * 6,
-        out_specs=[whole()] * 4,
+        out_specs=[whole()] * len(steps),
         compiler_params=params(24),
-        cost_estimate=cost(total * columns * 12, total * columns * 8),
+        cost_estimate=cost(high * columns * 12 * len(steps), high * columns * 8 * len(steps)),
         name="bulk_second_sum",
     )(own, *upper, *lower, after))
 
@@ -454,7 +462,7 @@
 def shards(half, metric, survive):
     parts = screen(survive, half)
     here = [parts[0]] + [None] * 3
-    for k in (1, 3, 2):
+    for k in (2, 1, 3):
         here[k] = send(parts[k], along_z(k))
     pair = jnp.concatenate([metric, send(metric, other_core)], axis=0)
     metrics = [pair] + [None] * 3
@@ -462,9 +470,9 @@
         metrics[k] = send(pair, along_z(k))
     mixed = join(metrics)
     there = [None] * 4
-    for k in (0, 1, 3, 2):
+    for k in (0, 2, 1, 3):
         there[k] = send(here[k], other_core)
-    bulk_rows, rest_rows, turned = fit([v for both in zip(here, there) for v in both], mixed)
+    bulk_rows, rest_rows, turned, *far = fit([v for both in zip(here, there) for v in both], mixed)
 
     def bulk_step(*blocks, arrived=()):
         return bulk_k(bulk_rows, turned, blocks, arrived)
@@ -481,7 +489,7 @@
         for k in (1, 2, 3):
             parts[k] = send(parts[k], shift(k))
 
-    far = near(first_axis, *bulk_step((2, 0, False), (2, 1, False)))
+    far = near(first_axis, *far)
     upper, lower, rest_own = rest_step((2, 0), ((0, 1), (2, 2)), ("message", "message", "all"))
     rest_far = near(along_z, upper, lower)
     lower_up, upper_down = near(first_axis, *bulk_step((1, 1, False), (3, 0, False)))
@@ -491,7 +499,10 @@
     up, down = rest_mid(keep_up, rest_far[0], keep_down, rest_far[1])
     mid = near(along_z, up, down)
     own = bulk_step((0, None, False))[0]
-    bulk = bulk_second(own, (upper_up, upper_down), (lower_up, lower_down), metric)
+    arrived = own, (upper_up, upper_down), (lower_up, lower_down), metric
+    bulk = [None] * 4
+    (bulk[2],) = bulk_second((2,), *arrived)
+    bulk[0], bulk[1], bulk[3] = bulk_second((0, 1, 3), *arrived)
     onward(bulk, second_axis)
     then = tick(metric)
     rest = rest_second(rest_own, (mid[0], rest_near[1]), (rest_near[0], mid[1]), then)

time: 137 us -> 140 us (1.022)
  the two profiles are of different devices: /device:TPU:8 before, /device:TPU:0 now
where the time goes in v3:
time: 140 us
  waiting for transfers between devices  75.3 us (54%)
  starting transfers between devices  44.2 us (32%)
  Pallas kernels  19.4 us (14%)
    ppermute x35, waiting for transfers between devices, send(): return lax.ppermute(v, AXES, moves(shift))  75.3 us
    ppermute x35, starting transfers between devices, send(): return lax.ppermute(v, AXES, moves(shift))  44.2 us
    pallas_call x3, Pallas kernels, bulk_k(): pl.pallas_call(functools.partial(bulk_body, blocks), out_shape=[jax.Shape...  4.84 us
    pallas_call x1, Pallas kernels, fit(): pl.pallas_call(fit_body, grid=(steps,), out_shape=[jax.ShapeDtypeStruct(*...  3.76 us
    pallas_call x1, Pallas kernels, screen(): pl.pallas_call(screen_body, out_shape=[out] * RING, in_specs=[scalars(),...  3.54 us
    pallas_call x2, Pallas kernels, rest_k(): pl.pallas_call(functools.partial(rest_body, steps, cut), out_shape=[jax.S...  3.18 us
  transfers between devices with their start and end apart: 35, of which 15 were waited for; matrix products, arithmetic and copies ran while one was open for 0% of the time, Pallas kernels for 8%

profile of v3, /device:TPU:0, one launch (start us, length us, event | category | flops | bytes accessed | tf_op | source)
XLA Modules:
  0.0 139.8 jit_solution(8001633423596016314)
XLA Ops:
  0.7 3.5 %screen.1 = (bf16[6,16,3072]{2,1,0:T(8,128)(2,1)S(1)}, bf16[6,16,3072]{2,1,0:T(8,128)(2,1)S(1)}, bf16[6,16,3072]{2,1,0:T(8,128)(2,1)S(1)}, bf16[6,16,3072]{2,1,0:T(8,128)(2,1)S(1)}) custom-call(s32[1,1,24]{2,1,0:T(1,128)S(1)} %copy-done.1, bf16[16,24,3072]{2,1,0:T(8,128)(2,1)} %half.1), custom_call_target="tpu_custom_call" | custom-call | flops 1179648 | bytes 4718592 | tf_op jit(solution)/shard_map/screen/pallas_call | solution.py:99
  4.2 2.1 %collective-permute-start.1 = (bf16[6,16,3072]{2,1,0:T(8,128)(2,1)S(1)}, bf16[6,16,3072]{2,1,0:T(8,128)(2,1)S(1)}, u32[]{:S(2)}, u32[]{:S(2)}) collective-permute-start(bf16[6,16,3072]{2,1,0:T(8,128)(2,1)S(1)} %get-tuple-element.43), channel_id=1, source_target_pairs={{0,32},{1,33},{2,34},{3,35},{4,36},{5,37},{6,38},{7,39},{8,40},{9,... | collective-permute-start | bytes 1769480 | tf_op jit(solution)/shard_map/ppermute | solution.py:51
  6.3 3.6 %collective-permute-start.3 = (bf16[6,16,3072]{2,1,0:T(8,128)(2,1)S(1)}, bf16[6,16,3072]{2,1,0:T(8,128)(2,1)S(1)}, u32[]{:S(2)}, u32[]{:S(2)}) collective-permute-start(bf16[6,16,3072]{2,1,0:T(8,128)(2,1)S(1)} %get-tuple-element.44), channel_id=1, source_target_pairs={{0,64},{1,65},{2,66},{3,67},{4,68},{5,69},{6,70},{7,71},{8,72},{9,... | collective-permute-start | bytes 1769480 | tf_op jit(solution)/shard_map/ppermute | solution.py:51
  10.9 10.9 %collective-permute-done.1.refs_2_ = bf16[6,16,3072]{2,1,0:T(8,128)(2,1)S(1)} collective-permute-done((bf16[6,16,3072]{2,1,0:T(8,128)(2,1)S(1)}, bf16[6,16,3072]{2,1,0:T(8,128)(2,1)S(1)}, u32[]{:S(2)}, u32[]{:S(2)}) %collective-permute-start.1) | collective-permute-done | bytes 589856 | tf_op jit(solution)/shard_map/ppermute | solution.py:51
  21.8 13.8 %collective-permute-done.3.refs_4_ = bf16[6,16,3072]{2,1,0:T(8,128)(2,1)S(1)} collective-permute-done((bf16[6,16,3072]{2,1,0:T(8,128)(2,1)S(1)}, bf16[6,16,3072]{2,1,0:T(8,128)(2,1)S(1)}, u32[]{:S(2)}, u32[]{:S(2)}) %collective-permute-start.3) | collective-permute-done | bytes 589856 | tf_op jit(solution)/shard_map/ppermute | solution.py:51
  36.2 2.2 %collective-permute-done.7 = bf16[16,128]{1,0:T(8,128)(2,1)S(1)} collective-permute-done((bf16[16,128]{1,0:T(8,128)(2,1)S(1)}, bf16[16,128]{1,0:T(8,128)(2,1)S(1)}, u32[]{:S(2)}, u32[]{:S(2)}) %collective-permute-start.7) | collective-permute-done | bytes 4128 | tf_op jit(solution)/shard_map/ppermute | solution.py:51
  39.8 2.3 %collective-permute-done.10.refs_3_ = bf16[32,128]{1,0:T(8,128)(2,1)S(1)} collective-permute-done((bf16[32,128]{1,0:T(8,128)(2,1)S(1)}, bf16[32,128]{1,0:T(8,128)(2,1)S(1)}, u32[]{:S(2)}, u32[]{:S(2)}) %collective-permute-start.10) | collective-permute-done | bytes 8224 | tf_op jit(solution)/shard_map/ppermute | solution.py:51
  42.5 4.5 %collective-permute-done.8.refs_1_ = bf16[32,128]{1,0:T(8,128)(2,1)S(1)} collective-permute-done((bf16[32,128]{1,0:T(8,128)(2,1)S(1)}, bf16[32,128]{1,0:T(8,128)(2,1)S(1)}, u32[]{:S(2)}, u32[]{:S(2)}) %collective-permute-start.8) | collective-permute-done | bytes 8224 | tf_op jit(solution)/shard_map/ppermute | solution.py:51
  47.4 4.7 %collective-permute-done.9.refs_2_ = bf16[32,128]{1,0:T(8,128)(2,1)S(1)} collective-permute-done((bf16[32,128]{1,0:T(8,128)(2,1)S(1)}, bf16[32,128]{1,0:T(8,128)(2,1)S(1)}, u32[]{:S(2)}, u32[]{:S(2)}) %collective-permute-start.9) | collective-permute-done | bytes 8224 | tf_op jit(solution)/shard_map/ppermute | solution.py:51
  52.3 3.8 %fit.1 = (bf16[768,1024]{1,0:T(8,128)(2,1)S(1)}, bf16[768,512]{1,0:T(8,128)(2,1)S(1)}, bf16[3072,768]{1,0:T(8,128)(2,1)S(1)}, s16[392,1024]{1,0:T(8,128)(2,1)S(1)}, s16[392,1024]{1,0:T(8,128)(2,1)S(1)}) custom-call(bf16[6,16,3072]{2,1,0:T(8,128)(2,1)S(1)} %get-tuple-element.42.refs_0_, bf16[6,16,3072]{2,1,0:T(8,128)(2,1)S(1)} %collective-permute-done.refs_1_, ...), custom_call_target="tpu_custom_call" | custom-call | flops 2415919104 | bytes 14155776 | tf_op jit(solution)/shard_map/fit/pallas_call | solution.py:184
  57.6 1.7 %collective-permute-start.12 = (s16[392,1024]{1,0:T(8,128)(2,1)S(1)}, s16[392,1024]{1,0:T(8,128)(2,1)S(1)}, u32[]{:S(2)}, u32[]{:S(2)}) collective-permute-start(s16[392,1024]{1,0:T(8,128)(2,1)S(1)} %get-tuple-element.49), channel_id=1, source_target_pairs={{0,12},{1,13},{2,14},{3,15},{4,0},{5,1},{6,2},{7,3},{8,4},{9,5},{1... | collective-permute-start | bytes 2408456 | tf_op jit(solution)/shard_map/ppermute | solution.py:51
  61.1 3.2 %collective-permute-start.24 = (s16[1552,128]{1,0:T(8,128)(2,1)S(1)}, s16[1552,128]{1,0:T(8,128)(2,1)S(1)}, u32[]{:S(2)}, u32[]{:S(2)}) collective-permute-start(s16[1552,128]{1,0:T(8,128)(2,1)S(1)} %get-tuple-element.66), channel_id=1, source_target_pairs={{0,96},{1,97},{2,98},{3,99},{4,100},{5,101},{6,102},{7,103},{8,104... | collective-permute-start | bytes 1191944 | tf_op jit(solution)/shard_map/ppermute | solution.py:51
  64.3 1.6 %shard_map.41 = (f32[1536,128]{1,0:T(8,128)S(1)}, s16[1552,128]{1,0:T(8,128)(2,1)S(1)}, s16[1552,128]{1,0:T(8,128)(2,1)S(1)}, f32[1536,128]{1,0:T(8,128)S(1)}) custom-call(bf16[768,512]{1,0:T(8,128)(2,1)S(1)} %get-tuple-element.61.rest, bf16[3072,768]{1,0:T(8,128)(2,1)S(1)} %get-tuple-element.47.turned), custom_call_target="tpu_custom_call" | custom-call | flops 1207959552 | bytes 1572864 | tf_op jit(solution)/shard_map/pallas_call | solution.py:289
  66.1 3.5 %collective-permute-done.11.refs_0_ = s16[392,1024]{1,0:T(8,128)(2,1)S(1)} collective-permute-done((s16[392,1024]{1,0:T(8,128)(2,1)S(1)}, s16[392,1024]{1,0:T(8,128)(2,1)S(1)}, u32[]{:S(2)}, u32[]{:S(2)}) %collective-permute-start.11) | collective-permute-done | bytes 802848 | tf_op jit(solution)/shard_map/ppermute | solution.py:51
  69.5 1.7 %shard_map.39 = (s16[392,1024]{1,0:T(8,128)(2,1)S(1)}, s16[392,1024]{1,0:T(8,128)(2,1)S(1)}) custom-call(bf16[768,1024]{1,0:T(8,128)(2,1)S(1)} %get-tuple-element.46.bulk, bf16[3072,768]{1,0:T(8,128)(2,1)S(1)} %get-tuple-element.47.turned), custom_call_target="tpu_custom_call" | custom-call | flops 1207959552 | bytes 1572864 | tf_op jit(solution)/shard_map/pallas_call | solution.py:254
  71.3 1.6 %collective-permute-start.14 = (s16[392,1024]{1,0:T(8,128)(2,1)S(1)}, s16[392,1024]{1,0:T(8,128)(2,1)S(1)}, u32[]{:S(2)}, u32[]{:S(2)}) collective-permute-start(s16[392,1024]{1,0:T(8,128)(2,1)S(1)} %get-tuple-element.51), channel_id=1, source_target_pairs={{0,12},{1,13},{2,14},{3,15},{4,0},{5,1},{6,2},{7,3},{8,4},{9,5},{1... | collective-permute-start | bytes 2408456 | tf_op jit(solution)/shard_map/ppermute | solution.py:51
  72.9 1.7 %shard_map.38 = (s16[392,1024]{1,0:T(8,128)(2,1)S(1)}, s16[392,1024]{1,0:T(8,128)(2,1)S(1)}) custom-call(bf16[768,1024]{1,0:T(8,128)(2,1)S(1)} %get-tuple-element.46.bulk, bf16[3072,768]{1,0:T(8,128)(2,1)S(1)} %get-tuple-element.47.turned, s16[392,1024]{1,0:T(8,128)(2,1)S(1)} %collective-permute-done.11.refs_0_, ...), custom_call_target="tpu_custom_call" | custom-call | flops 1207959552 | bytes 1572864 | tf_op jit(solution)/shard_map/pallas_call | solution.py:254
  75.5 1.9 %collective-permute-done.26.b = s16[1552,128]{1,0:T(8,128)(2,1)S(1)} collective-permute-done((s16[1552,128]{1,0:T(8,128)(2,1)S(1)}, s16[1552,128]{1,0:T(8,128)(2,1)S(1)}, u32[]{:S(2)}, u32[]{:S(2)}) %collective-permute-start.26) | collective-permute-done | bytes 397344 | tf_op jit(solution)/shard_map/ppermute | solution.py:51
  77.4 2.8 %collective-permute-start.16 = (s16[392,1024]{1,0:T(8,128)(2,1)S(1)}, s16[392,1024]{1,0:T(8,128)(2,1)S(1)}, u32[]{:S(2)}, u32[]{:S(2)}) collective-permute-start(s16[392,1024]{1,0:T(8,128)(2,1)S(1)} %get-tuple-element.53), channel_id=1, source_target_pairs={{0,12},{1,13},{2,14},{3,15},{4,0},{5,1},{6,2},{7,3},{8,4},{9,5},{1... | collective-permute-start | bytes 2408456 | tf_op jit(solution)/shard_map/ppermute | solution.py:51
  81.0 9.2 %collective-permute-done.25.a = s16[1552,128]{1,0:T(8,128)(2,1)S(1)} collective-permute-done((s16[1552,128]{1,0:T(8,128)(2,1)S(1)}, s16[1552,128]{1,0:T(8,128)(2,1)S(1)}, u32[]{:S(2)}, u32[]{:S(2)}) %collective-permute-start.25) | collective-permute-done | bytes 397344 | tf_op jit(solution)/shard_map/ppermute | solution.py:51
  90.2 2.0 %collective-permute-start.28 = (s16[1552,128]{1,0:T(8,128)(2,1)S(1)}, s16[1552,128]{1,0:T(8,128)(2,1)S(1)}, u32[]{:S(2)}, u32[]{:S(2)}) collective-permute-start(s16[1552,128]{1,0:T(8,128)(2,1)S(1)} %get-tuple-element.70), channel_id=1, source_target_pairs={{0,96},{1,97},{2,98},{3,99},{4,100},{5,101},{6,102},{7,103},{8,104... | collective-permute-start | bytes 1191944 | tf_op jit(solution)/shard_map/ppermute | solution.py:51
  93.6 4.4 %collective-permute-done.28.e = s16[1552,128]{1,0:T(8,128)(2,1)S(1)} collective-permute-done((s16[1552,128]{1,0:T(8,128)(2,1)S(1)}, s16[1552,128]{1,0:T(8,128)(2,1)S(1)}, u32[]{:S(2)}, u32[]{:S(2)}) %collective-permute-start.28) | collective-permute-done | bytes 397344 | tf_op jit(solution)/shard_map/ppermute | solution.py:51
  99.0 4.2 %collective-permute-done.13.a = s16[392,1024]{1,0:T(8,128)(2,1)S(1)} collective-permute-done((s16[392,1024]{1,0:T(8,128)(2,1)S(1)}, s16[392,1024]{1,0:T(8,128)(2,1)S(1)}, u32[]{:S(2)}, u32[]{:S(2)}) %collective-permute-start.13) | collective-permute-done | bytes 802848 | tf_op jit(solution)/shard_map/ppermute | solution.py:51
  103.5 3.4 %collective-permute-start.18 = (s16[200,1024]{1,0:T(8,128)(2,1)S(1)}, s16[200,1024]{1,0:T(8,128)(2,1)S(1)}, u32[]{:S(2)}, u32[]{:S(2)}) collective-permute-start(s16[200,1024]{1,0:T(8,128)(2,1)S(1)} %bulk_second_sum.3), channel_id=1, source_target_pairs={{0,2},{1,3},{2,0},{3,1},{4,6},{5,7},{6,4},{7,5},{8,10},{9,11},{10,... | collective-permute-start | bytes 1228808 | tf_op jit(solution)/shard_map/ppermute | solution.py:51
  108.7 2.6 %collective-permute-start.19 = (s16[200,1024]{1,0:T(8,128)(2,1)S(1)}, s16[200,1024]{1,0:T(8,128)(2,1)S(1)}, u32[]{:S(2)}, u32[]{:S(2)}) collective-permute-start(s16[200,1024]{1,0:T(8,128)(2,1)S(1)} %get-tuple-element.56), channel_id=1, source_target_pairs={{0,3},{1,0},{2,1},{3,2},{4,7},{5,4},{6,5},{7,6},{8,11},{9,8},{10,9... | collective-permute-start | bytes 1228808 | tf_op jit(solution)/shard_map/ppermute | solution.py:51
  111.2 2.1 %collective-permute-start.31 = (s16[200,512]{1,0:T(8,128)(2,1)S(1)}, s16[200,512]{1,0:T(8,128)(2,1)S(1)}, u32[]{:S(2)}, u32[]{:S(2)}) collective-permute-start(s16[200,512]{1,0:T(8,128)(2,1)S(1)} %get-tuple-element.74), channel_id=1, source_target_pairs={{0,3},{1,0},{2,1},{3,2},{4,7},{5,4},{6,5},{7,6},{8,11},{9,8},{10,9... | collective-permute-start | bytes 614408 | tf_op jit(solution)/shard_map/ppermute | solution.py:51
  113.4 7.3 %collective-permute-done.30.b = s16[200,512]{1,0:T(8,128)(2,1)S(1)} collective-permute-done((s16[200,512]{1,0:T(8,128)(2,1)S(1)}, s16[200,512]{1,0:T(8,128)(2,1)S(1)}, u32[]{:S(2)}, u32[]{:S(2)}) %collective-permute-start.30) | collective-permute-done | bytes 204832 | tf_op jit(solution)/shard_map/ppermute | solution.py:51
  120.7 2.8 %collective-permute-done.31.d = s16[200,512]{1,0:T(8,128)(2,1)S(1)} collective-permute-done((s16[200,512]{1,0:T(8,128)(2,1)S(1)}, s16[200,512]{1,0:T(8,128)(2,1)S(1)}, u32[]{:S(2)}, u32[]{:S(2)}) %collective-permute-start.31) | collective-permute-done | bytes 204832 | tf_op jit(solution)/shard_map/ppermute | solution.py:51
  125.7 4.8 %collective-permute-start.21 = (s16[200,256]{1,0:T(8,128)(2,1)S(1)}, s16[200,256]{1,0:T(8,128)(2,1)S(1)}, u32[]{:S(2)}, u32[]{:S(2)}) collective-permute-start(s16[200,256]{1,0:T(8,128)(2,1)S(1)} %get-tuple-element.59), channel_id=1, source_target_pairs={{0,64},{1,65},{2,66},{3,67},{4,68},{5,69},{6,70},{7,71},{8,72},{9,... | collective-permute-start | bytes 307208 | tf_op jit(solution)/shard_map/ppermute | solution.py:51
  130.5 1.7 %collective-permute-start.22 = (s16[200,256]{1,0:T(8,128)(2,1)S(1)}, s16[200,256]{1,0:T(8,128)(2,1)S(1)}, u32[]{:S(2)}, u32[]{:S(2)}) collective-permute-start(s16[200,256]{1,0:T(8,128)(2,1)S(1)} %get-tuple-element.60), channel_id=1, source_target_pairs={{0,96},{1,97},{2,98},{3,99},{4,100},{5,101},{6,102},{7,103},{8,104... | collective-permute-start | bytes 307208 | tf_op jit(solution)/shard_map/ppermute | solution.py:51
  133.3 2.2 %collective-permute-start.34 = (s16[200,128]{1,0:T(8,128)(2,1)S(1)}, s16[200,128]{1,0:T(8,128)(2,1)S(1)}, u32[]{:S(2)}, u32[]{:S(2)}) collective-permute-start(s16[200,128]{1,0:T(8,128)(2,1)S(1)} %get-tuple-element.78), channel_id=1, source_target_pairs={{0,12},{1,13},{2,14},{3,15},{4,0},{5,1},{6,2},{7,3},{8,4},{9,5},{1... | collective-permute-start | bytes 153608 | tf_op jit(solution)/shard_map/ppermute | solution.py:51
  135.5 2.4 %collective-permute-done.33.rb = s16[200,128]{1,0:T(8,128)(2,1)S(1)} collective-permute-done((s16[200,128]{1,0:T(8,128)(2,1)S(1)}, s16[200,128]{1,0:T(8,128)(2,1)S(1)}, u32[]{:S(2)}, u32[]{:S(2)}) %collective-permute-start.33) | collective-permute-done | bytes 51232 | tf_op jit(solution)/shard_map/ppermute | solution.py:51
  (62 shorter events, 19.2 us)
Async XLA Ops:
  4.2 17.5 %collective-permute-start.1 = (bf16[6,16,3072]{2,1,0:T(8,128)(2,1)S(1)}, bf16[6,16,3072]{2,1,0:T(8,128)(2,1)S(1)}, u32[]{:S(2)}, u32[]{:S(2)}) collective-permute-start(bf16[6,16,3072]{2,1,0:T(8,128)(2,1)S(1)} %get-tuple-element.43), channel_id=1, source_target_pairs={{0,32},{1,33},{2,34},{3,35},{4,36},{5,37},{6,38},{7,39},{8,40},{9,... | collective-permute-start | bytes 1769480 | tf_op jit(solution)/shard_map/ppermute | solution.py:51
  6.3 29.3 %collective-permute-start.3 = (bf16[6,16,3072]{2,1,0:T(8,128)(2,1)S(1)}, bf16[6,16,3072]{2,1,0:T(8,128)(2,1)S(1)}, u32[]{:S(2)}, u32[]{:S(2)}) collective-permute-start(bf16[6,16,3072]{2,1,0:T(8,128)(2,1)S(1)} %get-tuple-element.44), channel_id=1, source_target_pairs={{0,64},{1,65},{2,66},{3,67},{4,68},{5,69},{6,70},{7,71},{8,72},{9,... | collective-permute-start | bytes 1769480 | tf_op jit(solution)/shard_map/ppermute | solution.py:51
  9.9 25.7 %collective-permute-start.5 = (bf16[6,16,3072]{2,1,0:T(8,128)(2,1)S(1)}, bf16[6,16,3072]{2,1,0:T(8,128)(2,1)S(1)}, u32[]{:S(2)}, u32[]{:S(2)}) collective-permute-start(bf16[6,16,3072]{2,1,0:T(8,128)(2,1)S(1)} %get-tuple-element.45), channel_id=1, source_target_pairs={{0,96},{1,97},{2,98},{3,99},{4,100},{5,101},{6,102},{7,103},{8,104... | collective-permute-start | bytes 1769480 | tf_op jit(solution)/shard_map/ppermute | solution.py:51
  10.9 41.4 %collective-permute-start = (bf16[6,16,3072]{2,1,0:T(8,128)(2,1)S(1)}, bf16[6,16,3072]{2,1,0:T(8,128)(2,1)S(1)}, u32[]{:S(2)}, u32[]{:S(2)}) collective-permute-start(bf16[6,16,3072]{2,1,0:T(8,128)(2,1)S(1)} %get-tuple-element.42.refs_0_), channel_id=1, source_target_pairs={{0,16},{1,17},{2,18},{3,19},{4,20},{5,21},{6,22},{7,23},{8,24},{9,... | collective-permute-start | bytes 1769480 | tf_op jit(solution)/shard_map/ppermute | solution.py:51
  21.8 30.5 %collective-permute-start.2 = (bf16[6,16,3072]{2,1,0:T(8,128)(2,1)S(1)}, bf16[6,16,3072]{2,1,0:T(8,128)(2,1)S(1)}, u32[]{:S(2)}, u32[]{:S(2)}) collective-permute-start(bf16[6,16,3072]{2,1,0:T(8,128)(2,1)S(1)} %collective-permute-done.1.refs_2_), channel_id=1, source_target_pairs={{0,16},{1,17},{2,18},{3,19},{4,20},{5,21},{6,22},{7,23},{8,24},{9,... | collective-permute-start | bytes 1769480 | tf_op jit(solution)/shard_map/ppermute | solution.py:51
  35.6 16.7 %collective-permute-start.4 = (bf16[6,16,3072]{2,1,0:T(8,128)(2,1)S(1)}, bf16[6,16,3072]{2,1,0:T(8,128)(2,1)S(1)}, u32[]{:S(2)}, u32[]{:S(2)}) collective-permute-start(bf16[6,16,3072]{2,1,0:T(8,128)(2,1)S(1)} %collective-permute-done.3.refs_4_), channel_id=1, source_target_pairs={{0,16},{1,17},{2,18},{3,19},{4,20},{5,21},{6,22},{7,23},{8,24},{9,... | collective-permute-start | bytes 1769480 | tf_op jit(solution)/shard_map/ppermute | solution.py:51
  35.6 16.7 %collective-permute-start.6 = (bf16[6,16,3072]{2,1,0:T(8,128)(2,1)S(1)}, bf16[6,16,3072]{2,1,0:T(8,128)(2,1)S(1)}, u32[]{:S(2)}, u32[]{:S(2)}) collective-permute-start(bf16[6,16,3072]{2,1,0:T(8,128)(2,1)S(1)} %collective-permute-done.5.refs_6_), channel_id=1, source_target_pairs={{0,16},{1,17},{2,18},{3,19},{4,20},{5,21},{6,22},{7,23},{8,24},{9,... | collective-permute-start | bytes 1769480 | tf_op jit(solution)/shard_map/ppermute | solution.py:51
  46.9 5.2 %collective-permute-start.9 = (bf16[32,128]{1,0:T(8,128)(2,1)S(1)}, bf16[32,128]{1,0:T(8,128)(2,1)S(1)}, u32[]{:S(2)}, u32[]{:S(2)}) collective-permute-start(bf16[32,128]{1,0:T(8,128)(2,1)S(1)} %constant_dynamic-update-slice_fusion.refs_0_), channel_id=1, source_target_pairs={{0,64},{1,65},{2,66},{3,67},{4,68},{5,69},{6,70},{7,71},{8,72},{9,... | collective-permute-start | bytes 24584 | tf_op jit(solution)/shard_map/ppermute | solution.py:51
  56.1 13.4 %collective-permute-start.11 = (s16[392,1024]{1,0:T(8,128)(2,1)S(1)}, s16[392,1024]{1,0:T(8,128)(2,1)S(1)}, u32[]{:S(2)}, u32[]{:S(2)}) collective-permute-start(s16[392,1024]{1,0:T(8,128)(2,1)S(1)} %get-tuple-element.48), channel_id=1, source_target_pairs={{0,4},{1,5},{2,6},{3,7},{4,8},{5,9},{6,10},{7,11},{8,12},{9,13},{1... | collective-permute-start | bytes 2408456 | tf_op jit(solution)/shard_map/ppermute | solution.py:51
  57.6 13.6 %collective-permute-start.12 = (s16[392,1024]{1,0:T(8,128)(2,1)S(1)}, s16[392,1024]{1,0:T(8,128)(2,1)S(1)}, u32[]{:S(2)}, u32[]{:S(2)}) collective-permute-start(s16[392,1024]{1,0:T(8,128)(2,1)S(1)} %get-tuple-element.49), channel_id=1, source_target_pairs={{0,12},{1,13},{2,14},{3,15},{4,0},{5,1},{6,2},{7,3},{8,4},{9,5},{1... | collective-permute-start | bytes 2408456 | tf_op jit(solution)/shard_map/ppermute | solution.py:51
  61.0 13.7 %collective-permute-start.23 = (s16[1552,128]{1,0:T(8,128)(2,1)S(1)}, s16[1552,128]{1,0:T(8,128)(2,1)S(1)}, u32[]{:S(2)}, u32[]{:S(2)}) collective-permute-start(s16[1552,128]{1,0:T(8,128)(2,1)S(1)} %get-tuple-element.64), channel_id=1, source_target_pairs={{0,32},{1,33},{2,34},{3,35},{4,36},{5,37},{6,38},{7,39},{8,40},{9,... | collective-permute-start | bytes 1191944 | tf_op jit(solution)/shard_map/ppermute | solution.py:51
  61.1 14.1 %collective-permute-start.24 = (s16[1552,128]{1,0:T(8,128)(2,1)S(1)}, s16[1552,128]{1,0:T(8,128)(2,1)S(1)}, u32[]{:S(2)}, u32[]{:S(2)}) collective-permute-start(s16[1552,128]{1,0:T(8,128)(2,1)S(1)} %get-tuple-element.66), channel_id=1, source_target_pairs={{0,96},{1,97},{2,98},{3,99},{4,100},{5,101},{6,102},{7,103},{8,104... | collective-permute-start | bytes 1191944 | tf_op jit(solution)/shard_map/ppermute | solution.py:51
  65.9 11.5 %collective-permute-start.26 = (s16[1552,128]{1,0:T(8,128)(2,1)S(1)}, s16[1552,128]{1,0:T(8,128)(2,1)S(1)}, u32[]{:S(2)}, u32[]{:S(2)}) collective-permute-start(s16[1552,128]{1,0:T(8,128)(2,1)S(1)} %get-tuple-element.68), channel_id=1, source_target_pairs={{0,96},{1,97},{2,98},{3,99},{4,100},{5,101},{6,102},{7,103},{8,104... | collective-permute-start | bytes 1191944 | tf_op jit(solution)/shard_map/ppermute | solution.py:51
  69.5 11.1 %collective-permute-start.27 = (s16[1552,128]{1,0:T(8,128)(2,1)S(1)}, s16[1552,128]{1,0:T(8,128)(2,1)S(1)}, u32[]{:S(2)}, u32[]{:S(2)}) collective-permute-start(s16[1552,128]{1,0:T(8,128)(2,1)S(1)} %get-tuple-element.69), channel_id=1, source_target_pairs={{0,32},{1,33},{2,34},{3,35},{4,36},{5,37},{6,38},{7,39},{8,40},{9,... | collective-permute-start | bytes 1191944 | tf_op jit(solution)/shard_map/ppermute | solution.py:51
  71.3 27.7 %collective-permute-start.14 = (s16[392,1024]{1,0:T(8,128)(2,1)S(1)}, s16[392,1024]{1,0:T(8,128)(2,1)S(1)}, u32[]{:S(2)}, u32[]{:S(2)}) collective-permute-start(s16[392,1024]{1,0:T(8,128)(2,1)S(1)} %get-tuple-element.51), channel_id=1, source_target_pairs={{0,12},{1,13},{2,14},{3,15},{4,0},{5,1},{6,2},{7,3},{8,4},{9,5},{1... | collective-permute-start | bytes 2408456 | tf_op jit(solution)/shard_map/ppermute | solution.py:51
  74.6 24.4 %collective-permute-start.15 = (s16[392,1024]{1,0:T(8,128)(2,1)S(1)}, s16[392,1024]{1,0:T(8,128)(2,1)S(1)}, u32[]{:S(2)}, u32[]{:S(2)}) collective-permute-start(s16[392,1024]{1,0:T(8,128)(2,1)S(1)} %get-tuple-element.52), channel_id=1, source_target_pairs={{0,4},{1,5},{2,6},{3,7},{4,8},{5,9},{6,10},{7,11},{8,12},{9,13},{1... | collective-permute-start | bytes 2408456 | tf_op jit(solution)/shard_map/ppermute | solution.py:51
  75.2 28.0 %collective-permute-start.13 = (s16[392,1024]{1,0:T(8,128)(2,1)S(1)}, s16[392,1024]{1,0:T(8,128)(2,1)S(1)}, u32[]{:S(2)}, u32[]{:S(2)}) collective-permute-start(s16[392,1024]{1,0:T(8,128)(2,1)S(1)} %get-tuple-element.50), channel_id=1, source_target_pairs={{0,4},{1,5},{2,6},{3,7},{4,8},{5,9},{6,10},{7,11},{8,12},{9,13},{1... | collective-permute-start | bytes 2408456 | tf_op jit(solution)/shard_map/ppermute | solution.py:51
  77.4 25.8 %collective-permute-start.16 = (s16[392,1024]{1,0:T(8,128)(2,1)S(1)}, s16[392,1024]{1,0:T(8,128)(2,1)S(1)}, u32[]{:S(2)}, u32[]{:S(2)}) collective-permute-start(s16[392,1024]{1,0:T(8,128)(2,1)S(1)} %get-tuple-element.53), channel_id=1, source_target_pairs={{0,12},{1,13},{2,14},{3,15},{4,0},{5,1},{6,2},{7,3},{8,4},{9,5},{1... | collective-permute-start | bytes 2408456 | tf_op jit(solution)/shard_map/ppermute | solution.py:51
  80.7 9.6 %collective-permute-start.25 = (s16[1552,128]{1,0:T(8,128)(2,1)S(1)}, s16[1552,128]{1,0:T(8,128)(2,1)S(1)}, u32[]{:S(2)}, u32[]{:S(2)}) collective-permute-start(s16[1552,128]{1,0:T(8,128)(2,1)S(1)} %get-tuple-element.67), channel_id=1, source_target_pairs={{0,32},{1,33},{2,34},{3,35},{4,36},{5,37},{6,38},{7,39},{8,40},{9,... | collective-permute-start | bytes 1191944 | tf_op jit(solution)/shard_map/ppermute | solution.py:51
  90.2 7.8 %collective-permute-start.28 = (s16[1552,128]{1,0:T(8,128)(2,1)S(1)}, s16[1552,128]{1,0:T(8,128)(2,1)S(1)}, u32[]{:S(2)}, u32[]{:S(2)}) collective-permute-start(s16[1552,128]{1,0:T(8,128)(2,1)S(1)} %get-tuple-element.70), channel_id=1, source_target_pairs={{0,96},{1,97},{2,98},{3,99},{4,100},{5,101},{6,102},{7,103},{8,104... | collective-permute-start | bytes 1191944 | tf_op jit(solution)/shard_map/ppermute | solution.py:51
  98.7 12.5 %collective-permute-start.29 = (s16[200,512]{1,0:T(8,128)(2,1)S(1)}, s16[200,512]{1,0:T(8,128)(2,1)S(1)}, u32[]{:S(2)}, u32[]{:S(2)}) collective-permute-start(s16[200,512]{1,0:T(8,128)(2,1)S(1)} %get-tuple-element.72), channel_id=1, source_target_pairs={{0,1},{1,2},{2,3},{3,0},{4,5},{5,6},{6,7},{7,4},{8,9},{9,10},{10,1... | collective-permute-start | bytes 614408 | tf_op jit(solution)/shard_map/ppermute | solution.py:51
  103.5 20.3 %collective-permute-start.18 = (s16[200,1024]{1,0:T(8,128)(2,1)S(1)}, s16[200,1024]{1,0:T(8,128)(2,1)S(1)}, u32[]{:S(2)}, u32[]{:S(2)}) collective-permute-start(s16[200,1024]{1,0:T(8,128)(2,1)S(1)} %bulk_second_sum.3), channel_id=1, source_target_pairs={{0,2},{1,3},{2,0},{3,1},{4,6},{5,7},{6,4},{7,5},{8,10},{9,11},{10,... | collective-permute-start | bytes 1228808 | tf_op jit(solution)/shard_map/ppermute | solution.py:51
  107.9 15.9 %collective-permute-start.17 = (s16[200,1024]{1,0:T(8,128)(2,1)S(1)}, s16[200,1024]{1,0:T(8,128)(2,1)S(1)}, u32[]{:S(2)}, u32[]{:S(2)}) collective-permute-start(s16[200,1024]{1,0:T(8,128)(2,1)S(1)} %get-tuple-element.55), channel_id=1, source_target_pairs={{0,1},{1,2},{2,3},{3,0},{4,5},{5,6},{6,7},{7,4},{8,9},{9,10},{10,1... | collective-permute-start | bytes 1228808 | tf_op jit(solution)/shard_map/ppermute | solution.py:51
  108.7 15.2 %collective-permute-start.19 = (s16[200,1024]{1,0:T(8,128)(2,1)S(1)}, s16[200,1024]{1,0:T(8,128)(2,1)S(1)}, u32[]{:S(2)}, u32[]{:S(2)}) collective-permute-start(s16[200,1024]{1,0:T(8,128)(2,1)S(1)} %get-tuple-element.56), channel_id=1, source_target_pairs={{0,3},{1,0},{2,1},{3,2},{4,7},{5,4},{6,5},{7,6},{8,11},{9,8},{10,9... | collective-permute-start | bytes 1228808 | tf_op jit(solution)/shard_map/ppermute | solution.py:51
  111.2 9.5 %collective-permute-start.30 = (s16[200,512]{1,0:T(8,128)(2,1)S(1)}, s16[200,512]{1,0:T(8,128)(2,1)S(1)}, u32[]{:S(2)}, u32[]{:S(2)}) collective-permute-start(s16[200,512]{1,0:T(8,128)(2,1)S(1)} %get-tuple-element.73), channel_id=1, source_target_pairs={{0,2},{1,3},{2,0},{3,1},{4,6},{5,7},{6,4},{7,5},{8,10},{9,11},{10,... | collective-permute-start | bytes 614408 | tf_op jit(solution)/shard_map/ppermute | solution.py:51
  111.2 12.3 %collective-permute-start.31 = (s16[200,512]{1,0:T(8,128)(2,1)S(1)}, s16[200,512]{1,0:T(8,128)(2,1)S(1)}, u32[]{:S(2)}, u32[]{:S(2)}) collective-permute-start(s16[200,512]{1,0:T(8,128)(2,1)S(1)} %get-tuple-element.74), channel_id=1, source_target_pairs={{0,3},{1,0},{2,1},{3,2},{4,7},{5,4},{6,5},{7,6},{8,11},{9,8},{10,9... | collective-permute-start | bytes 614408 | tf_op jit(solution)/shard_map/ppermute | solution.py:51
  123.7 9.6 %collective-permute-start.32 = (s16[200,128]{1,0:T(8,128)(2,1)S(1)}, s16[200,128]{1,0:T(8,128)(2,1)S(1)}, u32[]{:S(2)}, u32[]{:S(2)}) collective-permute-start(s16[200,128]{1,0:T(8,128)(2,1)S(1)} %get-tuple-element.76), channel_id=1, source_target_pairs={{0,4},{1,5},{2,6},{3,7},{4,8},{5,9},{6,10},{7,11},{8,12},{9,13},{1... | collective-permute-start | bytes 153608 | tf_op jit(solution)/shard_map/ppermute | solution.py:51
  124.3 14.7 %collective-permute-start.20 = (s16[200,256]{1,0:T(8,128)(2,1)S(1)}, s16[200,256]{1,0:T(8,128)(2,1)S(1)}, u32[]{:S(2)}, u32[]{:S(2)}) collective-permute-start(s16[200,256]{1,0:T(8,128)(2,1)S(1)} %get-tuple-element.58), channel_id=1, source_target_pairs={{0,32},{1,33},{2,34},{3,35},{4,36},{5,37},{6,38},{7,39},{8,40},{9,... | collective-permute-start | bytes 307208 | tf_op jit(solution)/shard_map/ppermute | solution.py:51
  125.7 13.2 %collective-permute-start.21 = (s16[200,256]{1,0:T(8,128)(2,1)S(1)}, s16[200,256]{1,0:T(8,128)(2,1)S(1)}, u32[]{:S(2)}, u32[]{:S(2)}) collective-permute-start(s16[200,256]{1,0:T(8,128)(2,1)S(1)} %get-tuple-element.59), channel_id=1, source_target_pairs={{0,64},{1,65},{2,66},{3,67},{4,68},{5,69},{6,70},{7,71},{8,72},{9,... | collective-permute-start | bytes 307208 | tf_op jit(solution)/shard_map/ppermute | solution.py:51
  130.5 8.5 %collective-permute-start.22 = (s16[200,256]{1,0:T(8,128)(2,1)S(1)}, s16[200,256]{1,0:T(8,128)(2,1)S(1)}, u32[]{:S(2)}, u32[]{:S(2)}) collective-permute-start(s16[200,256]{1,0:T(8,128)(2,1)S(1)} %get-tuple-element.60), channel_id=1, source_target_pairs={{0,96},{1,97},{2,98},{3,99},{4,100},{5,101},{6,102},{7,103},{8,104... | collective-permute-start | bytes 307208 | tf_op jit(solution)/shard_map/ppermute | solution.py:51
  132.3 5.6 %collective-permute-start.33 = (s16[200,128]{1,0:T(8,128)(2,1)S(1)}, s16[200,128]{1,0:T(8,128)(2,1)S(1)}, u32[]{:S(2)}, u32[]{:S(2)}) collective-permute-start(s16[200,128]{1,0:T(8,128)(2,1)S(1)} %get-tuple-element.77), channel_id=1, source_target_pairs={{0,8},{1,9},{2,10},{3,11},{4,12},{5,13},{6,14},{7,15},{8,0},{9,1},... | collective-permute-start | bytes 153608 | tf_op jit(solution)/shard_map/ppermute | solution.py:51
  133.3 5.7 %collective-permute-start.34 = (s16[200,128]{1,0:T(8,128)(2,1)S(1)}, s16[200,128]{1,0:T(8,128)(2,1)S(1)}, u32[]{:S(2)}, u32[]{:S(2)}) collective-permute-start(s16[200,128]{1,0:T(8,128)(2,1)S(1)} %get-tuple-element.78), channel_id=1, source_target_pairs={{0,12},{1,13},{2,14},{3,15},{4,0},{5,1},{6,2},{7,3},{8,4},{9,5},{1... | collective-permute-start | bytes 153608 | tf_op jit(solution)/shard_map/ppermute | solution.py:51
  (5 other events, 46.9 us)

commit v4 on v3

--- a/solution.py
+++ b/solution.py
@@ -80,16 +80,21 @@
     ]
     for copy in copies:
         copy.start()
-    group = outs[0].shape[0]
     for n in range(chunks):
         copies[n].wait()
-        for m in range(n * (lanes // block), (n + 1) * (lanes // block)):
-            cut = slice(m * block, (m + 1) * block)
+
+        def step(m, carry):
+            m = n * (lanes // block) + m
+            cut = pl.ds(pl.multiple_of(m * block, block), block)
             keep = survive[0, 0, m].astype(F32)
             turned[:, :, cut] = jnp.swapaxes(held[:, :, cut].astype(F32) * keep, 0, 1).astype(BF)
-        cut = slice(n * lanes, (n + 1) * lanes)
-        for k in range(RING):
-            outs[k][:, :, cut] = turned[pl.ds(lax.rem(at[0] + k, RING) * group, group), :, cut]
+            return carry
+
+        lax.fori_loop(0, lanes // block, step, 0, unroll=True)
+    group = outs[0].shape[0]
+    for k in range(RING):
+        first = lax.rem(at[0] + k, RING) * group
+        outs[k][...] = turned[pl.ds(first, group)]
 
 
 def screen(survive, half):
@@ -194,7 +199,7 @@
 
 
 def exponent(top):
-    return jnp.floor(14.9 - jnp.log2(jnp.maximum(top, 1e-30)))
+    return jnp.floor(14.9 - jnp.log2(jnp.maximum(top, 1e-33)))
 
 
 def coded(v, e):

time: 140 us -> 140 us (level)
  no operation moved by 1% of the time
where the time goes in v4:
time: 140 us; the launch traced here: 139 us
  waiting for transfers between devices  75.3 us (54%)
  starting transfers between devices  44.2 us (32%)
  Pallas kernels  19 us (14%)
    ppermute x35, waiting for transfers between devices, send(): return lax.ppermute(v, AXES, moves(shift))  75.3 us
    ppermute x35, starting transfers between devices, send(): return lax.ppermute(v, AXES, moves(shift))  44.2 us
    pallas_call x3, Pallas kernels, bulk_k(): pl.pallas_call(functools.partial(bulk_body, blocks), out_shape=[jax.Shape...  4.83 us
    pallas_call x1, Pallas kernels, fit(): pl.pallas_call(fit_body, grid=(steps,), out_shape=[jax.ShapeDtypeStruct(*...  3.76 us
    pallas_call x2, Pallas kernels, rest_k(): pl.pallas_call(functools.partial(rest_body, steps, cut), out_shape=[jax.S...  3.17 us
    pallas_call x1, Pallas kernels, screen(): pl.pallas_call(screen_body, out_shape=[out] * RING, in_specs=[scalars(),...  3.12 us
  transfers between devices with their start and end apart: 35, of which 15 were waited for; matrix products, arithmetic and copies ran while one was open for 0% of the time, Pallas kernels for 8%

profile of v4, /device:TPU:0, one launch (start us, length us, event | category | flops | bytes accessed | tf_op | source)
XLA Modules:
  0.0 139.4 jit_solution(8053249793641147056)
XLA Ops:
  0.7 3.1 %screen.1 = (bf16[6,16,3072]{2,1,0:T(8,128)(2,1)S(1)}, bf16[6,16,3072]{2,1,0:T(8,128)(2,1)S(1)}, bf16[6,16,3072]{2,1,0:T(8,128)(2,1)S(1)}, bf16[6,16,3072]{2,1,0:T(8,128)(2,1)S(1)}) custom-call(s32[1,1,24]{2,1,0:T(1,128)S(1)} %copy-done.1, bf16[16,24,3072]{2,1,0:T(8,128)(2,1)} %half.1), custom_call_target="tpu_custom_call" | custom-call | flops 1179648 | bytes 4718592 | tf_op jit(solution)/shard_map/screen/pallas_call | solution.py:104
  3.8 2.1 %collective-permute-start.1 = (bf16[6,16,3072]{2,1,0:T(8,128)(2,1)S(1)}, bf16[6,16,3072]{2,1,0:T(8,128)(2,1)S(1)}, u32[]{:S(2)}, u32[]{:S(2)}) collective-permute-start(bf16[6,16,3072]{2,1,0:T(8,128)(2,1)S(1)} %get-tuple-element.43), channel_id=1, source_target_pairs={{0,32},{1,33},{2,34},{3,35},{4,36},{5,37},{6,38},{7,39},{8,40},{9,... | collective-permute-start | bytes 1769480 | tf_op jit(solution)/shard_map/ppermute | solution.py:51
  5.9 3.6 %collective-permute-start.3 = (bf16[6,16,3072]{2,1,0:T(8,128)(2,1)S(1)}, bf16[6,16,3072]{2,1,0:T(8,128)(2,1)S(1)}, u32[]{:S(2)}, u32[]{:S(2)}) collective-permute-start(bf16[6,16,3072]{2,1,0:T(8,128)(2,1)S(1)} %get-tuple-element.44), channel_id=1, source_target_pairs={{0,64},{1,65},{2,66},{3,67},{4,68},{5,69},{6,70},{7,71},{8,72},{9,... | collective-permute-start | bytes 1769480 | tf_op jit(solution)/shard_map/ppermute | solution.py:51
  10.5 10.9 %collective-permute-done.1.refs_2_ = bf16[6,16,3072]{2,1,0:T(8,128)(2,1)S(1)} collective-permute-done((bf16[6,16,3072]{2,1,0:T(8,128)(2,1)S(1)}, bf16[6,16,3072]{2,1,0:T(8,128)(2,1)S(1)}, u32[]{:S(2)}, u32[]{:S(2)}) %collective-permute-start.1) | collective-permute-done | bytes 589856 | tf_op jit(solution)/shard_map/ppermute | solution.py:51
  21.3 13.8 %collective-permute-done.3.refs_4_ = bf16[6,16,3072]{2,1,0:T(8,128)(2,1)S(1)} collective-permute-done((bf16[6,16,3072]{2,1,0:T(8,128)(2,1)S(1)}, bf16[6,16,3072]{2,1,0:T(8,128)(2,1)S(1)}, u32[]{:S(2)}, u32[]{:S(2)}) %collective-permute-start.3) | collective-permute-done | bytes 589856 | tf_op jit(solution)/shard_map/ppermute | solution.py:51
  35.8 2.2 %collective-permute-done.7 = bf16[16,128]{1,0:T(8,128)(2,1)S(1)} collective-permute-done((bf16[16,128]{1,0:T(8,128)(2,1)S(1)}, bf16[16,128]{1,0:T(8,128)(2,1)S(1)}, u32[]{:S(2)}, u32[]{:S(2)}) %collective-permute-start.7) | collective-permute-done | bytes 4128 | tf_op jit(solution)/shard_map/ppermute | solution.py:51
  39.3 2.3 %collective-permute-done.10.refs_3_ = bf16[32,128]{1,0:T(8,128)(2,1)S(1)} collective-permute-done((bf16[32,128]{1,0:T(8,128)(2,1)S(1)}, bf16[32,128]{1,0:T(8,128)(2,1)S(1)}, u32[]{:S(2)}, u32[]{:S(2)}) %collective-permute-start.10) | collective-permute-done | bytes 8224 | tf_op jit(solution)/shard_map/ppermute | solution.py:51
  42.1 4.5 %collective-permute-done.8.refs_1_ = bf16[32,128]{1,0:T(8,128)(2,1)S(1)} collective-permute-done((bf16[32,128]{1,0:T(8,128)(2,1)S(1)}, bf16[32,128]{1,0:T(8,128)(2,1)S(1)}, u32[]{:S(2)}, u32[]{:S(2)}) %collective-permute-start.8) | collective-permute-done | bytes 8224 | tf_op jit(solution)/shard_map/ppermute | solution.py:51
  47.0 4.7 %collective-permute-done.9.refs_2_ = bf16[32,128]{1,0:T(8,128)(2,1)S(1)} collective-permute-done((bf16[32,128]{1,0:T(8,128)(2,1)S(1)}, bf16[32,128]{1,0:T(8,128)(2,1)S(1)}, u32[]{:S(2)}, u32[]{:S(2)}) %collective-permute-start.9) | collective-permute-done | bytes 8224 | tf_op jit(solution)/shard_map/ppermute | solution.py:51
  51.9 3.8 %fit.1 = (bf16[768,1024]{1,0:T(8,128)(2,1)S(1)}, bf16[768,512]{1,0:T(8,128)(2,1)S(1)}, bf16[3072,768]{1,0:T(8,128)(2,1)S(1)}, s16[392,1024]{1,0:T(8,128)(2,1)S(1)}, s16[392,1024]{1,0:T(8,128)(2,1)S(1)}) custom-call(bf16[6,16,3072]{2,1,0:T(8,128)(2,1)S(1)} %get-tuple-element.42.refs_0_, bf16[6,16,3072]{2,1,0:T(8,128)(2,1)S(1)} %collective-permute-done.refs_1_, ...), custom_call_target="tpu_custom_call" | custom-call | flops 2415919104 | bytes 14155776 | tf_op jit(solution)/shard_map/fit/pallas_call | solution.py:189
  57.2 1.7 %collective-permute-start.12 = (s16[392,1024]{1,0:T(8,128)(2,1)S(1)}, s16[392,1024]{1,0:T(8,128)(2,1)S(1)}, u32[]{:S(2)}, u32[]{:S(2)}) collective-permute-start(s16[392,1024]{1,0:T(8,128)(2,1)S(1)} %get-tuple-element.49), channel_id=1, source_target_pairs={{0,12},{1,13},{2,14},{3,15},{4,0},{5,1},{6,2},{7,3},{8,4},{9,5},{1... | collective-permute-start | bytes 2408456 | tf_op jit(solution)/shard_map/ppermute | solution.py:51
  60.6 3.2 %collective-permute-start.24 = (s16[1552,128]{1,0:T(8,128)(2,1)S(1)}, s16[1552,128]{1,0:T(8,128)(2,1)S(1)}, u32[]{:S(2)}, u32[]{:S(2)}) collective-permute-start(s16[1552,128]{1,0:T(8,128)(2,1)S(1)} %get-tuple-element.66), channel_id=1, source_target_pairs={{0,96},{1,97},{2,98},{3,99},{4,100},{5,101},{6,102},{7,103},{8,104... | collective-permute-start | bytes 1191944 | tf_op jit(solution)/shard_map/ppermute | solution.py:51
  63.9 1.6 %shard_map.41 = (f32[1536,128]{1,0:T(8,128)S(1)}, s16[1552,128]{1,0:T(8,128)(2,1)S(1)}, s16[1552,128]{1,0:T(8,128)(2,1)S(1)}, f32[1536,128]{1,0:T(8,128)S(1)}) custom-call(bf16[768,512]{1,0:T(8,128)(2,1)S(1)} %get-tuple-element.61.rest, bf16[3072,768]{1,0:T(8,128)(2,1)S(1)} %get-tuple-element.47.turned), custom_call_target="tpu_custom_call" | custom-call | flops 1207959552 | bytes 1572864 | tf_op jit(solution)/shard_map/pallas_call | solution.py:294
  65.6 3.5 %collective-permute-done.11.refs_0_ = s16[392,1024]{1,0:T(8,128)(2,1)S(1)} collective-permute-done((s16[392,1024]{1,0:T(8,128)(2,1)S(1)}, s16[392,1024]{1,0:T(8,128)(2,1)S(1)}, u32[]{:S(2)}, u32[]{:S(2)}) %collective-permute-start.11) | collective-permute-done | bytes 802848 | tf_op jit(solution)/shard_map/ppermute | solution.py:51
  69.1 1.7 %shard_map.39 = (s16[392,1024]{1,0:T(8,128)(2,1)S(1)}, s16[392,1024]{1,0:T(8,128)(2,1)S(1)}) custom-call(bf16[768,1024]{1,0:T(8,128)(2,1)S(1)} %get-tuple-element.46.bulk, bf16[3072,768]{1,0:T(8,128)(2,1)S(1)} %get-tuple-element.47.turned), custom_call_target="tpu_custom_call" | custom-call | flops 1207959552 | bytes 1572864 | tf_op jit(solution)/shard_map/pallas_call | solution.py:259
  70.8 1.6 %collective-permute-start.14 = (s16[392,1024]{1,0:T(8,128)(2,1)S(1)}, s16[392,1024]{1,0:T(8,128)(2,1)S(1)}, u32[]{:S(2)}, u32[]{:S(2)}) collective-permute-start(s16[392,1024]{1,0:T(8,128)(2,1)S(1)} %get-tuple-element.51), channel_id=1, source_target_pairs={{0,12},{1,13},{2,14},{3,15},{4,0},{5,1},{6,2},{7,3},{8,4},{9,5},{1... | collective-permute-start | bytes 2408456 | tf_op jit(solution)/shard_map/ppermute | solution.py:51
  72.5 1.7 %shard_map.38 = (s16[392,1024]{1,0:T(8,128)(2,1)S(1)}, s16[392,1024]{1,0:T(8,128)(2,1)S(1)}) custom-call(bf16[768,1024]{1,0:T(8,128)(2,1)S(1)} %get-tuple-element.46.bulk, bf16[3072,768]{1,0:T(8,128)(2,1)S(1)} %get-tuple-element.47.turned, s16[392,1024]{1,0:T(8,128)(2,1)S(1)} %collective-permute-done.11.refs_0_, ...), custom_call_target="tpu_custom_call" | custom-call | flops 1207959552 | bytes 1572864 | tf_op jit(solution)/shard_map/pallas_call | solution.py:259
  75.1 1.9 %collective-permute-done.26.b = s16[1552,128]{1,0:T(8,128)(2,1)S(1)} collective-permute-done((s16[1552,128]{1,0:T(8,128)(2,1)S(1)}, s16[1552,128]{1,0:T(8,128)(2,1)S(1)}, u32[]{:S(2)}, u32[]{:S(2)}) %collective-permute-start.26) | collective-permute-done | bytes 397344 | tf_op jit(solution)/shard_map/ppermute | solution.py:51
  77.0 2.8 %collective-permute-start.16 = (s16[392,1024]{1,0:T(8,128)(2,1)S(1)}, s16[392,1024]{1,0:T(8,128)(2,1)S(1)}, u32[]{:S(2)}, u32[]{:S(2)}) collective-permute-start(s16[392,1024]{1,0:T(8,128)(2,1)S(1)} %get-tuple-element.53), channel_id=1, source_target_pairs={{0,12},{1,13},{2,14},{3,15},{4,0},{5,1},{6,2},{7,3},{8,4},{9,5},{1... | collective-permute-start | bytes 2408456 | tf_op jit(solution)/shard_map/ppermute | solution.py:51
  80.6 9.2 %collective-permute-done.25.a = s16[1552,128]{1,0:T(8,128)(2,1)S(1)} collective-permute-done((s16[1552,128]{1,0:T(8,128)(2,1)S(1)}, s16[1552,128]{1,0:T(8,128)(2,1)S(1)}, u32[]{:S(2)}, u32[]{:S(2)}) %collective-permute-start.25) | collective-permute-done | bytes 397344 | tf_op jit(solution)/shard_map/ppermute | solution.py:51
  89.8 2.0 %collective-permute-start.28 = (s16[1552,128]{1,0:T(8,128)(2,1)S(1)}, s16[1552,128]{1,0:T(8,128)(2,1)S(1)}, u32[]{:S(2)}, u32[]{:S(2)}) collective-permute-start(s16[1552,128]{1,0:T(8,128)(2,1)S(1)} %get-tuple-element.70), channel_id=1, source_target_pairs={{0,96},{1,97},{2,98},{3,99},{4,100},{5,101},{6,102},{7,103},{8,104... | collective-permute-start | bytes 1191944 | tf_op jit(solution)/shard_map/ppermute | solution.py:51
  93.2 4.4 %collective-permute-done.28.e = s16[1552,128]{1,0:T(8,128)(2,1)S(1)} collective-permute-done((s16[1552,128]{1,0:T(8,128)(2,1)S(1)}, s16[1552,128]{1,0:T(8,128)(2,1)S(1)}, u32[]{:S(2)}, u32[]{:S(2)}) %collective-permute-start.28) | collective-permute-done | bytes 397344 | tf_op jit(solution)/shard_map/ppermute | solution.py:51
  98.6 4.2 %collective-permute-done.13.a = s16[392,1024]{1,0:T(8,128)(2,1)S(1)} collective-permute-done((s16[392,1024]{1,0:T(8,128)(2,1)S(1)}, s16[392,1024]{1,0:T(8,128)(2,1)S(1)}, u32[]{:S(2)}, u32[]{:S(2)}) %collective-permute-start.13) | collective-permute-done | bytes 802848 | tf_op jit(solution)/shard_map/ppermute | solution.py:51
  103.1 3.4 %collective-permute-start.18 = (s16[200,1024]{1,0:T(8,128)(2,1)S(1)}, s16[200,1024]{1,0:T(8,128)(2,1)S(1)}, u32[]{:S(2)}, u32[]{:S(2)}) collective-permute-start(s16[200,1024]{1,0:T(8,128)(2,1)S(1)} %bulk_second_sum.3), channel_id=1, source_target_pairs={{0,2},{1,3},{2,0},{3,1},{4,6},{5,7},{6,4},{7,5},{8,10},{9,11},{10,... | collective-permute-start | bytes 1228808 | tf_op jit(solution)/shard_map/ppermute | solution.py:51
  108.2 2.6 %collective-permute-start.19 = (s16[200,1024]{1,0:T(8,128)(2,1)S(1)}, s16[200,1024]{1,0:T(8,128)(2,1)S(1)}, u32[]{:S(2)}, u32[]{:S(2)}) collective-permute-start(s16[200,1024]{1,0:T(8,128)(2,1)S(1)} %get-tuple-element.56), channel_id=1, source_target_pairs={{0,3},{1,0},{2,1},{3,2},{4,7},{5,4},{6,5},{7,6},{8,11},{9,8},{10,9... | collective-permute-start | bytes 1228808 | tf_op jit(solution)/shard_map/ppermute | solution.py:51
  110.8 2.1 %collective-permute-start.31 = (s16[200,512]{1,0:T(8,128)(2,1)S(1)}, s16[200,512]{1,0:T(8,128)(2,1)S(1)}, u32[]{:S(2)}, u32[]{:S(2)}) collective-permute-start(s16[200,512]{1,0:T(8,128)(2,1)S(1)} %get-tuple-element.74), channel_id=1, source_target_pairs={{0,3},{1,0},{2,1},{3,2},{4,7},{5,4},{6,5},{7,6},{8,11},{9,8},{10,9... | collective-permute-start | bytes 614408 | tf_op jit(solution)/shard_map/ppermute | solution.py:51
  113.0 7.3 %collective-permute-done.30.b = s16[200,512]{1,0:T(8,128)(2,1)S(1)} collective-permute-done((s16[200,512]{1,0:T(8,128)(2,1)S(1)}, s16[200,512]{1,0:T(8,128)(2,1)S(1)}, u32[]{:S(2)}, u32[]{:S(2)}) %collective-permute-start.30) | collective-permute-done | bytes 204832 | tf_op jit(solution)/shard_map/ppermute | solution.py:51
  120.3 2.8 %collective-permute-done.31.d = s16[200,512]{1,0:T(8,128)(2,1)S(1)} collective-permute-done((s16[200,512]{1,0:T(8,128)(2,1)S(1)}, s16[200,512]{1,0:T(8,128)(2,1)S(1)}, u32[]{:S(2)}, u32[]{:S(2)}) %collective-permute-start.31) | collective-permute-done | bytes 204832 | tf_op jit(solution)/shard_map/ppermute | solution.py:51
  125.3 4.8 %collective-permute-start.21 = (s16[200,256]{1,0:T(8,128)(2,1)S(1)}, s16[200,256]{1,0:T(8,128)(2,1)S(1)}, u32[]{:S(2)}, u32[]{:S(2)}) collective-permute-start(s16[200,256]{1,0:T(8,128)(2,1)S(1)} %get-tuple-element.59), channel_id=1, source_target_pairs={{0,64},{1,65},{2,66},{3,67},{4,68},{5,69},{6,70},{7,71},{8,72},{9,... | collective-permute-start | bytes 307208 | tf_op jit(solution)/shard_map/ppermute | solution.py:51
  130.1 1.7 %collective-permute-start.22 = (s16[200,256]{1,0:T(8,128)(2,1)S(1)}, s16[200,256]{1,0:T(8,128)(2,1)S(1)}, u32[]{:S(2)}, u32[]{:S(2)}) collective-permute-start(s16[200,256]{1,0:T(8,128)(2,1)S(1)} %get-tuple-element.60), channel_id=1, source_target_pairs={{0,96},{1,97},{2,98},{3,99},{4,100},{5,101},{6,102},{7,103},{8,104... | collective-permute-start | bytes 307208 | tf_op jit(solution)/shard_map/ppermute | solution.py:51
  132.9 2.2 %collective-permute-start.34 = (s16[200,128]{1,0:T(8,128)(2,1)S(1)}, s16[200,128]{1,0:T(8,128)(2,1)S(1)}, u32[]{:S(2)}, u32[]{:S(2)}) collective-permute-start(s16[200,128]{1,0:T(8,128)(2,1)S(1)} %get-tuple-element.78), channel_id=1, source_target_pairs={{0,12},{1,13},{2,14},{3,15},{4,0},{5,1},{6,2},{7,3},{8,4},{9,5},{1... | collective-permute-start | bytes 153608 | tf_op jit(solution)/shard_map/ppermute | solution.py:51
  135.1 2.4 %collective-permute-done.33.rb = s16[200,128]{1,0:T(8,128)(2,1)S(1)} collective-permute-done((s16[200,128]{1,0:T(8,128)(2,1)S(1)}, s16[200,128]{1,0:T(8,128)(2,1)S(1)}, u32[]{:S(2)}, u32[]{:S(2)}) %collective-permute-start.33) | collective-permute-done | bytes 51232 | tf_op jit(solution)/shard_map/ppermute | solution.py:51
  (62 shorter events, 19.2 us)
Async XLA Ops:
  3.8 17.5 %collective-permute-start.1 = (bf16[6,16,3072]{2,1,0:T(8,128)(2,1)S(1)}, bf16[6,16,3072]{2,1,0:T(8,128)(2,1)S(1)}, u32[]{:S(2)}, u32[]{:S(2)}) collective-permute-start(bf16[6,16,3072]{2,1,0:T(8,128)(2,1)S(1)} %get-tuple-element.43), channel_id=1, source_target_pairs={{0,32},{1,33},{2,34},{3,35},{4,36},{5,37},{6,38},{7,39},{8,40},{9,... | collective-permute-start | bytes 1769480 | tf_op jit(solution)/shard_map/ppermute | solution.py:51
  5.9 29.3 %collective-permute-start.3 = (bf16[6,16,3072]{2,1,0:T(8,128)(2,1)S(1)}, bf16[6,16,3072]{2,1,0:T(8,128)(2,1)S(1)}, u32[]{:S(2)}, u32[]{:S(2)}) collective-permute-start(bf16[6,16,3072]{2,1,0:T(8,128)(2,1)S(1)} %get-tuple-element.44), channel_id=1, source_target_pairs={{0,64},{1,65},{2,66},{3,67},{4,68},{5,69},{6,70},{7,71},{8,72},{9,... | collective-permute-start | bytes 1769480 | tf_op jit(solution)/shard_map/ppermute | solution.py:51
  9.5 25.7 %collective-permute-start.5 = (bf16[6,16,3072]{2,1,0:T(8,128)(2,1)S(1)}, bf16[6,16,3072]{2,1,0:T(8,128)(2,1)S(1)}, u32[]{:S(2)}, u32[]{:S(2)}) collective-permute-start(bf16[6,16,3072]{2,1,0:T(8,128)(2,1)S(1)} %get-tuple-element.45), channel_id=1, source_target_pairs={{0,96},{1,97},{2,98},{3,99},{4,100},{5,101},{6,102},{7,103},{8,104... | collective-permute-start | bytes 1769480 | tf_op jit(solution)/shard_map/ppermute | solution.py:51
  10.5 41.4 %collective-permute-start = (bf16[6,16,3072]{2,1,0:T(8,128)(2,1)S(1)}, bf16[6,16,3072]{2,1,0:T(8,128)(2,1)S(1)}, u32[]{:S(2)}, u32[]{:S(2)}) collective-permute-start(bf16[6,16,3072]{2,1,0:T(8,128)(2,1)S(1)} %get-tuple-element.42.refs_0_), channel_id=1, source_target_pairs={{0,16},{1,17},{2,18},{3,19},{4,20},{5,21},{6,22},{7,23},{8,24},{9,... | collective-permute-start | bytes 1769480 | tf_op jit(solution)/shard_map/ppermute | solution.py:51
  21.3 30.5 %collective-permute-start.2 = (bf16[6,16,3072]{2,1,0:T(8,128)(2,1)S(1)}, bf16[6,16,3072]{2,1,0:T(8,128)(2,1)S(1)}, u32[]{:S(2)}, u32[]{:S(2)}) collective-permute-start(bf16[6,16,3072]{2,1,0:T(8,128)(2,1)S(1)} %collective-permute-done.1.refs_2_), channel_id=1, source_target_pairs={{0,16},{1,17},{2,18},{3,19},{4,20},{5,21},{6,22},{7,23},{8,24},{9,... | collective-permute-start | bytes 1769480 | tf_op jit(solution)/shard_map/ppermute | solution.py:51
  35.2 16.7 %collective-permute-start.4 = (bf16[6,16,3072]{2,1,0:T(8,128)(2,1)S(1)}, bf16[6,16,3072]{2,1,0:T(8,128)(2,1)S(1)}, u32[]{:S(2)}, u32[]{:S(2)}) collective-permute-start(bf16[6,16,3072]{2,1,0:T(8,128)(2,1)S(1)} %collective-permute-done.3.refs_4_), channel_id=1, source_target_pairs={{0,16},{1,17},{2,18},{3,19},{4,20},{5,21},{6,22},{7,23},{8,24},{9,... | collective-permute-start | bytes 1769480 | tf_op jit(solution)/shard_map/ppermute | solution.py:51
  35.2 16.7 %collective-permute-start.6 = (bf16[6,16,3072]{2,1,0:T(8,128)(2,1)S(1)}, bf16[6,16,3072]{2,1,0:T(8,128)(2,1)S(1)}, u32[]{:S(2)}, u32[]{:S(2)}) collective-permute-start(bf16[6,16,3072]{2,1,0:T(8,128)(2,1)S(1)} %collective-permute-done.5.refs_6_), channel_id=1, source_target_pairs={{0,16},{1,17},{2,18},{3,19},{4,20},{5,21},{6,22},{7,23},{8,24},{9,... | collective-permute-start | bytes 1769480 | tf_op jit(solution)/shard_map/ppermute | solution.py:51
  46.5 5.2 %collective-permute-start.9 = (bf16[32,128]{1,0:T(8,128)(2,1)S(1)}, bf16[32,128]{1,0:T(8,128)(2,1)S(1)}, u32[]{:S(2)}, u32[]{:S(2)}) collective-permute-start(bf16[32,128]{1,0:T(8,128)(2,1)S(1)} %constant_dynamic-update-slice_fusion.refs_0_), channel_id=1, source_target_pairs={{0,64},{1,65},{2,66},{3,67},{4,68},{5,69},{6,70},{7,71},{8,72},{9,... | collective-permute-start | bytes 24584 | tf_op jit(solution)/shard_map/ppermute | solution.py:51
  55.7 13.4 %collective-permute-start.11 = (s16[392,1024]{1,0:T(8,128)(2,1)S(1)}, s16[392,1024]{1,0:T(8,128)(2,1)S(1)}, u32[]{:S(2)}, u32[]{:S(2)}) collective-permute-start(s16[392,1024]{1,0:T(8,128)(2,1)S(1)} %get-tuple-element.48), channel_id=1, source_target_pairs={{0,4},{1,5},{2,6},{3,7},{4,8},{5,9},{6,10},{7,11},{8,12},{9,13},{1... | collective-permute-start | bytes 2408456 | tf_op jit(solution)/shard_map/ppermute | solution.py:51
  57.2 13.6 %collective-permute-start.12 = (s16[392,1024]{1,0:T(8,128)(2,1)S(1)}, s16[392,1024]{1,0:T(8,128)(2,1)S(1)}, u32[]{:S(2)}, u32[]{:S(2)}) collective-permute-start(s16[392,1024]{1,0:T(8,128)(2,1)S(1)} %get-tuple-element.49), channel_id=1, source_target_pairs={{0,12},{1,13},{2,14},{3,15},{4,0},{5,1},{6,2},{7,3},{8,4},{9,5},{1... | collective-permute-start | bytes 2408456 | tf_op jit(solution)/shard_map/ppermute | solution.py:51
  60.6 13.7 %collective-permute-start.23 = (s16[1552,128]{1,0:T(8,128)(2,1)S(1)}, s16[1552,128]{1,0:T(8,128)(2,1)S(1)}, u32[]{:S(2)}, u32[]{:S(2)}) collective-permute-start(s16[1552,128]{1,0:T(8,128)(2,1)S(1)} %get-tuple-element.64), channel_id=1, source_target_pairs={{0,32},{1,33},{2,34},{3,35},{4,36},{5,37},{6,38},{7,39},{8,40},{9,... | collective-permute-start | bytes 1191944 | tf_op jit(solution)/shard_map/ppermute | solution.py:51
  60.6 14.1 %collective-permute-start.24 = (s16[1552,128]{1,0:T(8,128)(2,1)S(1)}, s16[1552,128]{1,0:T(8,128)(2,1)S(1)}, u32[]{:S(2)}, u32[]{:S(2)}) collective-permute-start(s16[1552,128]{1,0:T(8,128)(2,1)S(1)} %get-tuple-element.66), channel_id=1, source_target_pairs={{0,96},{1,97},{2,98},{3,99},{4,100},{5,101},{6,102},{7,103},{8,104... | collective-permute-start | bytes 1191944 | tf_op jit(solution)/shard_map/ppermute | solution.py:51
  65.5 11.5 %collective-permute-start.26 = (s16[1552,128]{1,0:T(8,128)(2,1)S(1)}, s16[1552,128]{1,0:T(8,128)(2,1)S(1)}, u32[]{:S(2)}, u32[]{:S(2)}) collective-permute-start(s16[1552,128]{1,0:T(8,128)(2,1)S(1)} %get-tuple-element.68), channel_id=1, source_target_pairs={{0,96},{1,97},{2,98},{3,99},{4,100},{5,101},{6,102},{7,103},{8,104... | collective-permute-start | bytes 1191944 | tf_op jit(solution)/shard_map/ppermute | solution.py:51
  69.1 11.1 %collective-permute-start.27 = (s16[1552,128]{1,0:T(8,128)(2,1)S(1)}, s16[1552,128]{1,0:T(8,128)(2,1)S(1)}, u32[]{:S(2)}, u32[]{:S(2)}) collective-permute-start(s16[1552,128]{1,0:T(8,128)(2,1)S(1)} %get-tuple-element.69), channel_id=1, source_target_pairs={{0,32},{1,33},{2,34},{3,35},{4,36},{5,37},{6,38},{7,39},{8,40},{9,... | collective-permute-start | bytes 1191944 | tf_op jit(solution)/shard_map/ppermute | solution.py:51
  70.8 27.7 %collective-permute-start.14 = (s16[392,1024]{1,0:T(8,128)(2,1)S(1)}, s16[392,1024]{1,0:T(8,128)(2,1)S(1)}, u32[]{:S(2)}, u32[]{:S(2)}) collective-permute-start(s16[392,1024]{1,0:T(8,128)(2,1)S(1)} %get-tuple-element.51), channel_id=1, source_target_pairs={{0,12},{1,13},{2,14},{3,15},{4,0},{5,1},{6,2},{7,3},{8,4},{9,5},{1... | collective-permute-start | bytes 2408456 | tf_op jit(solution)/shard_map/ppermute | solution.py:51
  74.2 24.4 %collective-permute-start.15 = (s16[392,1024]{1,0:T(8,128)(2,1)S(1)}, s16[392,1024]{1,0:T(8,128)(2,1)S(1)}, u32[]{:S(2)}, u32[]{:S(2)}) collective-permute-start(s16[392,1024]{1,0:T(8,128)(2,1)S(1)} %get-tuple-element.52), channel_id=1, source_target_pairs={{0,4},{1,5},{2,6},{3,7},{4,8},{5,9},{6,10},{7,11},{8,12},{9,13},{1... | collective-permute-start | bytes 2408456 | tf_op jit(solution)/shard_map/ppermute | solution.py:51
  74.8 28.0 %collective-permute-start.13 = (s16[392,1024]{1,0:T(8,128)(2,1)S(1)}, s16[392,1024]{1,0:T(8,128)(2,1)S(1)}, u32[]{:S(2)}, u32[]{:S(2)}) collective-permute-start(s16[392,1024]{1,0:T(8,128)(2,1)S(1)} %get-tuple-element.50), channel_id=1, source_target_pairs={{0,4},{1,5},{2,6},{3,7},{4,8},{5,9},{6,10},{7,11},{8,12},{9,13},{1... | collective-permute-start | bytes 2408456 | tf_op jit(solution)/shard_map/ppermute | solution.py:51
  77.0 25.8 %collective-permute-start.16 = (s16[392,1024]{1,0:T(8,128)(2,1)S(1)}, s16[392,1024]{1,0:T(8,128)(2,1)S(1)}, u32[]{:S(2)}, u32[]{:S(2)}) collective-permute-start(s16[392,1024]{1,0:T(8,128)(2,1)S(1)} %get-tuple-element.53), channel_id=1, source_target_pairs={{0,12},{1,13},{2,14},{3,15},{4,0},{5,1},{6,2},{7,3},{8,4},{9,5},{1... | collective-permute-start | bytes 2408456 | tf_op jit(solution)/shard_map/ppermute | solution.py:51
  80.3 9.6 %collective-permute-start.25 = (s16[1552,128]{1,0:T(8,128)(2,1)S(1)}, s16[1552,128]{1,0:T(8,128)(2,1)S(1)}, u32[]{:S(2)}, u32[]{:S(2)}) collective-permute-start(s16[1552,128]{1,0:T(8,128)(2,1)S(1)} %get-tuple-element.67), channel_id=1, source_target_pairs={{0,32},{1,33},{2,34},{3,35},{4,36},{5,37},{6,38},{7,39},{8,40},{9,... | collective-permute-start | bytes 1191944 | tf_op jit(solution)/shard_map/ppermute | solution.py:51
  89.8 7.8 %collective-permute-start.28 = (s16[1552,128]{1,0:T(8,128)(2,1)S(1)}, s16[1552,128]{1,0:T(8,128)(2,1)S(1)}, u32[]{:S(2)}, u32[]{:S(2)}) collective-permute-start(s16[1552,128]{1,0:T(8,128)(2,1)S(1)} %get-tuple-element.70), channel_id=1, source_target_pairs={{0,96},{1,97},{2,98},{3,99},{4,100},{5,101},{6,102},{7,103},{8,104... | collective-permute-start | bytes 1191944 | tf_op jit(solution)/shard_map/ppermute | solution.py:51
  98.3 12.5 %collective-permute-start.29 = (s16[200,512]{1,0:T(8,128)(2,1)S(1)}, s16[200,512]{1,0:T(8,128)(2,1)S(1)}, u32[]{:S(2)}, u32[]{:S(2)}) collective-permute-start(s16[200,512]{1,0:T(8,128)(2,1)S(1)} %get-tuple-element.72), channel_id=1, source_target_pairs={{0,1},{1,2},{2,3},{3,0},{4,5},{5,6},{6,7},{7,4},{8,9},{9,10},{10,1... | collective-permute-start | bytes 614408 | tf_op jit(solution)/shard_map/ppermute | solution.py:51
  103.1 20.3 %collective-permute-start.18 = (s16[200,1024]{1,0:T(8,128)(2,1)S(1)}, s16[200,1024]{1,0:T(8,128)(2,1)S(1)}, u32[]{:S(2)}, u32[]{:S(2)}) collective-permute-start(s16[200,1024]{1,0:T(8,128)(2,1)S(1)} %bulk_second_sum.3), channel_id=1, source_target_pairs={{0,2},{1,3},{2,0},{3,1},{4,6},{5,7},{6,4},{7,5},{8,10},{9,11},{10,... | collective-permute-start | bytes 1228808 | tf_op jit(solution)/shard_map/ppermute | solution.py:51
  107.5 15.9 %collective-permute-start.17 = (s16[200,1024]{1,0:T(8,128)(2,1)S(1)}, s16[200,1024]{1,0:T(8,128)(2,1)S(1)}, u32[]{:S(2)}, u32[]{:S(2)}) collective-permute-start(s16[200,1024]{1,0:T(8,128)(2,1)S(1)} %get-tuple-element.55), channel_id=1, source_target_pairs={{0,1},{1,2},{2,3},{3,0},{4,5},{5,6},{6,7},{7,4},{8,9},{9,10},{10,1... | collective-permute-start | bytes 1228808 | tf_op jit(solution)/shard_map/ppermute | solution.py:51
  108.2 15.2 %collective-permute-start.19 = (s16[200,1024]{1,0:T(8,128)(2,1)S(1)}, s16[200,1024]{1,0:T(8,128)(2,1)S(1)}, u32[]{:S(2)}, u32[]{:S(2)}) collective-permute-start(s16[200,1024]{1,0:T(8,128)(2,1)S(1)} %get-tuple-element.56), channel_id=1, source_target_pairs={{0,3},{1,0},{2,1},{3,2},{4,7},{5,4},{6,5},{7,6},{8,11},{9,8},{10,9... | collective-permute-start | bytes 1228808 | tf_op jit(solution)/shard_map/ppermute | solution.py:51
  110.8 9.5 %collective-permute-start.30 = (s16[200,512]{1,0:T(8,128)(2,1)S(1)}, s16[200,512]{1,0:T(8,128)(2,1)S(1)}, u32[]{:S(2)}, u32[]{:S(2)}) collective-permute-start(s16[200,512]{1,0:T(8,128)(2,1)S(1)} %get-tuple-element.73), channel_id=1, source_target_pairs={{0,2},{1,3},{2,0},{3,1},{4,6},{5,7},{6,4},{7,5},{8,10},{9,11},{10,... | collective-permute-start | bytes 614408 | tf_op jit(solution)/shard_map/ppermute | solution.py:51
  110.8 12.3 %collective-permute-start.31 = (s16[200,512]{1,0:T(8,128)(2,1)S(1)}, s16[200,512]{1,0:T(8,128)(2,1)S(1)}, u32[]{:S(2)}, u32[]{:S(2)}) collective-permute-start(s16[200,512]{1,0:T(8,128)(2,1)S(1)} %get-tuple-element.74), channel_id=1, source_target_pairs={{0,3},{1,0},{2,1},{3,2},{4,7},{5,4},{6,5},{7,6},{8,11},{9,8},{10,9... | collective-permute-start | bytes 614408 | tf_op jit(solution)/shard_map/ppermute | solution.py:51
  123.3 9.6 %collective-permute-start.32 = (s16[200,128]{1,0:T(8,128)(2,1)S(1)}, s16[200,128]{1,0:T(8,128)(2,1)S(1)}, u32[]{:S(2)}, u32[]{:S(2)}) collective-permute-start(s16[200,128]{1,0:T(8,128)(2,1)S(1)} %get-tuple-element.76), channel_id=1, source_target_pairs={{0,4},{1,5},{2,6},{3,7},{4,8},{5,9},{6,10},{7,11},{8,12},{9,13},{1... | collective-permute-start | bytes 153608 | tf_op jit(solution)/shard_map/ppermute | solution.py:51
  123.9 14.7 %collective-permute-start.20 = (s16[200,256]{1,0:T(8,128)(2,1)S(1)}, s16[200,256]{1,0:T(8,128)(2,1)S(1)}, u32[]{:S(2)}, u32[]{:S(2)}) collective-permute-start(s16[200,256]{1,0:T(8,128)(2,1)S(1)} %get-tuple-element.58), channel_id=1, source_target_pairs={{0,32},{1,33},{2,34},{3,35},{4,36},{5,37},{6,38},{7,39},{8,40},{9,... | collective-permute-start | bytes 307208 | tf_op jit(solution)/shard_map/ppermute | solution.py:51
  125.3 13.3 %collective-permute-start.21 = (s16[200,256]{1,0:T(8,128)(2,1)S(1)}, s16[200,256]{1,0:T(8,128)(2,1)S(1)}, u32[]{:S(2)}, u32[]{:S(2)}) collective-permute-start(s16[200,256]{1,0:T(8,128)(2,1)S(1)} %get-tuple-element.59), channel_id=1, source_target_pairs={{0,64},{1,65},{2,66},{3,67},{4,68},{5,69},{6,70},{7,71},{8,72},{9,... | collective-permute-start | bytes 307208 | tf_op jit(solution)/shard_map/ppermute | solution.py:51
  130.1 8.4 %collective-permute-start.22 = (s16[200,256]{1,0:T(8,128)(2,1)S(1)}, s16[200,256]{1,0:T(8,128)(2,1)S(1)}, u32[]{:S(2)}, u32[]{:S(2)}) collective-permute-start(s16[200,256]{1,0:T(8,128)(2,1)S(1)} %get-tuple-element.60), channel_id=1, source_target_pairs={{0,96},{1,97},{2,98},{3,99},{4,100},{5,101},{6,102},{7,103},{8,104... | collective-permute-start | bytes 307208 | tf_op jit(solution)/shard_map/ppermute | solution.py:51
  131.9 5.6 %collective-permute-start.33 = (s16[200,128]{1,0:T(8,128)(2,1)S(1)}, s16[200,128]{1,0:T(8,128)(2,1)S(1)}, u32[]{:S(2)}, u32[]{:S(2)}) collective-permute-start(s16[200,128]{1,0:T(8,128)(2,1)S(1)} %get-tuple-element.77), channel_id=1, source_target_pairs={{0,8},{1,9},{2,10},{3,11},{4,12},{5,13},{6,14},{7,15},{8,0},{9,1},... | collective-permute-start | bytes 153608 | tf_op jit(solution)/shard_map/ppermute | solution.py:51
  132.9 5.7 %collective-permute-start.34 = (s16[200,128]{1,0:T(8,128)(2,1)S(1)}, s16[200,128]{1,0:T(8,128)(2,1)S(1)}, u32[]{:S(2)}, u32[]{:S(2)}) collective-permute-start(s16[200,128]{1,0:T(8,128)(2,1)S(1)} %get-tuple-element.78), channel_id=1, source_target_pairs={{0,12},{1,13},{2,14},{3,15},{4,0},{5,1},{6,2},{7,3},{8,4},{9,5},{1... | collective-permute-start | bytes 153608 | tf_op jit(solution)/shard_map/ppermute | solution.py:51
  (5 other events, 46.5 us)

commit v5 on v4

--- a/solution.py
+++ b/solution.py
@@ -60,11 +60,11 @@
 
 
 def first_axis(k):
-    return lambda z, c, x, y: (z, c, x + k, y) if c == 0 else (z, c, x, y + k)
+    return lambda z, c, x, y: (z, c, x + k, y) if c == 1 else (z, c, x, y + k)
 
 
 def second_axis(k):
-    return lambda z, c, x, y: (z, c, x, y + k) if c == 0 else (z, c, x + k, y)
+    return lambda z, c, x, y: (z, c, x, y + k) if c == 1 else (z, c, x + k, y)
 
 
 def screen_body(survive, half, *rest):
@@ -109,7 +109,7 @@
         scratch_shapes=[
             pltpu.VMEM(half.shape, BF),
             pltpu.VMEM((occ, aux, ao), BF),
-            pltpu.SemaphoreType.DMA((4,)),
+            pltpu.SemaphoreType.DMA((8,)),
         ],
         compiler_params=params(50),
         cost_estimate=cost(half.size, half.size * 4),
@@ -173,7 +173,7 @@
     for x in range(RING):
         for y in range(RING):
             n = x * RING + y
-            to = jnp.where(at[1] == 0, n, y * RING + x) * high
+            to = jnp.where(at[1] == 1, n, y * RING + x) * high
             turned[pl.ds(pl.multiple_of(to, 64), high), cut] = flipped[n * high:(n + 1) * high]
 
     @pl.when(step == pl.num_programs(0) - 1)
@@ -235,7 +235,7 @@
 def bulk_body(blocks, bulk, turned, *refs):
     at = position()
     total = turned.shape[0] // RING
-    own = jnp.where(at[1] == 0, at[2], at[3])
+    own = jnp.where(at[1] == 1, at[2], at[3])
     outs = refs[len(refs) - len(blocks):]
     arrived = iter(refs)
     wide = bulk.shape[1] // 2
@@ -337,7 +337,7 @@
     at = position()
     high = kept.shape[0]
     total, step = own.shape[0] // RING, own.shape[1]
-    h = jnp.where(at[1] == 0, at[3], at[2])
+    h = jnp.where(at[1] == 1, at[3], at[2])
     for k in range(RING):
         row = lax.rem(h + k, RING) * high
         out = kept if k == 0 else outs[k - 1]
@@ -365,7 +365,7 @@
 def bulk_second_body(steps, own, a, b, d, e, after, *outs):
     at = position()
     high = own.shape[0] // RING
-    h = jnp.where(at[1] == 0, at[3], at[2])
+    h = jnp.where(at[1] == 1, at[3], at[2])
     half = own.shape[0] // 2
     step = 256
     for k, out in zip(steps, outs):
@@ -407,7 +407,7 @@
 def third_body(by_z, own, a, b, d, after, *outs):
     at = position()
     high, step = outs[0].shape
-    start = at[0] if by_z else jnp.where(at[1] == 0, at[2], at[3])
+    start = at[0] if by_z else jnp.where(at[1] == 1, at[2], at[3])
     for k in range(RING):
         cut = pl.ds(pl.multiple_of(lax.rem(start + k, RING) * step, 128), step)
         write(outs[k], 0, gathered(own, (a, b, d), (0, 0, high), high, 0, cut))

time: 140 us -> 139 us (level)
  no operation moved by 1% of the time
where the time goes in v5:
time: 139 us
  waiting for transfers between devices  75.4 us (54%)
  starting transfers between devices  44 us (32%)
  Pallas kernels  18.9 us (14%)
    ppermute x35, waiting for transfers between devices, send(): return lax.ppermute(v, AXES, moves(shift))  75.4 us
    ppermute x35, starting transfers between devices, send(): return lax.ppermute(v, AXES, moves(shift))  44 us
    pallas_call x3, Pallas kernels, bulk_k(): pl.pallas_call(functools.partial(bulk_body, blocks), out_shape=[jax.Shape...  4.83 us
    pallas_call x1, Pallas kernels, fit(): pl.pallas_call(fit_body, grid=(steps,), out_shape=[jax.ShapeDtypeStruct(*...  3.76 us
    pallas_call x2, Pallas kernels, rest_k(): pl.pallas_call(functools.partial(rest_body, steps, cut), out_shape=[jax.S...  3.17 us
    pallas_call x1, Pallas kernels, screen(): pl.pallas_call(screen_body, out_shape=[out] * RING, in_specs=[scalars(),...  3.03 us
  transfers between devices with their start and end apart: 35, of which 15 were waited for; matrix products, arithmetic and copies ran while one was open for 0% of the time, Pallas kernels for 8%

profile of v5, /device:TPU:0, one launch (start us, length us, event | category | flops | bytes accessed | tf_op | source)
XLA Modules:
  0.0 139.2 jit_solution(18290050026301746981)
XLA Ops:
  0.7 3.0 %screen.1 = (bf16[6,16,3072]{2,1,0:T(8,128)(2,1)S(1)}, bf16[6,16,3072]{2,1,0:T(8,128)(2,1)S(1)}, bf16[6,16,3072]{2,1,0:T(8,128)(2,1)S(1)}, bf16[6,16,3072]{2,1,0:T(8,128)(2,1)S(1)}) custom-call(s32[1,1,24]{2,1,0:T(1,128)S(1)} %copy-done.1, bf16[16,24,3072]{2,1,0:T(8,128)(2,1)} %half.1), custom_call_target="tpu_custom_call" | custom-call | flops 1179648 | bytes 4718592 | tf_op jit(solution)/shard_map/screen/pallas_call | solution.py:104
  3.7 2.1 %collective-permute-start.1 = (bf16[6,16,3072]{2,1,0:T(8,128)(2,1)S(1)}, bf16[6,16,3072]{2,1,0:T(8,128)(2,1)S(1)}, u32[]{:S(2)}, u32[]{:S(2)}) collective-permute-start(bf16[6,16,3072]{2,1,0:T(8,128)(2,1)S(1)} %get-tuple-element.43), channel_id=1, source_target_pairs={{0,32},{1,33},{2,34},{3,35},{4,36},{5,37},{6,38},{7,39},{8,40},{9,... | collective-permute-start | bytes 1769480 | tf_op jit(solution)/shard_map/ppermute | solution.py:51
  5.8 3.6 %collective-permute-start.3 = (bf16[6,16,3072]{2,1,0:T(8,128)(2,1)S(1)}, bf16[6,16,3072]{2,1,0:T(8,128)(2,1)S(1)}, u32[]{:S(2)}, u32[]{:S(2)}) collective-permute-start(bf16[6,16,3072]{2,1,0:T(8,128)(2,1)S(1)} %get-tuple-element.44), channel_id=1, source_target_pairs={{0,64},{1,65},{2,66},{3,67},{4,68},{5,69},{6,70},{7,71},{8,72},{9,... | collective-permute-start | bytes 1769480 | tf_op jit(solution)/shard_map/ppermute | solution.py:51
  10.4 10.9 %collective-permute-done.1.refs_2_ = bf16[6,16,3072]{2,1,0:T(8,128)(2,1)S(1)} collective-permute-done((bf16[6,16,3072]{2,1,0:T(8,128)(2,1)S(1)}, bf16[6,16,3072]{2,1,0:T(8,128)(2,1)S(1)}, u32[]{:S(2)}, u32[]{:S(2)}) %collective-permute-start.1) | collective-permute-done | bytes 589856 | tf_op jit(solution)/shard_map/ppermute | solution.py:51
  21.2 13.8 %collective-permute-done.3.refs_4_ = bf16[6,16,3072]{2,1,0:T(8,128)(2,1)S(1)} collective-permute-done((bf16[6,16,3072]{2,1,0:T(8,128)(2,1)S(1)}, bf16[6,16,3072]{2,1,0:T(8,128)(2,1)S(1)}, u32[]{:S(2)}, u32[]{:S(2)}) %collective-permute-start.3) | collective-permute-done | bytes 589856 | tf_op jit(solution)/shard_map/ppermute | solution.py:51
  35.7 2.2 %collective-permute-done.7 = bf16[16,128]{1,0:T(8,128)(2,1)S(1)} collective-permute-done((bf16[16,128]{1,0:T(8,128)(2,1)S(1)}, bf16[16,128]{1,0:T(8,128)(2,1)S(1)}, u32[]{:S(2)}, u32[]{:S(2)}) %collective-permute-start.7) | collective-permute-done | bytes 4128 | tf_op jit(solution)/shard_map/ppermute | solution.py:51
  39.2 2.3 %collective-permute-done.10.refs_3_ = bf16[32,128]{1,0:T(8,128)(2,1)S(1)} collective-permute-done((bf16[32,128]{1,0:T(8,128)(2,1)S(1)}, bf16[32,128]{1,0:T(8,128)(2,1)S(1)}, u32[]{:S(2)}, u32[]{:S(2)}) %collective-permute-start.10) | collective-permute-done | bytes 8224 | tf_op jit(solution)/shard_map/ppermute | solution.py:51
  42.0 4.5 %collective-permute-done.8.refs_1_ = bf16[32,128]{1,0:T(8,128)(2,1)S(1)} collective-permute-done((bf16[32,128]{1,0:T(8,128)(2,1)S(1)}, bf16[32,128]{1,0:T(8,128)(2,1)S(1)}, u32[]{:S(2)}, u32[]{:S(2)}) %collective-permute-start.8) | collective-permute-done | bytes 8224 | tf_op jit(solution)/shard_map/ppermute | solution.py:51
  46.9 4.7 %collective-permute-done.9.refs_2_ = bf16[32,128]{1,0:T(8,128)(2,1)S(1)} collective-permute-done((bf16[32,128]{1,0:T(8,128)(2,1)S(1)}, bf16[32,128]{1,0:T(8,128)(2,1)S(1)}, u32[]{:S(2)}, u32[]{:S(2)}) %collective-permute-start.9) | collective-permute-done | bytes 8224 | tf_op jit(solution)/shard_map/ppermute | solution.py:51
  51.8 3.8 %fit.1 = (bf16[768,1024]{1,0:T(8,128)(2,1)S(1)}, bf16[768,512]{1,0:T(8,128)(2,1)S(1)}, bf16[3072,768]{1,0:T(8,128)(2,1)S(1)}, s16[392,1024]{1,0:T(8,128)(2,1)S(1)}, s16[392,1024]{1,0:T(8,128)(2,1)S(1)}) custom-call(bf16[6,16,3072]{2,1,0:T(8,128)(2,1)S(1)} %get-tuple-element.42.refs_0_, bf16[6,16,3072]{2,1,0:T(8,128)(2,1)S(1)} %collective-permute-done.refs_1_, ...), custom_call_target="tpu_custom_call" | custom-call | flops 2415919104 | bytes 14155776 | tf_op jit(solution)/shard_map/fit/pallas_call | solution.py:189
  55.6 1.6 %collective-permute-start.11 = (s16[392,1024]{1,0:T(8,128)(2,1)S(1)}, s16[392,1024]{1,0:T(8,128)(2,1)S(1)}, u32[]{:S(2)}, u32[]{:S(2)}) collective-permute-start(s16[392,1024]{1,0:T(8,128)(2,1)S(1)} %get-tuple-element.48), channel_id=1, source_target_pairs={{0,1},{1,2},{2,3},{3,0},{4,5},{5,6},{6,7},{7,4},{8,9},{9,10},{10,1... | collective-permute-start | bytes 2408456 | tf_op jit(solution)/shard_map/ppermute | solution.py:51
  57.2 1.7 %collective-permute-start.12 = (s16[392,1024]{1,0:T(8,128)(2,1)S(1)}, s16[392,1024]{1,0:T(8,128)(2,1)S(1)}, u32[]{:S(2)}, u32[]{:S(2)}) collective-permute-start(s16[392,1024]{1,0:T(8,128)(2,1)S(1)} %get-tuple-element.49), channel_id=1, source_target_pairs={{0,3},{1,0},{2,1},{3,2},{4,7},{5,4},{6,5},{7,6},{8,11},{9,8},{10,9... | collective-permute-start | bytes 2408456 | tf_op jit(solution)/shard_map/ppermute | solution.py:51
  60.5 3.2 %collective-permute-start.24 = (s16[1552,128]{1,0:T(8,128)(2,1)S(1)}, s16[1552,128]{1,0:T(8,128)(2,1)S(1)}, u32[]{:S(2)}, u32[]{:S(2)}) collective-permute-start(s16[1552,128]{1,0:T(8,128)(2,1)S(1)} %get-tuple-element.66), channel_id=1, source_target_pairs={{0,96},{1,97},{2,98},{3,99},{4,100},{5,101},{6,102},{7,103},{8,104... | collective-permute-start | bytes 1191944 | tf_op jit(solution)/shard_map/ppermute | solution.py:51
  65.5 3.5 %collective-permute-done.11.refs_0_ = s16[392,1024]{1,0:T(8,128)(2,1)S(1)} collective-permute-done((s16[392,1024]{1,0:T(8,128)(2,1)S(1)}, s16[392,1024]{1,0:T(8,128)(2,1)S(1)}, u32[]{:S(2)}, u32[]{:S(2)}) %collective-permute-start.11) | collective-permute-done | bytes 802848 | tf_op jit(solution)/shard_map/ppermute | solution.py:51
  69.0 1.7 %shard_map.39 = (s16[392,1024]{1,0:T(8,128)(2,1)S(1)}, s16[392,1024]{1,0:T(8,128)(2,1)S(1)}) custom-call(bf16[768,1024]{1,0:T(8,128)(2,1)S(1)} %get-tuple-element.46.bulk, bf16[3072,768]{1,0:T(8,128)(2,1)S(1)} %get-tuple-element.47.turned), custom_call_target="tpu_custom_call" | custom-call | flops 1207959552 | bytes 1572864 | tf_op jit(solution)/shard_map/pallas_call | solution.py:259
  70.8 1.9 %collective-permute-start.14 = (s16[392,1024]{1,0:T(8,128)(2,1)S(1)}, s16[392,1024]{1,0:T(8,128)(2,1)S(1)}, u32[]{:S(2)}, u32[]{:S(2)}) collective-permute-start(s16[392,1024]{1,0:T(8,128)(2,1)S(1)} %get-tuple-element.51), channel_id=1, source_target_pairs={{0,3},{1,0},{2,1},{3,2},{4,7},{5,4},{6,5},{7,6},{8,11},{9,8},{10,9... | collective-permute-start | bytes 2408456 | tf_op jit(solution)/shard_map/ppermute | solution.py:51
  72.6 1.7 %shard_map.38 = (s16[392,1024]{1,0:T(8,128)(2,1)S(1)}, s16[392,1024]{1,0:T(8,128)(2,1)S(1)}) custom-call(bf16[768,1024]{1,0:T(8,128)(2,1)S(1)} %get-tuple-element.46.bulk, bf16[3072,768]{1,0:T(8,128)(2,1)S(1)} %get-tuple-element.47.turned, s16[392,1024]{1,0:T(8,128)(2,1)S(1)} %collective-permute-done.11.refs_0_, ...), custom_call_target="tpu_custom_call" | custom-call | flops 1207959552 | bytes 1572864 | tf_op jit(solution)/shard_map/pallas_call | solution.py:259
  75.1 1.7 %collective-permute-done.26.b = s16[1552,128]{1,0:T(8,128)(2,1)S(1)} collective-permute-done((s16[1552,128]{1,0:T(8,128)(2,1)S(1)}, s16[1552,128]{1,0:T(8,128)(2,1)S(1)}, u32[]{:S(2)}, u32[]{:S(2)}) %collective-permute-start.26) | collective-permute-done | bytes 397344 | tf_op jit(solution)/shard_map/ppermute | solution.py:51
  76.8 3.0 %collective-permute-start.16 = (s16[392,1024]{1,0:T(8,128)(2,1)S(1)}, s16[392,1024]{1,0:T(8,128)(2,1)S(1)}, u32[]{:S(2)}, u32[]{:S(2)}) collective-permute-start(s16[392,1024]{1,0:T(8,128)(2,1)S(1)} %get-tuple-element.53), channel_id=1, source_target_pairs={{0,3},{1,0},{2,1},{3,2},{4,7},{5,4},{6,5},{7,6},{8,11},{9,8},{10,9... | collective-permute-start | bytes 2408456 | tf_op jit(solution)/shard_map/ppermute | solution.py:51
  80.6 9.2 %collective-permute-done.25.a = s16[1552,128]{1,0:T(8,128)(2,1)S(1)} collective-permute-done((s16[1552,128]{1,0:T(8,128)(2,1)S(1)}, s16[1552,128]{1,0:T(8,128)(2,1)S(1)}, u32[]{:S(2)}, u32[]{:S(2)}) %collective-permute-start.25) | collective-permute-done | bytes 397344 | tf_op jit(solution)/shard_map/ppermute | solution.py:51
  89.8 2.0 %collective-permute-start.28 = (s16[1552,128]{1,0:T(8,128)(2,1)S(1)}, s16[1552,128]{1,0:T(8,128)(2,1)S(1)}, u32[]{:S(2)}, u32[]{:S(2)}) collective-permute-start(s16[1552,128]{1,0:T(8,128)(2,1)S(1)} %get-tuple-element.70), channel_id=1, source_target_pairs={{0,96},{1,97},{2,98},{3,99},{4,100},{5,101},{6,102},{7,103},{8,104... | collective-permute-start | bytes 1191944 | tf_op jit(solution)/shard_map/ppermute | solution.py:51
  93.2 4.4 %collective-permute-done.28.e = s16[1552,128]{1,0:T(8,128)(2,1)S(1)} collective-permute-done((s16[1552,128]{1,0:T(8,128)(2,1)S(1)}, s16[1552,128]{1,0:T(8,128)(2,1)S(1)}, u32[]{:S(2)}, u32[]{:S(2)}) %collective-permute-start.28) | collective-permute-done | bytes 397344 | tf_op jit(solution)/shard_map/ppermute | solution.py:51
  98.7 4.5 %collective-permute-done.13.a = s16[392,1024]{1,0:T(8,128)(2,1)S(1)} collective-permute-done((s16[392,1024]{1,0:T(8,128)(2,1)S(1)}, s16[392,1024]{1,0:T(8,128)(2,1)S(1)}, u32[]{:S(2)}, u32[]{:S(2)}) %collective-permute-start.13) | collective-permute-done | bytes 802848 | tf_op jit(solution)/shard_map/ppermute | solution.py:51
  103.6 3.2 %collective-permute-start.18 = (s16[200,1024]{1,0:T(8,128)(2,1)S(1)}, s16[200,1024]{1,0:T(8,128)(2,1)S(1)}, u32[]{:S(2)}, u32[]{:S(2)}) collective-permute-start(s16[200,1024]{1,0:T(8,128)(2,1)S(1)} %bulk_second_sum.3), channel_id=1, source_target_pairs={{0,8},{1,9},{2,10},{3,11},{4,12},{5,13},{6,14},{7,15},{8,0},{9,1},... | collective-permute-start | bytes 1228808 | tf_op jit(solution)/shard_map/ppermute | solution.py:51
  108.4 2.6 %collective-permute-start.19 = (s16[200,1024]{1,0:T(8,128)(2,1)S(1)}, s16[200,1024]{1,0:T(8,128)(2,1)S(1)}, u32[]{:S(2)}, u32[]{:S(2)}) collective-permute-start(s16[200,1024]{1,0:T(8,128)(2,1)S(1)} %get-tuple-element.56), channel_id=1, source_target_pairs={{0,12},{1,13},{2,14},{3,15},{4,0},{5,1},{6,2},{7,3},{8,4},{9,5},{1... | collective-permute-start | bytes 1228808 | tf_op jit(solution)/shard_map/ppermute | solution.py:51
  111.0 2.1 %collective-permute-start.31 = (s16[200,512]{1,0:T(8,128)(2,1)S(1)}, s16[200,512]{1,0:T(8,128)(2,1)S(1)}, u32[]{:S(2)}, u32[]{:S(2)}) collective-permute-start(s16[200,512]{1,0:T(8,128)(2,1)S(1)} %get-tuple-element.74), channel_id=1, source_target_pairs={{0,12},{1,13},{2,14},{3,15},{4,0},{5,1},{6,2},{7,3},{8,4},{9,5},{1... | collective-permute-start | bytes 614408 | tf_op jit(solution)/shard_map/ppermute | solution.py:51
  113.1 7.7 %collective-permute-done.30.b = s16[200,512]{1,0:T(8,128)(2,1)S(1)} collective-permute-done((s16[200,512]{1,0:T(8,128)(2,1)S(1)}, s16[200,512]{1,0:T(8,128)(2,1)S(1)}, u32[]{:S(2)}, u32[]{:S(2)}) %collective-permute-start.30) | collective-permute-done | bytes 204832 | tf_op jit(solution)/shard_map/ppermute | solution.py:51
  120.8 2.4 %collective-permute-done.31.d = s16[200,512]{1,0:T(8,128)(2,1)S(1)} collective-permute-done((s16[200,512]{1,0:T(8,128)(2,1)S(1)}, s16[200,512]{1,0:T(8,128)(2,1)S(1)}, u32[]{:S(2)}, u32[]{:S(2)}) %collective-permute-start.31) | collective-permute-done | bytes 204832 | tf_op jit(solution)/shard_map/ppermute | solution.py:51
  125.5 4.5 %collective-permute-start.21 = (s16[200,256]{1,0:T(8,128)(2,1)S(1)}, s16[200,256]{1,0:T(8,128)(2,1)S(1)}, u32[]{:S(2)}, u32[]{:S(2)}) collective-permute-start(s16[200,256]{1,0:T(8,128)(2,1)S(1)} %get-tuple-element.59), channel_id=1, source_target_pairs={{0,64},{1,65},{2,66},{3,67},{4,68},{5,69},{6,70},{7,71},{8,72},{9,... | collective-permute-start | bytes 307208 | tf_op jit(solution)/shard_map/ppermute | solution.py:51
  130.0 1.7 %collective-permute-start.22 = (s16[200,256]{1,0:T(8,128)(2,1)S(1)}, s16[200,256]{1,0:T(8,128)(2,1)S(1)}, u32[]{:S(2)}, u32[]{:S(2)}) collective-permute-start(s16[200,256]{1,0:T(8,128)(2,1)S(1)} %get-tuple-element.60), channel_id=1, source_target_pairs={{0,96},{1,97},{2,98},{3,99},{4,100},{5,101},{6,102},{7,103},{8,104... | collective-permute-start | bytes 307208 | tf_op jit(solution)/shard_map/ppermute | solution.py:51
  132.7 2.2 %collective-permute-start.34 = (s16[200,128]{1,0:T(8,128)(2,1)S(1)}, s16[200,128]{1,0:T(8,128)(2,1)S(1)}, u32[]{:S(2)}, u32[]{:S(2)}) collective-permute-start(s16[200,128]{1,0:T(8,128)(2,1)S(1)} %get-tuple-element.78), channel_id=1, source_target_pairs={{0,3},{1,0},{2,1},{3,2},{4,7},{5,4},{6,5},{7,6},{8,11},{9,8},{10,9... | collective-permute-start | bytes 153608 | tf_op jit(solution)/shard_map/ppermute | solution.py:51
  134.9 2.4 %collective-permute-done.33.rb = s16[200,128]{1,0:T(8,128)(2,1)S(1)} collective-permute-done((s16[200,128]{1,0:T(8,128)(2,1)S(1)}, s16[200,128]{1,0:T(8,128)(2,1)S(1)}, u32[]{:S(2)}, u32[]{:S(2)}) %collective-permute-start.33) | collective-permute-done | bytes 51232 | tf_op jit(solution)/shard_map/ppermute | solution.py:51
  (62 shorter events, 19.0 us)
Async XLA Ops:
  3.7 17.5 %collective-permute-start.1 = (bf16[6,16,3072]{2,1,0:T(8,128)(2,1)S(1)}, bf16[6,16,3072]{2,1,0:T(8,128)(2,1)S(1)}, u32[]{:S(2)}, u32[]{:S(2)}) collective-permute-start(bf16[6,16,3072]{2,1,0:T(8,128)(2,1)S(1)} %get-tuple-element.43), channel_id=1, source_target_pairs={{0,32},{1,33},{2,34},{3,35},{4,36},{5,37},{6,38},{7,39},{8,40},{9,... | collective-permute-start | bytes 1769480 | tf_op jit(solution)/shard_map/ppermute | solution.py:51
  5.8 29.3 %collective-permute-start.3 = (bf16[6,16,3072]{2,1,0:T(8,128)(2,1)S(1)}, bf16[6,16,3072]{2,1,0:T(8,128)(2,1)S(1)}, u32[]{:S(2)}, u32[]{:S(2)}) collective-permute-start(bf16[6,16,3072]{2,1,0:T(8,128)(2,1)S(1)} %get-tuple-element.44), channel_id=1, source_target_pairs={{0,64},{1,65},{2,66},{3,67},{4,68},{5,69},{6,70},{7,71},{8,72},{9,... | collective-permute-start | bytes 1769480 | tf_op jit(solution)/shard_map/ppermute | solution.py:51
  9.4 25.7 %collective-permute-start.5 = (bf16[6,16,3072]{2,1,0:T(8,128)(2,1)S(1)}, bf16[6,16,3072]{2,1,0:T(8,128)(2,1)S(1)}, u32[]{:S(2)}, u32[]{:S(2)}) collective-permute-start(bf16[6,16,3072]{2,1,0:T(8,128)(2,1)S(1)} %get-tuple-element.45), channel_id=1, source_target_pairs={{0,96},{1,97},{2,98},{3,99},{4,100},{5,101},{6,102},{7,103},{8,104... | collective-permute-start | bytes 1769480 | tf_op jit(solution)/shard_map/ppermute | solution.py:51
  10.4 41.4 %collective-permute-start = (bf16[6,16,3072]{2,1,0:T(8,128)(2,1)S(1)}, bf16[6,16,3072]{2,1,0:T(8,128)(2,1)S(1)}, u32[]{:S(2)}, u32[]{:S(2)}) collective-permute-start(bf16[6,16,3072]{2,1,0:T(8,128)(2,1)S(1)} %get-tuple-element.42.refs_0_), channel_id=1, source_target_pairs={{0,16},{1,17},{2,18},{3,19},{4,20},{5,21},{6,22},{7,23},{8,24},{9,... | collective-permute-start | bytes 1769480 | tf_op jit(solution)/shard_map/ppermute | solution.py:51
  21.2 30.5 %collective-permute-start.2 = (bf16[6,16,3072]{2,1,0:T(8,128)(2,1)S(1)}, bf16[6,16,3072]{2,1,0:T(8,128)(2,1)S(1)}, u32[]{:S(2)}, u32[]{:S(2)}) collective-permute-start(bf16[6,16,3072]{2,1,0:T(8,128)(2,1)S(1)} %collective-permute-done.1.refs_2_), channel_id=1, source_target_pairs={{0,16},{1,17},{2,18},{3,19},{4,20},{5,21},{6,22},{7,23},{8,24},{9,... | collective-permute-start | bytes 1769480 | tf_op jit(solution)/shard_map/ppermute | solution.py:51
  35.1 16.7 %collective-permute-start.4 = (bf16[6,16,3072]{2,1,0:T(8,128)(2,1)S(1)}, bf16[6,16,3072]{2,1,0:T(8,128)(2,1)S(1)}, u32[]{:S(2)}, u32[]{:S(2)}) collective-permute-start(bf16[6,16,3072]{2,1,0:T(8,128)(2,1)S(1)} %collective-permute-done.3.refs_4_), channel_id=1, source_target_pairs={{0,16},{1,17},{2,18},{3,19},{4,20},{5,21},{6,22},{7,23},{8,24},{9,... | collective-permute-start | bytes 1769480 | tf_op jit(solution)/shard_map/ppermute | solution.py:51
  35.1 16.7 %collective-permute-start.6 = (bf16[6,16,3072]{2,1,0:T(8,128)(2,1)S(1)}, bf16[6,16,3072]{2,1,0:T(8,128)(2,1)S(1)}, u32[]{:S(2)}, u32[]{:S(2)}) collective-permute-start(bf16[6,16,3072]{2,1,0:T(8,128)(2,1)S(1)} %collective-permute-done.5.refs_6_), channel_id=1, source_target_pairs={{0,16},{1,17},{2,18},{3,19},{4,20},{5,21},{6,22},{7,23},{8,24},{9,... | collective-permute-start | bytes 1769480 | tf_op jit(solution)/shard_map/ppermute | solution.py:51
  46.4 5.2 %collective-permute-start.9 = (bf16[32,128]{1,0:T(8,128)(2,1)S(1)}, bf16[32,128]{1,0:T(8,128)(2,1)S(1)}, u32[]{:S(2)}, u32[]{:S(2)}) collective-permute-start(bf16[32,128]{1,0:T(8,128)(2,1)S(1)} %constant_dynamic-update-slice_fusion.refs_0_), channel_id=1, source_target_pairs={{0,64},{1,65},{2,66},{3,67},{4,68},{5,69},{6,70},{7,71},{8,72},{9,... | collective-permute-start | bytes 24584 | tf_op jit(solution)/shard_map/ppermute | solution.py:51
  55.6 13.4 %collective-permute-start.11 = (s16[392,1024]{1,0:T(8,128)(2,1)S(1)}, s16[392,1024]{1,0:T(8,128)(2,1)S(1)}, u32[]{:S(2)}, u32[]{:S(2)}) collective-permute-start(s16[392,1024]{1,0:T(8,128)(2,1)S(1)} %get-tuple-element.48), channel_id=1, source_target_pairs={{0,1},{1,2},{2,3},{3,0},{4,5},{5,6},{6,7},{7,4},{8,9},{9,10},{10,1... | collective-permute-start | bytes 2408456 | tf_op jit(solution)/shard_map/ppermute | solution.py:51
  57.2 13.5 %collective-permute-start.12 = (s16[392,1024]{1,0:T(8,128)(2,1)S(1)}, s16[392,1024]{1,0:T(8,128)(2,1)S(1)}, u32[]{:S(2)}, u32[]{:S(2)}) collective-permute-start(s16[392,1024]{1,0:T(8,128)(2,1)S(1)} %get-tuple-element.49), channel_id=1, source_target_pairs={{0,3},{1,0},{2,1},{3,2},{4,7},{5,4},{6,5},{7,6},{8,11},{9,8},{10,9... | collective-permute-start | bytes 2408456 | tf_op jit(solution)/shard_map/ppermute | solution.py:51
  60.5 13.9 %collective-permute-start.23 = (s16[1552,128]{1,0:T(8,128)(2,1)S(1)}, s16[1552,128]{1,0:T(8,128)(2,1)S(1)}, u32[]{:S(2)}, u32[]{:S(2)}) collective-permute-start(s16[1552,128]{1,0:T(8,128)(2,1)S(1)} %get-tuple-element.64), channel_id=1, source_target_pairs={{0,32},{1,33},{2,34},{3,35},{4,36},{5,37},{6,38},{7,39},{8,40},{9,... | collective-permute-start | bytes 1191944 | tf_op jit(solution)/shard_map/ppermute | solution.py:51
  60.5 14.1 %collective-permute-start.24 = (s16[1552,128]{1,0:T(8,128)(2,1)S(1)}, s16[1552,128]{1,0:T(8,128)(2,1)S(1)}, u32[]{:S(2)}, u32[]{:S(2)}) collective-permute-start(s16[1552,128]{1,0:T(8,128)(2,1)S(1)} %get-tuple-element.66), channel_id=1, source_target_pairs={{0,96},{1,97},{2,98},{3,99},{4,100},{5,101},{6,102},{7,103},{8,104... | collective-permute-start | bytes 1191944 | tf_op jit(solution)/shard_map/ppermute | solution.py:51
  65.4 11.4 %collective-permute-start.26 = (s16[1552,128]{1,0:T(8,128)(2,1)S(1)}, s16[1552,128]{1,0:T(8,128)(2,1)S(1)}, u32[]{:S(2)}, u32[]{:S(2)}) collective-permute-start(s16[1552,128]{1,0:T(8,128)(2,1)S(1)} %get-tuple-element.68), channel_id=1, source_target_pairs={{0,96},{1,97},{2,98},{3,99},{4,100},{5,101},{6,102},{7,103},{8,104... | collective-permute-start | bytes 1191944 | tf_op jit(solution)/shard_map/ppermute | solution.py:51
  69.0 11.3 %collective-permute-start.27 = (s16[1552,128]{1,0:T(8,128)(2,1)S(1)}, s16[1552,128]{1,0:T(8,128)(2,1)S(1)}, u32[]{:S(2)}, u32[]{:S(2)}) collective-permute-start(s16[1552,128]{1,0:T(8,128)(2,1)S(1)} %get-tuple-element.69), channel_id=1, source_target_pairs={{0,32},{1,33},{2,34},{3,35},{4,36},{5,37},{6,38},{7,39},{8,40},{9,... | collective-permute-start | bytes 1191944 | tf_op jit(solution)/shard_map/ppermute | solution.py:51
  70.8 27.9 %collective-permute-start.14 = (s16[392,1024]{1,0:T(8,128)(2,1)S(1)}, s16[392,1024]{1,0:T(8,128)(2,1)S(1)}, u32[]{:S(2)}, u32[]{:S(2)}) collective-permute-start(s16[392,1024]{1,0:T(8,128)(2,1)S(1)} %get-tuple-element.51), channel_id=1, source_target_pairs={{0,3},{1,0},{2,1},{3,2},{4,7},{5,4},{6,5},{7,6},{8,11},{9,8},{10,9... | collective-permute-start | bytes 2408456 | tf_op jit(solution)/shard_map/ppermute | solution.py:51
  74.4 24.3 %collective-permute-start.15 = (s16[392,1024]{1,0:T(8,128)(2,1)S(1)}, s16[392,1024]{1,0:T(8,128)(2,1)S(1)}, u32[]{:S(2)}, u32[]{:S(2)}) collective-permute-start(s16[392,1024]{1,0:T(8,128)(2,1)S(1)} %get-tuple-element.52), channel_id=1, source_target_pairs={{0,1},{1,2},{2,3},{3,0},{4,5},{5,6},{6,7},{7,4},{8,9},{9,10},{10,1... | collective-permute-start | bytes 2408456 | tf_op jit(solution)/shard_map/ppermute | solution.py:51
  74.7 28.5 %collective-permute-start.13 = (s16[392,1024]{1,0:T(8,128)(2,1)S(1)}, s16[392,1024]{1,0:T(8,128)(2,1)S(1)}, u32[]{:S(2)}, u32[]{:S(2)}) collective-permute-start(s16[392,1024]{1,0:T(8,128)(2,1)S(1)} %get-tuple-element.50), channel_id=1, source_target_pairs={{0,1},{1,2},{2,3},{3,0},{4,5},{5,6},{6,7},{7,4},{8,9},{9,10},{10,1... | collective-permute-start | bytes 2408456 | tf_op jit(solution)/shard_map/ppermute | solution.py:51
  76.8 26.4 %collective-permute-start.16 = (s16[392,1024]{1,0:T(8,128)(2,1)S(1)}, s16[392,1024]{1,0:T(8,128)(2,1)S(1)}, u32[]{:S(2)}, u32[]{:S(2)}) collective-permute-start(s16[392,1024]{1,0:T(8,128)(2,1)S(1)} %get-tuple-element.53), channel_id=1, source_target_pairs={{0,3},{1,0},{2,1},{3,2},{4,7},{5,4},{6,5},{7,6},{8,11},{9,8},{10,9... | collective-permute-start | bytes 2408456 | tf_op jit(solution)/shard_map/ppermute | solution.py:51
  80.3 9.6 %collective-permute-start.25 = (s16[1552,128]{1,0:T(8,128)(2,1)S(1)}, s16[1552,128]{1,0:T(8,128)(2,1)S(1)}, u32[]{:S(2)}, u32[]{:S(2)}) collective-permute-start(s16[1552,128]{1,0:T(8,128)(2,1)S(1)} %get-tuple-element.67), channel_id=1, source_target_pairs={{0,32},{1,33},{2,34},{3,35},{4,36},{5,37},{6,38},{7,39},{8,40},{9,... | collective-permute-start | bytes 1191944 | tf_op jit(solution)/shard_map/ppermute | solution.py:51
  89.8 7.8 %collective-permute-start.28 = (s16[1552,128]{1,0:T(8,128)(2,1)S(1)}, s16[1552,128]{1,0:T(8,128)(2,1)S(1)}, u32[]{:S(2)}, u32[]{:S(2)}) collective-permute-start(s16[1552,128]{1,0:T(8,128)(2,1)S(1)} %get-tuple-element.70), channel_id=1, source_target_pairs={{0,96},{1,97},{2,98},{3,99},{4,100},{5,101},{6,102},{7,103},{8,104... | collective-permute-start | bytes 1191944 | tf_op jit(solution)/shard_map/ppermute | solution.py:51
  98.3 12.7 %collective-permute-start.29 = (s16[200,512]{1,0:T(8,128)(2,1)S(1)}, s16[200,512]{1,0:T(8,128)(2,1)S(1)}, u32[]{:S(2)}, u32[]{:S(2)}) collective-permute-start(s16[200,512]{1,0:T(8,128)(2,1)S(1)} %get-tuple-element.72), channel_id=1, source_target_pairs={{0,4},{1,5},{2,6},{3,7},{4,8},{5,9},{6,10},{7,11},{8,12},{9,13},{1... | collective-permute-start | bytes 614408 | tf_op jit(solution)/shard_map/ppermute | solution.py:51
  103.6 20.0 %collective-permute-start.18 = (s16[200,1024]{1,0:T(8,128)(2,1)S(1)}, s16[200,1024]{1,0:T(8,128)(2,1)S(1)}, u32[]{:S(2)}, u32[]{:S(2)}) collective-permute-start(s16[200,1024]{1,0:T(8,128)(2,1)S(1)} %bulk_second_sum.3), channel_id=1, source_target_pairs={{0,8},{1,9},{2,10},{3,11},{4,12},{5,13},{6,14},{7,15},{8,0},{9,1},... | collective-permute-start | bytes 1228808 | tf_op jit(solution)/shard_map/ppermute | solution.py:51
  107.7 15.8 %collective-permute-start.17 = (s16[200,1024]{1,0:T(8,128)(2,1)S(1)}, s16[200,1024]{1,0:T(8,128)(2,1)S(1)}, u32[]{:S(2)}, u32[]{:S(2)}) collective-permute-start(s16[200,1024]{1,0:T(8,128)(2,1)S(1)} %get-tuple-element.55), channel_id=1, source_target_pairs={{0,4},{1,5},{2,6},{3,7},{4,8},{5,9},{6,10},{7,11},{8,12},{9,13},{1... | collective-permute-start | bytes 1228808 | tf_op jit(solution)/shard_map/ppermute | solution.py:51
  108.4 15.2 %collective-permute-start.19 = (s16[200,1024]{1,0:T(8,128)(2,1)S(1)}, s16[200,1024]{1,0:T(8,128)(2,1)S(1)}, u32[]{:S(2)}, u32[]{:S(2)}) collective-permute-start(s16[200,1024]{1,0:T(8,128)(2,1)S(1)} %get-tuple-element.56), channel_id=1, source_target_pairs={{0,12},{1,13},{2,14},{3,15},{4,0},{5,1},{6,2},{7,3},{8,4},{9,5},{1... | collective-permute-start | bytes 1228808 | tf_op jit(solution)/shard_map/ppermute | solution.py:51
  111.0 9.7 %collective-permute-start.30 = (s16[200,512]{1,0:T(8,128)(2,1)S(1)}, s16[200,512]{1,0:T(8,128)(2,1)S(1)}, u32[]{:S(2)}, u32[]{:S(2)}) collective-permute-start(s16[200,512]{1,0:T(8,128)(2,1)S(1)} %get-tuple-element.73), channel_id=1, source_target_pairs={{0,8},{1,9},{2,10},{3,11},{4,12},{5,13},{6,14},{7,15},{8,0},{9,1},... | collective-permute-start | bytes 614408 | tf_op jit(solution)/shard_map/ppermute | solution.py:51
  111.0 12.2 %collective-permute-start.31 = (s16[200,512]{1,0:T(8,128)(2,1)S(1)}, s16[200,512]{1,0:T(8,128)(2,1)S(1)}, u32[]{:S(2)}, u32[]{:S(2)}) collective-permute-start(s16[200,512]{1,0:T(8,128)(2,1)S(1)} %get-tuple-element.74), channel_id=1, source_target_pairs={{0,12},{1,13},{2,14},{3,15},{4,0},{5,1},{6,2},{7,3},{8,4},{9,5},{1... | collective-permute-start | bytes 614408 | tf_op jit(solution)/shard_map/ppermute | solution.py:51
  123.5 9.2 %collective-permute-start.32 = (s16[200,128]{1,0:T(8,128)(2,1)S(1)}, s16[200,128]{1,0:T(8,128)(2,1)S(1)}, u32[]{:S(2)}, u32[]{:S(2)}) collective-permute-start(s16[200,128]{1,0:T(8,128)(2,1)S(1)} %get-tuple-element.76), channel_id=1, source_target_pairs={{0,1},{1,2},{2,3},{3,0},{4,5},{5,6},{6,7},{7,4},{8,9},{9,10},{10,1... | collective-permute-start | bytes 153608 | tf_op jit(solution)/shard_map/ppermute | solution.py:51
  124.0 14.3 %collective-permute-start.20 = (s16[200,256]{1,0:T(8,128)(2,1)S(1)}, s16[200,256]{1,0:T(8,128)(2,1)S(1)}, u32[]{:S(2)}, u32[]{:S(2)}) collective-permute-start(s16[200,256]{1,0:T(8,128)(2,1)S(1)} %get-tuple-element.58), channel_id=1, source_target_pairs={{0,32},{1,33},{2,34},{3,35},{4,36},{5,37},{6,38},{7,39},{8,40},{9,... | collective-permute-start | bytes 307208 | tf_op jit(solution)/shard_map/ppermute | solution.py:51
  125.5 12.9 %collective-permute-start.21 = (s16[200,256]{1,0:T(8,128)(2,1)S(1)}, s16[200,256]{1,0:T(8,128)(2,1)S(1)}, u32[]{:S(2)}, u32[]{:S(2)}) collective-permute-start(s16[200,256]{1,0:T(8,128)(2,1)S(1)} %get-tuple-element.59), channel_id=1, source_target_pairs={{0,64},{1,65},{2,66},{3,67},{4,68},{5,69},{6,70},{7,71},{8,72},{9,... | collective-permute-start | bytes 307208 | tf_op jit(solution)/shard_map/ppermute | solution.py:51
  130.0 8.4 %collective-permute-start.22 = (s16[200,256]{1,0:T(8,128)(2,1)S(1)}, s16[200,256]{1,0:T(8,128)(2,1)S(1)}, u32[]{:S(2)}, u32[]{:S(2)}) collective-permute-start(s16[200,256]{1,0:T(8,128)(2,1)S(1)} %get-tuple-element.60), channel_id=1, source_target_pairs={{0,96},{1,97},{2,98},{3,99},{4,100},{5,101},{6,102},{7,103},{8,104... | collective-permute-start | bytes 307208 | tf_op jit(solution)/shard_map/ppermute | solution.py:51
  131.7 5.6 %collective-permute-start.33 = (s16[200,128]{1,0:T(8,128)(2,1)S(1)}, s16[200,128]{1,0:T(8,128)(2,1)S(1)}, u32[]{:S(2)}, u32[]{:S(2)}) collective-permute-start(s16[200,128]{1,0:T(8,128)(2,1)S(1)} %get-tuple-element.77), channel_id=1, source_target_pairs={{0,2},{1,3},{2,0},{3,1},{4,6},{5,7},{6,4},{7,5},{8,10},{9,11},{10,... | collective-permute-start | bytes 153608 | tf_op jit(solution)/shard_map/ppermute | solution.py:51
  132.7 5.7 %collective-permute-start.34 = (s16[200,128]{1,0:T(8,128)(2,1)S(1)}, s16[200,128]{1,0:T(8,128)(2,1)S(1)}, u32[]{:S(2)}, u32[]{:S(2)}) collective-permute-start(s16[200,128]{1,0:T(8,128)(2,1)S(1)} %get-tuple-element.78), channel_id=1, source_target_pairs={{0,3},{1,0},{2,1},{3,2},{4,7},{5,4},{6,5},{7,6},{8,11},{9,8},{10,9... | collective-permute-start | bytes 153608 | tf_op jit(solution)/shard_map/ppermute | solution.py:51
  (5 other events, 46.4 us)
